TPU v7x, 32 devices: a whole 2x2x4 slice. The times are simulated.
32 devices in a mesh: fsdp: 32 (over z, y, x, core).
Axes of the slice: x: 2, y: 2, z: 4, core: 2. Of those that a mesh axis runs over, the one named last changes fastest.
Arguments:
- tok_ids: int32 [32, 128], P('fsdp')
- tok_labels: int32 [32, 128], P('fsdp')
- embed: bfloat16 [32128, 768], P('fsdp')
- w_gate: bfloat16 [768, 3072], P('fsdp')
- w_up: bfloat16 [768, 3072], P('fsdp')
- w_down: bfloat16 [3072, 768], P('fsdp')
- gain_mlp: float32 [768], replicated
- gain_final: float32 [768], replicated
Outputs:
- output 1: float32 [], replicated
- output 2: float32 [32128, 768], P('fsdp')
- output 3: float32 [768, 3072], P('fsdp')
- output 4: float32 [768, 3072], P('fsdp')
- output 5: float32 [3072, 768], P('fsdp')
All inputs are finite; a program needn't handle non-finite values.
Results may differ from a plain program's by a relative error of at most 0.0122675.
Values are sent between devices in bfloat16 or wider.
A program may use at most 1 GiB of HBM per device.

v0:
```python
import math
import jax
import jax.numpy as jnp
from jax import lax
from jax.sharding import PartitionSpec as P

NORM_EPS = 1e-6


def dot_plain(left_mat, right_mat):
    return lax.dot_general(left_mat, right_mat, (((1,), (0,)), ((), ())), preferred_element_type=jnp.float32)


def dot_last(left_mat, right_mat):
    return lax.dot_general(left_mat, right_mat, (((1,), (1,)), ((), ())), preferred_element_type=jnp.float32)


def dot_first(left_mat, right_mat):
    return lax.dot_general(left_mat, right_mat, (((0,), (0,)), ((), ())), preferred_element_type=jnp.float32)


def rms_apply(values, gain_vec):
    inv_rms = lax.rsqrt(jnp.mean(values * values, axis=-1, keepdims=True) + NORM_EPS)
    return (values * inv_rms * gain_vec).astype(jnp.bfloat16), inv_rms


def rms_backward(values, inv_rms, gain_vec, grad_out):
    scaled = grad_out * gain_vec
    return inv_rms * scaled - values * (inv_rms ** 3) * jnp.mean(scaled * values, axis=-1, keepdims=True)


def mlp_forward(x_emb, w_gate, w_up, w_down, gain_mlp, gain_final):
    normed, inv_first = rms_apply(x_emb, gain_mlp)
    gate = dot_plain(normed, w_gate).astype(jnp.bfloat16)
    up_val = dot_plain(normed, w_up).astype(jnp.bfloat16)
    hidden_act = (jax.nn.silu(gate.astype(jnp.float32)) * up_val.astype(jnp.float32)).astype(jnp.bfloat16)
    mlp_out = dot_plain(hidden_act, w_down).astype(jnp.bfloat16)
    hid32 = (x_emb + mlp_out.astype(jnp.float32)).astype(jnp.bfloat16).astype(jnp.float32)
    hid_norm, inv_final = rms_apply(hid32, gain_final)
    return hid_norm, (x_emb, inv_first, normed, gate, up_val, hidden_act, hid32, inv_final)


def mlp_backward(d_hid, saved, w_gate, w_up, w_down, gain_mlp, gain_final):
    x_emb, inv_first, normed, gate, up_val, hidden_act, hid32, inv_final = saved
    d_hidden = rms_backward(hid32, inv_final, gain_final, d_hid)
    d_mlp = d_hidden.astype(jnp.bfloat16)
    d_down = dot_first(hidden_act, d_mlp)
    d_act = dot_last(d_mlp, w_down)
    gate32 = gate.astype(jnp.float32)
    gate_sig = jax.nn.sigmoid(gate32)
    d_gate_pre = (d_act * up_val.astype(jnp.float32) * gate_sig * (1.0 + gate32 * (1.0 - gate_sig))).astype(jnp.bfloat16)
    d_up_pre = (d_act * gate32 * gate_sig).astype(jnp.bfloat16)
    d_gate = dot_first(normed, d_gate_pre)
    d_up = dot_first(normed, d_up_pre)
    d_normed = dot_last(d_gate_pre, w_gate) + dot_last(d_up_pre, w_up)
    d_x = (d_hidden + rms_backward(x_emb, inv_first, gain_mlp, d_normed)).astype(jnp.bfloat16)
    return d_x, d_gate, d_up, d_down


def head_forward(hid_norm, emb_chunks, lab_flat):
    chunk_rows = emb_chunks.shape[1]
    tok_count = hid_norm.shape[0]
    col_ids = jnp.arange(chunk_rows, dtype=jnp.int32)

    def chunk_step(carry, chunk_in):
        run_max, run_sum, lab_logit = carry
        chunk_emb, chunk_idx = chunk_in
        logits = dot_last(hid_norm, chunk_emb)
        label_hit = (lab_flat - chunk_idx * chunk_rows)[:, None] == col_ids[None, :]
        new_max = jnp.maximum(run_max, jnp.max(logits, axis=1))
        run_sum = run_sum * jnp.exp(run_max - new_max) + jnp.sum(jnp.exp(logits - new_max[:, None]), axis=1)
        lab_logit = lab_logit + jnp.sum(jnp.where(label_hit, logits, 0.0), axis=1)
        return (new_max, run_sum, lab_logit), None

    zero_tok = jnp.zeros((tok_count,), jnp.float32)
    start = (jnp.full((tok_count,), -jnp.inf, jnp.float32), zero_tok, zero_tok)
    chunk_ids = jnp.arange(emb_chunks.shape[0], dtype=jnp.int32)
    (run_max, run_sum, lab_logit), unused = lax.scan(chunk_step, start, (emb_chunks, chunk_ids))
    return run_max + jnp.log(run_sum), lab_logit


def head_backward(hid_norm, emb_chunks, lab_flat, log_norm, inv_count):
    chunk_rows = emb_chunks.shape[1]
    col_ids = jnp.arange(chunk_rows, dtype=jnp.int32)

    def chunk_step(d_hid, chunk_in):
        chunk_emb, chunk_idx = chunk_in
        logits = dot_last(hid_norm, chunk_emb)
        label_hit = (lab_flat - chunk_idx * chunk_rows)[:, None] == col_ids[None, :]
        prob_mat = jnp.exp(logits - log_norm[:, None])
        grad_logits = ((prob_mat - label_hit.astype(jnp.float32)) * inv_count).astype(jnp.bfloat16)
        return d_hid + dot_plain(grad_logits, chunk_emb), dot_first(grad_logits, hid_norm)

    chunk_ids = jnp.arange(emb_chunks.shape[0], dtype=jnp.int32)
    d_hid, d_head = lax.scan(chunk_step, jnp.zeros(hid_norm.shape, jnp.float32), (emb_chunks, chunk_ids))
    return d_hid, d_head.reshape(-1, hid_norm.shape[1])


def solution(mesh):
    group = mesh.shape['fsdp']

    def local_step(ids_blk, lab_blk, emb_shard, gate_shard, up_shard, down_shard, gain_mlp, gain_final):
        embed_full = lax.all_gather(emb_shard, 'fsdp', tiled=True)
        w_gate = lax.all_gather(gate_shard, 'fsdp', tiled=True)
        w_up = lax.all_gather(up_shard, 'fsdp', tiled=True)
        w_down = lax.all_gather(down_shard, 'fsdp', tiled=True)
        ids_flat = ids_blk.reshape(-1)
        lab_flat = lab_blk.reshape(-1)
        model_dim = embed_full.shape[1]
        emb_scale = math.sqrt(model_dim)
        inv_count = 1.0 / (ids_flat.shape[0] * group)
        x_emb = jnp.take(embed_full, ids_flat, axis=0).astype(jnp.float32) * emb_scale
        hid_norm, saved = mlp_forward(x_emb, w_gate, w_up, w_down, gain_mlp, gain_final)
        emb_chunks = embed_full.reshape(group, -1, model_dim)
        log_norm, lab_logit = head_forward(hid_norm, emb_chunks, lab_flat)
        loss = lax.psum(jnp.sum(log_norm - lab_logit), 'fsdp') * inv_count
        d_hid, d_head = head_backward(hid_norm, emb_chunks, lab_flat, log_norm, inv_count)
        d_x, d_gate, d_up, d_down = mlp_backward(d_hid, saved, w_gate, w_up, w_down, gain_mlp, gain_final)
        d_full = d_head.at[ids_flat].add(d_x.astype(jnp.float32) * emb_scale)
        d_embed = lax.psum_scatter(d_full, 'fsdp', scatter_dimension=0, tiled=True)
        d_gate = lax.psum_scatter(d_gate, 'fsdp', scatter_dimension=0, tiled=True)
        d_up = lax.psum_scatter(d_up, 'fsdp', scatter_dimension=0, tiled=True)
        d_down = lax.psum_scatter(d_down, 'fsdp', scatter_dimension=0, tiled=True)
        return loss, d_embed, d_gate, d_up, d_down

    shard_spec = P('fsdp', None)
    return jax.shard_map(local_step, mesh=mesh, in_specs=(shard_spec, shard_spec, shard_spec, shard_spec, shard_spec, shard_spec, P(), P()), out_specs=(P(), shard_spec, shard_spec, shard_spec, shard_spec), check_vma=False)
```

profile of v0, /device:TPU:0, one launch (start us, length us, event | category | flops | bytes accessed | tf_op | source)
XLA Modules:
  0.0 2139.9 jit_solution(10412408280530968210)
XLA Ops:
  11.4 272.5 %all-gather.12.cloned.1.call-done = bf16[32,1004,768]{2,1,0:T(8,128)(2,1)} async-done(((bf16[1,1004,768]{2,1,0:T(8,128)(2,1)}), bf16[32,1004,768]{2,1,0:T(8,128)(2,1)}) %all-gather.12.cloned.1.call-update) | async-done | bytes 49348624 | tf_op jit(solution)/shard_map/all_gather | solution.py:103
  283.9 38.3 %reshape.132 = bf16[32128,768]{1,0:T(8,128)(2,1)} reshape(bf16[32,1004,768]{2,1,0:T(8,128)(2,1)} %all-gather.12.cloned.1.call-done) | data formatting | bytes 98697216
  322.2 2.0 gather_fusion
  324.4 24.7 %all-gather.6.cloned.1.call-done = bf16[768,3072]{1,0:T(8,128)(2,1)} async-done(((bf16[24,3072]{1,0:T(8,128)(2,1)}), bf16[768,3072]{1,0:T(8,128)(2,1)}) %all-gather.6.cloned.1.call-update) | async-done | bytes 4718608 | tf_op jit(solution)/shard_map/all_gather | solution.py:104
  349.1 4.3 fusion.46
  353.5 60.8 %all-gather.8.cloned.1.call-done = bf16[768,3072]{1,0:T(8,128)(2,1)} async-done(((bf16[24,3072]{1,0:T(8,128)(2,1)}), bf16[768,3072]{1,0:T(8,128)(2,1)}) %all-gather.8.cloned.1.call-update) | async-done | bytes 4718608 | tf_op jit(solution)/shard_map/all_gather | solution.py:105
  414.2 5.1 multiply_convert_fusion.2
  419.3 59.9 %all-gather.10.cloned.1.call-done = bf16[3072,768]{1,0:T(8,128)(2,1)} async-done(((bf16[96,768]{1,0:T(8,128)(2,1)}), bf16[3072,768]{1,0:T(8,128)(2,1)}) %all-gather.10.cloned.1.call-update) | async-done | bytes 4718608 | tf_op jit(solution)/shard_map/all_gather | solution.py:106
  479.2 3.2 multiply_reduce_fusion.1
  482.6 110.5 %while.28 = (s32[]{:T(128)}, f32[128]{0:T(128)S(1)}, f32[128]{0:T(128)S(1)}, f32[128]{0:T(128)S(1)}, bf16[32,1004,768]{2,1,0:T(8,128)(2,1)}, /*index=5*/bf16[128...) while((s32[]{:T(128)}, f32[128]{0:T(128)S(1)}, ...), condition=%wide.region_6.7_spmd.clone, body=%wide.region_2.0_spmd.clone.sunk | while | flops 198166400 | bytes 2783392 | solution.py:78
  593.8 234.7 %while.29 = (s32[]{:T(128)}, f32[128,768]{1,0:T(8,128)S(1)}, f32[32,1004,768]{2,1,0:T(8,128)}, bf16[32,1004,768]{2,1,0:T(8,128)(2,1)}, bf16[128,768]{1,0:T(8,128...) while((s32[]{:T(128)}, f32[128,768]{1,0:T(8,128)S(1)}, ...), condition=%wide.region_10.11_spmd.clone, body=%wide.region_9.10_spmd.clone.sunk | while | flops 593151104 | bytes 8146087 | solution.py:95
  598.9 2.2 bitcast_dynamic-update-slice_fusion.2
  606.2 2.2 bitcast_dynamic-update-slice_fusion.2
  613.6 2.2 bitcast_dynamic-update-slice_fusion.2
  617.1 2.0 fusion.117
  621.0 2.2 bitcast_dynamic-update-slice_fusion.2
  628.2 2.2 bitcast_dynamic-update-slice_fusion.2
  635.6 2.2 bitcast_dynamic-update-slice_fusion.2
  642.9 2.2 bitcast_dynamic-update-slice_fusion.2
  650.2 2.2 bitcast_dynamic-update-slice_fusion.2
  657.5 2.3 bitcast_dynamic-update-slice_fusion.2
  664.9 2.3 bitcast_dynamic-update-slice_fusion.2
  668.5 2.0 fusion.117
  672.3 2.2 bitcast_dynamic-update-slice_fusion.2
  679.6 2.2 bitcast_dynamic-update-slice_fusion.2
  686.9 2.2 bitcast_dynamic-update-slice_fusion.2
  694.3 2.2 bitcast_dynamic-update-slice_fusion.2
  701.6 2.2 bitcast_dynamic-update-slice_fusion.2
  708.8 2.2 bitcast_dynamic-update-slice_fusion.2
  716.1 2.2 bitcast_dynamic-update-slice_fusion.2
  719.6 2.0 fusion.117
  723.4 2.2 bitcast_dynamic-update-slice_fusion.2
  730.8 2.2 bitcast_dynamic-update-slice_fusion.2
  738.1 2.2 bitcast_dynamic-update-slice_fusion.2
  745.4 2.3 bitcast_dynamic-update-slice_fusion.2
  749.0 2.0 fusion.117
  752.8 2.2 bitcast_dynamic-update-slice_fusion.2
  756.3 2.0 fusion.117
  760.2 2.2 bitcast_dynamic-update-slice_fusion.2
  763.6 2.0 fusion.117
  767.5 2.2 bitcast_dynamic-update-slice_fusion.2
  770.9 2.0 fusion.117
  774.8 2.2 bitcast_dynamic-update-slice_fusion.2
  782.1 2.3 bitcast_dynamic-update-slice_fusion.2
  789.6 2.2 bitcast_dynamic-update-slice_fusion.2
  796.8 2.2 bitcast_dynamic-update-slice_fusion.2
  804.2 2.3 bitcast_dynamic-update-slice_fusion.2
  811.6 2.2 bitcast_dynamic-update-slice_fusion.2
  815.0 2.0 fusion.117
  818.9 2.2 bitcast_dynamic-update-slice_fusion.2
  826.2 2.3 bitcast_dynamic-update-slice_fusion.2
  828.8 5.0 multiply_convert_fusion
  834.7 5.1 fusion.70
  839.9 5.2 fusion.68
  845.4 95.1 %reshape.114 = f32[32128,768]{1,0:T(8,128)} reshape(f32[32,1004,768]{2,1,0:T(8,128)} %get-tuple-element.105) | data formatting | bytes 197394432 | tf_op jit(solution)/shard_map/reshape | solution.py:96
  940.5 4.3 fusion.75
  944.7 4.1 fusion.55
  949.1 17.0 scatter_fusion
  966.0 5.1 fusion.62
  971.1 1072.5 %fusion.4 = f32[1008,768]{1,0:T(8,128)S(1)} fusion(f32[32128,768]{1,0:T(8,128)} %scatter_fusion), kind=kCustom, calls=%all-reduce-scatter | all-reduce-scatter fusion | flops 24772608 | bytes 101793792
  2043.6 37.6 %collective-permute-start = (f32[124,768]{1,0:T(8,128)S(1)}, f32[124,768]{1,0:T(8,128)}, u32[]{:S(2)}, u32[]{:S(2)}) collective-permute-start(f32[124,768]{1,0:T(8,128)S(1)} %slice.2), channel_id=1, source_target_pairs={{0,1},{1,2},{2,3},{3,4},{4,5},{5,6},{6,7},{7,8},{8,9},{9,10},{10,1... | collective-permute-start | bytes 1142792
  2081.3 37.0 %psum.7 = f32[]{:T(128)} all-reduce(f32[]{:T(128)} %get-tuple-element.201), channel_id=1, replica_groups=mesh['fsdp'=32] {'fsdp'}, use_global_device_ids=true, to_apply=%region_8.9 | all-reduce | flops 1 | bytes 8 | tf_op jit(solution)/shard_map/psum | solution.py:116
  2119.0 9.1 concatenate
  2128.1 3.8 constant_dynamic-slice_fusion
  (392 shorter events, 221.4 us)
Async XLA Ops:
  7.2 276.7 %all-gather.12.cloned.1.call-start = ((), (), s32[]{:S(2)}) async-start(), calls=%async_computation.9 | async-start | bytes 51093504 | tf_op jit(solution)/shard_map/all_gather | solution.py:103
  7.9 341.2 %all-gather.6.cloned.1.call-start = ((), (), s32[]{:S(2)}) async-start(), calls=%async_computation.3 | async-start | bytes 4866048 | tf_op jit(solution)/shard_map/all_gather | solution.py:104
  8.6 405.6 %all-gather.8.cloned.1.call-start = ((), (), s32[]{:S(2)}) async-start(), calls=%async_computation.4 | async-start | bytes 4866048 | tf_op jit(solution)/shard_map/all_gather | solution.py:105
  9.4 469.9 %all-gather.10.cloned.1.call-start = ((), (), s32[]{:S(2)}) async-start(), calls=%async_computation.5 | async-start | bytes 4866048 | tf_op jit(solution)/shard_map/all_gather | solution.py:106
  10.0 2121.9 %reduce-scatter.6.cloned.1.call-start = ((), (), s32[]{:S(2)}) async-start(), calls=%async_computation.6 | async-start | bytes 9732096 | tf_op jit(solution)/shard_map/reduce_scatter | solution.py:121
  11.4 337.7 %copy-start.1 = (f32[768]{0:T(1024)S(1)}, f32[768]{0:T(1024)}, u32[]{:S(2)}) copy-start(f32[768]{0:T(1024)} %param.18) | copy-start | bytes 9220
  419.3 63.2 %copy-start.2 = (f32[768]{0:T(1024)S(1)}, f32[768]{0:T(1024)}, u32[]{:S(2)}) copy-start(f32[768]{0:T(1024)} %param.19) | copy-start | bytes 9220
  419.3 63.3 %copy-start.3 = (s32[1,128]{1,0:T(1,128)S(1)}, s32[1,128]{1,0:T(1,128)}, u32[]{:S(2)}) copy-start(s32[1,128]{1,0:T(1,128)} %param.13) | copy-start | bytes 1540
  833.8 0.9 copy-start
  839.8 1292.0 %reduce-scatter.8.cloned.1.call-start = ((), (), s32[]{:S(2)}) async-start(), calls=%async_computation.7 | async-start | bytes 9732096 | tf_op jit(solution)/shard_map/reduce_scatter | solution.py:122
  845.1 1286.7 %reduce-scatter.10.cloned.1.call-start = ((), (), s32[]{:S(2)}) async-start(), calls=%async_computation.8 | async-start | bytes 9732096 | tf_op jit(solution)/shard_map/reduce_scatter | solution.py:123
  2043.6 75.3 %collective-permute-start = (f32[124,768]{1,0:T(8,128)S(1)}, f32[124,768]{1,0:T(8,128)}, u32[]{:S(2)}, u32[]{:S(2)}) collective-permute-start(f32[124,768]{1,0:T(8,128)S(1)} %slice.2), channel_id=1, source_target_pairs={{0,1},{1,2},{2,3},{3,4},{4,5},{5,6},{6,7},{7,8},{8,9},{9,10},{10,1... | collective-permute-start | bytes 1142792
Sparse Core Ops, SparseCore 0:
  10.9 272.9 all-gather.11
  286.8 62.2 all-gather.5
  352.0 62.1 all-gather.7
  417.0 62.1 all-gather.9
  840.0 134.9 reduce-scatter.5
  981.2 183.6 reduce-scatter.7
  1171.4 178.6 reduce-scatter.9
where the time goes:
time: 2150 us; the launch traced here: 2140 us
  blocking collectives  1110 us (52%)
  waiting for transfers between devices  420 us (20%)
  matrix products  299 us (14%)
  local copies, waits for them, and re-layouts  187 us (9%)
  loops' own time  43.9 us (2%)
  starting transfers between devices  38.1 us (2%)
  other arithmetic  26 us (1%)
    unnamed x1, blocking collectives  1070 us
    all_gather x1, waiting for transfers between devices, local_step(): embed_full = lax.all_gather(emb_shard, 'fsdp', tiled=True)  272 us
    dot_general x67, matrix products, dot_last(): lax.dot_general(left_mat, right_mat, (((1,), (1,)), ((), ())), preferred_...  140 us
    reshape x1, local copies, waits for them, and re-layouts, head_backward(): return (d_hid, d_head.reshape(-1, hid_norm.shape[1]))  95.1 us
    dot_general x35, matrix products, dot_first(): lax.dot_general(left_mat, right_mat, (((0,), (0,)), ((), ())), preferred_...  86.2 us
    dot_general x35, matrix products, dot_plain(): lax.dot_general(left_mat, right_mat, (((1,), (0,)), ((), ())), preferred_...  72.8 us
    all_gather x1, waiting for transfers between devices, local_step(): w_up = lax.all_gather(up_shard, 'fsdp', tiled=True)  60.8 us
    all_gather x1, waiting for transfers between devices, local_step(): w_down = lax.all_gather(down_shard, 'fsdp', tiled=True)  59.9 us
  transfers between devices with their start and end apart: 8, of which 4 were waited for; matrix products, arithmetic and copies ran while one was open for 59% of the time, Pallas kernels for 0%

commit v1 on v0

v1 whole, which is shorter than its diff:
```python
import math
import jax
import jax.numpy as jnp
from jax import lax
from jax.experimental import pallas as pl
from jax.experimental.pallas import tpu as pltpu
from jax.sharding import PartitionSpec as P

NORM_EPS = 1e-6
MESH = pl.DeviceIdType.MESH
F32 = jnp.float32
BF16 = jnp.bfloat16
VMEM_CAP = 63 * 1024 * 1024
LANE = 128
DIM = 768
WIDE = 1536
PIECE = 288
GUROWS = 192
TWICE = 256
PAIR = 48
NDEV = 32
VPAD = 1024
VROWS = 1004
VSPEC = pl.BlockSpec(memory_space=pltpu.VMEM)


def my_place():
    me = lax.axis_index('fsdp')
    core = lax.rem(me, 2)
    x = lax.rem(lax.div(me, 2), 2)
    y = lax.rem(lax.div(me, 4), 2)
    z = lax.div(me, 8)
    p = x * (1 - core) + y * core
    q = y * (1 - core) + x * core
    return me, z, p, q, core


def chip_of(z, p, q, core):
    x = p * (1 - core) + q * core
    y = q * (1 - core) + p * core
    return (z * 2 + y) * 2 + x


def device_of(z, p, q, core):
    return chip_of(z, p, q, core) * 2 + core


def barrier_neighbours(place):
    me, z, p, q, core = place
    sem = pltpu.get_barrier_semaphore()
    for dev in (device_of(z, 1 - p, q, core), device_of(z, p, 1 - q, core), device_of(z, p, q, core) + 1 - 2 * core):
        pl.semaphore_signal(sem, inc=1, device_id=(dev,), device_id_type=MESH)

    @pl.when(z > 0)
    def _():
        pl.semaphore_signal(sem, inc=1, device_id=(me - 8,), device_id_type=MESH)

    @pl.when(z < 3)
    def _():
        pl.semaphore_signal(sem, inc=1, device_id=(me + 8,), device_id_type=MESH)

    at_end = jnp.logical_or(z == 0, z == 3)

    @pl.when(at_end)
    def _():
        pl.semaphore_wait(sem, 4)

    @pl.when(jnp.logical_not(at_end))
    def _():
        pl.semaphore_wait(sem, 5)


def when_level(z, step, body):
    if step == 0:
        body()
    elif step > 0:
        pl.when(z + step < 4)(body)
    else:
        pl.when(z + step >= 0)(body)


def gather_blocks(in_ref, out_ref, send_sem, recv_sem, place, on_block=None):
    me, z, p, q, core = place
    peers = (me + 8, me - 8, device_of(z, 1 - p, q, core), device_of(z, p, 1 - q, core), me + 1 - 2 * core)

    def desc(block, way):
        src = out_ref.at[block]
        return pltpu.make_async_remote_copy(
            src_ref=src, dst_ref=out_ref.at[block], send_sem=send_sem.at[way, block], recv_sem=recv_sem.at[block],
            device_id=(peers[way],), device_id_type=MESH)

    def desc_own(way):
        return pltpu.make_async_remote_copy(
            src_ref=in_ref, dst_ref=out_ref.at[me], send_sem=send_sem.at[way, me], recv_sem=recv_sem.at[me],
            device_id=(peers[way],), device_id_type=MESH)

    pl.when(z < 3)(lambda: desc_own(0).start())
    pl.when(z > 0)(lambda: desc_own(1).start())
    for way in (3, 2, 4):
        desc_own(way).start()
    out_ref[me] = in_ref[...]
    if on_block is not None:
        on_block(me)

    def got(block):
        desc(block, 4).wait_recv()

    def take_z(step):
        def body():
            block = me + 8 * step
            got(block)
            if step < 0:
                pl.when(z < 3)(lambda: desc(block, 0).start())
            else:
                pl.when(z > 0)(lambda: desc(block, 1).start())
            for way in (3, 2, 4):
                desc(block, way).start()
            if on_block is not None:
                on_block(block)
        when_level(z, step, body)

    def take_p(step):
        def body():
            block = device_of(z + step, 1 - p, q, core)
            got(block)
            for way in (3, 4):
                desc(block, way).start()
            if on_block is not None:
                on_block(block)
        when_level(z, step, body)

    def take_q(step, mid):
        def body():
            block = device_of(z + step, mid, 1 - q, core)
            got(block)
            desc(block, 4).start()
            if on_block is not None:
                on_block(block)
        when_level(z, step, body)

    for far in range(6):
        for step in ((far + 1, -far - 1) if far < 3 else ()):
            take_z(step)
        for step in ((far, -far) if far else (0,)) if far < 4 else ():
            take_p(step)
        for step in ((far, -far) if far else (0,)) if far < 4 else ():
            take_q(step, p)
        if far >= 1:
            near = far - 1
            for step in ((near, -near) if near else (0,)) if near < 4 else ():
                take_q(step, 1 - p)

    for chip in range(16):
        block = chip * 2 + 1 - core
        got(block)
        if on_block is not None:
            on_block(block)
    for level in range(4):
        desc(device_of(level, p, q, core), 2).wait_send()
        for mid in range(2):
            desc(device_of(level, mid, q, core), 3).wait_send()
        pl.when(jnp.logical_and(z < 3, level <= z))(lambda: desc(device_of(level, p, q, core), 0).wait_send())
        pl.when(jnp.logical_and(z > 0, level >= z))(lambda: desc(device_of(level, p, q, core), 1).wait_send())
    for chip in range(16):
        desc(chip * 2 + core, 4).wait_send()


def gather_call(block, cid):
    rows, cols = block.shape

    def kernel(in_ref, out_ref, send_sem, recv_sem):
        place = my_place()
        barrier_neighbours(place)
        gather_blocks(in_ref, out_ref, send_sem, recv_sem, place)

    return pl.pallas_call(
        kernel,
        out_shape=jax.ShapeDtypeStruct((NDEV, rows, cols), block.dtype),
        in_specs=[VSPEC], out_specs=VSPEC,
        scratch_shapes=[pltpu.SemaphoreType.DMA((5, NDEV)), pltpu.SemaphoreType.DMA((NDEV,))],
        compiler_params=pltpu.CompilerParams(collective_id=cid, has_side_effects=True, vmem_limit_bytes=VMEM_CAP),
        name='gather%d' % cid,
    )(block)


def add_into(dst, srcs, rows):
    step = 32

    def body(i, carry):
        sl = pl.ds(pl.multiple_of(i * step, step), step)
        total = srcs[0][sl, :].astype(F32)
        for src in srcs[1:]:
            total = total + src[sl, :].astype(F32)
        dst[sl, :] = total.astype(dst.dtype)
        return carry

    lax.fori_loop(0, rows // step, body, 0)


def scatter_scratch(rows, cols):
    return [
        pltpu.VMEM((16, rows, cols), BF16), pltpu.VMEM((8, rows, cols), BF16), pltpu.VMEM((4, rows, cols), BF16),
        pltpu.VMEM((4, rows, cols), BF16), pltpu.VMEM((4, rows, cols), BF16), pltpu.VMEM((16, rows, cols), BF16),
        pltpu.VMEM((rows, cols), F32),
        pltpu.SemaphoreType.DMA((2, 16)), pltpu.SemaphoreType.DMA((2, 8)), pltpu.SemaphoreType.DMA((2, 4)),
        pltpu.SemaphoreType.DMA((2, 4)), pltpu.SemaphoreType.DMA((2, 4)),
    ]


def scatter_blocks(in_ref, out_ref, scratch, place):
    from_core, from_q, from_p, from_low, from_high, outgo, acc, sem_c, sem_q, sem_p, sem_up, sem_dn = scratch
    me, z, p, q, core = place
    rows = out_ref.shape[0]

    def copy(src, dst, sems, slot, dev):
        return pltpu.make_async_remote_copy(
            src_ref=src, dst_ref=dst, send_sem=sems.at[0, slot], recv_sem=sems.at[1, slot],
            device_id=(dev,), device_id_type=MESH)

    def core_copy(chip):
        return copy(in_ref.at[chip * 2 + 1 - core], from_core.at[chip], sem_c, chip, me + 1 - 2 * core)

    def local(level, mid, last):
        return level * 4 + mid * 2 + last

    def q_copy(level, mid):
        return copy(outgo.at[local(level, mid, 1 - q)], from_q.at[level * 2 + mid], sem_q, level * 2 + mid,
                    device_of(z, p, 1 - q, core))

    def p_copy(level):
        return copy(outgo.at[local(level, 1 - p, q)], from_p.at[level], sem_p, level, device_of(z, 1 - p, q, core))

    def up_copy(level):
        return copy(outgo.at[local(level, p, q)], from_low.at[level], sem_up, level, me + 8)

    def dn_copy(level):
        return copy(outgo.at[local(level, p, q)], from_high.at[level], sem_dn, level, me - 8)

    levels = [lax.rem(z + k, 4) for k in (2, 3, 1, 0)]
    for last in (0, 1):
        for mid in (0, 1):
            for level in levels:
                other = 1 - core
                their_p, their_q = q, p
                mid_d = 1 - their_p if mid == 0 else their_p
                last_d = 1 - their_q if last == 0 else their_q
                core_copy(chip_of(level, mid_d, last_d, other)).start()

    def own(level, mid, last):
        chip = chip_of(level, mid, last, core)
        return [in_ref.at[chip * 2 + core], from_core.at[chip]]

    def wait_core(level, mid, last):
        core_copy(chip_of(level, mid, last, core)).wait_recv()

    for mid in (1 - p, p):
        for level in levels:
            wait_core(level, mid, 1 - q)
            add_into(outgo.at[local(level, mid, 1 - q)], own(level, mid, 1 - q), rows)
            q_copy(level, mid).start()
    for level in levels:
        wait_core(level, 1 - p, q)
        q_copy(level, 1 - p).wait_recv()
        add_into(outgo.at[local(level, 1 - p, q)], own(level, 1 - p, q) + [from_q.at[level * 2 + 1 - p]], rows)
        p_copy(level).start()

    def gather_here(level):
        wait_core(level, p, q)
        q_copy(level, p).wait_recv()
        p_copy(level).wait_recv()
        return own(level, p, q) + [from_q.at[level * 2 + p], from_p.at[level]]

    def send_up(step):
        level = z + step

        @pl.when(level < 4)
        def _():
            add_into(acc, gather_here(level), rows)

            @pl.when(z > 0)
            def _():
                up_copy(level).wait_recv()
                add_into(acc, [acc, from_low.at[level]], rows)
            add_into(outgo.at[local(level, p, q)], [acc], rows)
            up_copy(level).start()

    def send_down(step):
        level = z - step

        @pl.when(level >= 0)
        def _():
            add_into(acc, gather_here(level), rows)

            @pl.when(z < 3)
            def _():
                dn_copy(level).wait_recv()
                add_into(acc, [acc, from_high.at[level]], rows)
            add_into(outgo.at[local(level, p, q)], [acc], rows)
            dn_copy(level).start()

    for step in (3, 2, 1):
        send_up(step)
        send_down(step)
    add_into(out_ref, gather_here(z), rows)

    @pl.when(z > 0)
    def _():
        up_copy(z).wait_recv()
        add_into(out_ref, [out_ref, from_low.at[z]], rows)

    @pl.when(z < 3)
    def _():
        dn_copy(z).wait_recv()
        add_into(out_ref, [out_ref, from_high.at[z]], rows)

    for chip in range(16):
        core_copy(chip).wait_send()
    for level in range(4):
        for mid in range(2):
            q_copy(level, mid).wait_send()
        p_copy(level).wait_send()
        pl.when(level > z)(lambda: up_copy(level).wait_send())
        pl.when(level < z)(lambda: dn_copy(level).wait_send())


def scatter_call(parts, cid):
    _, rows, cols = parts.shape

    def kernel(in_ref, out_ref, *scratch):
        place = my_place()
        barrier_neighbours(place)
        scatter_blocks(in_ref, out_ref, scratch, place)

    return pl.pallas_call(
        kernel,
        out_shape=jax.ShapeDtypeStruct((rows, cols), F32),
        in_specs=[VSPEC], out_specs=VSPEC,
        scratch_shapes=scatter_scratch(rows, cols),
        compiler_params=pltpu.CompilerParams(collective_id=cid, has_side_effects=True, vmem_limit_bytes=VMEM_CAP),
        name='scatter%d' % cid,
    )(parts)


def dot(left, right, ld, rd):
    return lax.dot_general(left, right, (((ld,), (rd,)), ((), ())), preferred_element_type=F32)


TILE = 4
TOKS = TILE * LANE


def id_rows(tok_ref, row, start):
    ids = jnp.concatenate([tok_ref[t, row:row + 1, :] for t in range(TILE)], axis=1) - start
    return jnp.where(jnp.logical_and(ids >= 0, ids < VROWS), ids, -1)


def hits_of(ids):
    return lax.broadcasted_iota(jnp.int32, (VPAD, TOKS), 0) == ids


def shard_start():
    return lax.axis_index('fsdp') * VROWS


TOK_SPEC = pl.BlockSpec((TILE, 8, LANE), lambda i: (i, 0, 0))
ACT_SPEC = pl.BlockSpec((TILE, LANE, DIM), lambda i: (i, 0, 0))
EMB_SPEC = pl.BlockSpec((VPAD, DIM), lambda i: (0, 0))


def lookup_call(toks, emb_pad):
    def kernel(tok_ref, emb_ref, out_ref):
        hit = hits_of(id_rows(tok_ref, 0, shard_start())).astype(F32).astype(BF16)
        out_ref[...] = dot(hit, emb_ref[...], 0, 0).astype(BF16).reshape(TILE, LANE, DIM)

    return pl.pallas_call(
        kernel, grid=(NDEV // TILE,),
        out_shape=jax.ShapeDtypeStruct((NDEV, LANE, DIM), BF16),
        in_specs=[TOK_SPEC, EMB_SPEC], out_specs=ACT_SPEC,
        compiler_params=pltpu.CompilerParams(vmem_limit_bytes=VMEM_CAP),
        cost_estimate=pl.CostEstimate(flops=6400000000, bytes_accessed=8000000, transcendentals=0),
        name='lookup',
    )(toks, emb_pad)


def head_forward_call(toks, emb_pad, hid_all):
    def kernel(tok_ref, emb_ref, hid_ref, out_ref, lab_ref):
        i = pl.program_id(0)
        hid = hid_ref[...].reshape(TOKS, DIM)
        logits = dot(emb_ref[...], hid, 1, 1)
        row = lax.broadcasted_iota(jnp.int32, (VPAD, TOKS), 0)
        real = row < VROWS
        hit = row == id_rows(tok_ref, 1, shard_start())
        lab = jnp.sum(jnp.where(hit, logits, 0.0), axis=0, keepdims=True)
        logits = jnp.where(real, logits, -1e30)
        top = jnp.max(logits, axis=0, keepdims=True)
        total = jnp.sum(jnp.exp(logits - top), axis=0, keepdims=True)
        local = top + jnp.log(total)
        for t in range(TILE):
            out_ref[pl.ds(i * TILE + t, 1), :] = local[:, t * LANE:(t + 1) * LANE]

        @pl.when(i == 0)
        def _():
            lab_ref[...] = jnp.zeros_like(lab_ref)
        part = lab[:, 0:LANE]
        for t in range(1, TILE):
            part = part + lab[:, t * LANE:(t + 1) * LANE]
        lab_ref[0:1, :] = lab_ref[0:1, :] + part

    return pl.pallas_call(
        kernel, grid=(NDEV // TILE,),
        out_shape=(jax.ShapeDtypeStruct((NDEV, LANE), F32), jax.ShapeDtypeStruct((8, LANE), F32)),
        in_specs=[TOK_SPEC, EMB_SPEC, ACT_SPEC],
        out_specs=(pl.BlockSpec((NDEV, LANE), lambda i: (0, 0)), pl.BlockSpec((8, LANE), lambda i: (0, 0))),
        compiler_params=pltpu.CompilerParams(vmem_limit_bytes=VMEM_CAP),
        cost_estimate=pl.CostEstimate(flops=6400000000, bytes_accessed=8000000, transcendentals=4200000),
        name='head_forward',
    )(toks, emb_pad, hid_all)


def head_backward_call(toks, emb_pad, hid_all, stats, inv_count):
    def kernel(tok_ref, emb_ref, hid_ref, stat_ref, dhid_ref, demb_ref, loss_ref, lse_ref):
        i = pl.program_id(0)

        @pl.when(i == 0)
        def _():
            local = stat_ref[:, 0:NDEV, :]
            top = jnp.max(local, axis=0)
            lse = top + jnp.log(jnp.sum(jnp.exp(local - top[None]), axis=0))
            lse_ref[...] = lse
            labs = jnp.sum(jnp.sum(stat_ref[:, NDEV:40, :], axis=0))
            loss_ref[...] = jnp.full((8, LANE), (jnp.sum(lse) - labs) * inv_count, F32)
            demb_ref[...] = jnp.zeros_like(demb_ref)

        hid = hid_ref[...].reshape(TOKS, DIM)
        emb = emb_ref[...]
        logits = dot(emb, hid, 1, 1)
        lse_row = jnp.concatenate([lse_ref[pl.ds(i * TILE + t, 1), :] for t in range(TILE)], axis=1)
        row = lax.broadcasted_iota(jnp.int32, (VPAD, TOKS), 0)
        hit = row == id_rows(tok_ref, 1, shard_start())
        prob = jnp.exp(jnp.where(row < VROWS, logits, -1e30) - lse_row)
        grad = ((prob - jnp.where(hit, 1.0, 0.0)) * inv_count).astype(BF16)
        dhid_ref[...] = dot(grad, emb, 0, 0).astype(BF16).reshape(TILE, LANE, DIM)
        demb_ref[...] += dot(grad, hid, 1, 0)

    return pl.pallas_call(
        kernel, grid=(NDEV // TILE,),
        out_shape=(jax.ShapeDtypeStruct((NDEV, LANE, DIM), BF16), jax.ShapeDtypeStruct((VPAD, DIM), F32),
                   jax.ShapeDtypeStruct((8, LANE), F32)),
        in_specs=[TOK_SPEC, EMB_SPEC, ACT_SPEC, pl.BlockSpec((NDEV, 40, LANE), lambda i: (0, 0, 0))],
        out_specs=(ACT_SPEC, EMB_SPEC, pl.BlockSpec((8, LANE), lambda i: (0, 0))),
        scratch_shapes=[pltpu.VMEM((NDEV, LANE), F32)],
        compiler_params=pltpu.CompilerParams(vmem_limit_bytes=VMEM_CAP),
        cost_estimate=pl.CostEstimate(flops=19300000000, bytes_accessed=17000000, transcendentals=4200000),
        name='head_backward',
    )(toks, emb_pad, hid_all, stats)


def scatter_rows_call(toks, d_head, dx_all, emb_scale):
    steps = NDEV // TILE

    def kernel(tok_ref, head_ref, dx_ref, out_ref, acc_ref):
        i = pl.program_id(0)

        @pl.when(i == 0)
        def _():
            acc_ref[...] = jnp.zeros_like(acc_ref)
        hit = hits_of(id_rows(tok_ref, 0, shard_start())).astype(F32).astype(BF16)
        acc_ref[...] += dot(hit, dx_ref[...].reshape(TOKS, DIM), 1, 0)

        @pl.when(i == steps - 1)
        def _():
            out_ref[...] = head_ref[0:VROWS, :] + acc_ref[0:VROWS, :] * emb_scale

    return pl.pallas_call(
        kernel, grid=(steps,),
        out_shape=jax.ShapeDtypeStruct((VROWS, DIM), F32),
        in_specs=[TOK_SPEC, EMB_SPEC, ACT_SPEC],
        out_specs=pl.BlockSpec((VROWS, DIM), lambda i: (0, 0)),
        scratch_shapes=[pltpu.VMEM((VPAD, DIM), F32)],
        compiler_params=pltpu.CompilerParams(vmem_limit_bytes=VMEM_CAP),
        cost_estimate=pl.CostEstimate(flops=6400000000, bytes_accessed=13000000, transcendentals=0),
        name='scatter_rows',
    )(toks, d_head, dx_all)


def wide_split():
    col = lax.broadcasted_iota(jnp.int32, (1, WIDE), 1)
    dev = lax.shift_right_logical(col * 1366, 16)
    off = col - dev * PAIR
    is_up = off >= 24
    return is_up, dev * 24 + jnp.where(is_up, off - 24, off)


def place_matrix():
    is_up, home = wide_split()
    row = lax.broadcasted_iota(jnp.int32, (DIM, WIDE), 0)
    return is_up, jnp.where(row == home, 1.0, 0.0).astype(BF16)


def rms_inv(values):
    return lax.rsqrt(jnp.mean(values * values, axis=-1, keepdims=True) + NORM_EPS)


def rms_backward(values, inv_rms, gain_vec, grad_out):
    scaled = grad_out * gain_vec
    return inv_rms * scaled - values * (inv_rms ** 3) * jnp.mean(scaled * values, axis=-1, keepdims=True)


def gate_up(wall_ref, j):
    return wall_ref[:, j * PAIR:(j + 1) * PAIR, :].reshape(WIDE, DIM)


def down(wall_ref, j):
    return wall_ref[8 * j:8 * j + 8, GUROWS:PIECE, :].reshape(DIM, DIM)


def both_wide(normed, place, is_up):
    wide = dot(normed, place, 1, 0).astype(BF16)
    zero = jnp.zeros_like(wide)
    return jnp.concatenate([jnp.where(is_up, zero, wide), jnp.where(is_up, wide, zero)], axis=0)


def mlp_forward_call(x_raw, wall, gain_mlp, gain_final, emb_scale):
    def kernel(x_ref, wall_ref, gm_ref, gf_ref, hn_ref, h_ref, gu_ref):
        x = x_ref[...] * emb_scale
        normed = (x * rms_inv(x) * gm_ref[...]).astype(BF16)
        is_up, place = place_matrix()
        wide = both_wide(normed, place, is_up)
        mlp = jnp.zeros((LANE, DIM), F32)
        for j in range(4):
            gu = dot(wide, gate_up(wall_ref, j), 1, 0).astype(BF16)
            gu_ref[j] = gu
            g = gu[0:LANE].astype(F32)
            act = (jax.nn.silu(g) * gu[LANE:TWICE].astype(F32)).astype(BF16)
            mlp = mlp + dot(act, down(wall_ref, j), 1, 0)
        h = (x + mlp.astype(BF16).astype(F32)).astype(BF16)
        h_ref[...] = h
        h32 = h.astype(F32)
        hn_ref[...] = (h32 * rms_inv(h32) * gf_ref[...]).astype(BF16)

    return pl.pallas_call(
        kernel,
        out_shape=(jax.ShapeDtypeStruct((LANE, DIM), BF16), jax.ShapeDtypeStruct((LANE, DIM), BF16),
                   jax.ShapeDtypeStruct((4, TWICE, DIM), BF16)),
        in_specs=[VSPEC] * 4, out_specs=(VSPEC,) * 3,
        compiler_params=pltpu.CompilerParams(vmem_limit_bytes=VMEM_CAP),
        cost_estimate=pl.CostEstimate(flops=3000000000, bytes_accessed=15000000, transcendentals=400000),
        name='mlp_forward',
    )(x_raw, wall, gain_mlp, gain_final)


def mlp_backward_call(dhn, x_raw, h, gu_all, wall, gain_mlp, gain_final, emb_scale):
    def kernel(dhn_ref, x_ref, h_ref, gu_ref, wall_ref, gm_ref, gf_ref, dx_ref, grad_ref):
        x = x_ref[...] * emb_scale
        inv_x = rms_inv(x)
        normed = (x * inv_x * gm_ref[...]).astype(BF16)
        is_up, place = place_matrix()
        wide = both_wide(normed, place, is_up)
        h32 = h_ref[...].astype(F32)
        dh = rms_backward(h32, rms_inv(h32), gf_ref[...], dhn_ref[...])
        dm = dh.astype(BF16)
        dwide = jnp.zeros((TWICE, WIDE), F32)
        for j in range(4):
            gu = gu_ref[j]
            g = gu[0:LANE].astype(F32)
            u = gu[LANE:TWICE].astype(F32)
            act = (jax.nn.silu(g) * u).astype(BF16)
            wd = down(wall_ref, j)
            grad_ref[8 * j:8 * j + 8, GUROWS:PIECE, :] = dot(act, dm, 0, 0).astype(BF16).reshape(8, 96, DIM)
            dq = dot(dm, wd, 1, 1)
            sig = jax.nn.sigmoid(g)
            dg = (dq * u * sig * (1.0 + g * (1.0 - sig))).astype(BF16)
            du = (dq * g * sig).astype(BF16)
            dgu = jnp.concatenate([dg, du], axis=0)
            grad_ref[:, j * PAIR:(j + 1) * PAIR, :] = dot(wide, dgu, 0, 0).astype(BF16).reshape(NDEV, PAIR, DIM)
            dwide = dwide + dot(dgu, gate_up(wall_ref, j), 1, 1)
        dsel = jnp.where(is_up, dwide[LANE:TWICE], dwide[0:LANE])
        hi = dsel.astype(BF16)
        rest = dsel - hi.astype(F32)
        mid = rest.astype(BF16)
        low = (rest - mid.astype(F32)).astype(BF16)
        back = dot(jnp.concatenate([hi, mid, low], axis=0), place, 1, 1)
        da = back[0:LANE] + back[LANE:TWICE] + back[TWICE:384]
        dx_ref[...] = (dh + rms_backward(x, inv_x, gm_ref[...], da)).astype(BF16)

    return pl.pallas_call(
        kernel,
        out_shape=(jax.ShapeDtypeStruct((LANE, DIM), BF16), jax.ShapeDtypeStruct((NDEV, PIECE, DIM), BF16)),
        in_specs=[VSPEC] * 7, out_specs=(VSPEC,) * 2,
        compiler_params=pltpu.CompilerParams(vmem_limit_bytes=VMEM_CAP),
        cost_estimate=pl.CostEstimate(flops=9000000000, bytes_accessed=30000000, transcendentals=800000),
        name='mlp_backward',
    )(dhn, x_raw, h, gu_all, wall, gain_mlp, gain_final)


def solution(mesh):
    group = mesh.shape['fsdp']

    def local_step(ids_blk, lab_blk, emb_shard, gate_shard, up_shard, down_shard, gain_mlp, gain_final):
        model_dim = emb_shard.shape[1]
        emb_scale = math.sqrt(model_dim)
        inv_count = 1.0 / (ids_blk.size * group)
        gm, gf = gain_mlp.reshape(1, -1), gain_final.reshape(1, -1)
        emb_pad = jnp.pad(emb_shard, ((0, VPAD - VROWS), (0, 0)))
        tok_blk = jnp.concatenate([ids_blk, lab_blk, jnp.zeros((6, LANE), jnp.int32)], axis=0)
        gu = jnp.concatenate([gate_shard, up_shard], axis=0).reshape(PAIR, 4, DIM).transpose(1, 0, 2).reshape(GUROWS, DIM)
        wall = gather_call(jnp.concatenate([gu, down_shard], axis=0), 0)
        toks = gather_call(tok_blk, 1)
        x_raw = scatter_call(lookup_call(toks, emb_pad), 2)
        hid_norm, h, gu_all = mlp_forward_call(x_raw, wall, gm, gf, emb_scale)
        hid_all = gather_call(hid_norm, 3)
        local_lse, lab_part = head_forward_call(toks, emb_pad, hid_all)
        stats = gather_call(jnp.concatenate([local_lse, lab_part], axis=0), 4)
        d_hid, d_head, loss = head_backward_call(toks, emb_pad, hid_all, stats, inv_count)
        dhn = scatter_call(d_hid, 5)
        d_x, w_grads = mlp_backward_call(dhn, x_raw, h, gu_all, wall, gm, gf, emb_scale)
        mine = scatter_call(w_grads, 6)
        dx_all = gather_call(d_x, 7)
        d_embed = scatter_rows_call(toks, d_head, dx_all, emb_scale)
        dgu = mine[0:GUROWS].reshape(4, PAIR, DIM).transpose(1, 0, 2).reshape(PAIR, 3072)
        return loss[0, 0], d_embed, dgu[0:24], dgu[24:PAIR], mine[GUROWS:PIECE]

    shard_spec = P('fsdp', None)
    return jax.shard_map(local_step, mesh=mesh, in_specs=(shard_spec, shard_spec, shard_spec, shard_spec, shard_spec, shard_spec, P(), P()), out_specs=(P(), shard_spec, shard_spec, shard_spec, shard_spec), check_vma=False)
```

time: 2150 us -> 487 us (0.23)
  blocking collectives: 1110 us -> 0 us
  Pallas kernels: 0 us -> 469 us
  waiting for transfers between devices: 420 us -> 0 us
  matrix products: 299 us -> 0 us
  local copies, waits for them, and re-layouts: 187 us -> 10.8 us
  loops' own time: 43.9 us -> 0 us
  starting transfers between devices: 38.1 us -> 0 us
    unnamed x1 -> x0, blocking collectives: 1070 us -> none
    pallas_call x0 -> x14, Pallas kernels: none -> 469 us  [the longest x3 194 us: scatter_call(): pl.pallas_call(kernel, out_shape=jax.ShapeDtypeStruct((rows, cols), F32),...]
    all_gather x4 -> x0, waiting for transfers between devices: 418 us -> none  [the longest x1 272 us: local_step(): embed_full = lax.all_gather(emb_shard, 'fsdp', tiled=True)]
    dot_general x137 -> x0, matrix products: 299 us -> none  [the longest x67 140 us: dot_last(): lax.dot_general(left_mat, right_mat, (((1,), (1,)), ((), ())), preferred_...]
    reshape x1 -> x3, local copies, waits for them, and re-layouts: 95.1 us -> 2.58 us  [the longest x2 2.56 us: local_step(): gm, gf = (gain_mlp.reshape(1, -1), gain_final.reshape(1, -1))]
    unnamed x12 -> x1, local copies, waits for them, and re-layouts: 52.1 us -> 0.04 us
    another operation x2 -> x0, loops' own time: 43.9 us -> none  [the longest x1 22.2 us: head_forward(): lax.scan(chunk_step, start, (emb_chunks, chunk_ids))]
    unnamed x1 -> x0, starting transfers between devices: 37.6 us -> none
  transfers between devices with their start and end apart: 8 -> 0, of which waited for: 4 -> 0; matrix products, arithmetic and copies ran while one was open for 59% -> 0% of each run, Pallas kernels for 0% -> 0%
where the time goes in v1:
time: 487 us; the launch traced here: 486 us
  Pallas kernels  469 us (96%)
  local copies, waits for them, and re-layouts  10.8 us (2%)
  other arithmetic  5.38 us (1%)
    pallas_call x3, Pallas kernels, scatter_call(): pl.pallas_call(kernel, out_shape=jax.ShapeDtypeStruct((rows, cols), F32),...  194 us
    pallas_call x5, Pallas kernels, gather_call(): pl.pallas_call(kernel, out_shape=jax.ShapeDtypeStruct((NDEV, rows, cols),...  181 us
    pallas_call x1, Pallas kernels, head_backward_call(): pl.pallas_call(kernel, grid=(NDEV // TILE,), out_shape=(jax.ShapeDtypeStr...  26.1 us
    pallas_call x1, Pallas kernels, mlp_backward_call(): pl.pallas_call(kernel, out_shape=(jax.ShapeDtypeStruct((LANE, DIM), BF16)...  19.8 us
    pallas_call x1, Pallas kernels, head_forward_call(): pl.pallas_call(kernel, grid=(NDEV // TILE,), out_shape=(jax.ShapeDtypeStr...  13.8 us
    pallas_call x1, Pallas kernels, scatter_rows_call(): pl.pallas_call(kernel, grid=(steps,), out_shape=jax.ShapeDtypeStruct((VRO...  12.9 us
    pallas_call x1, Pallas kernels, mlp_forward_call(): pl.pallas_call(kernel, out_shape=(jax.ShapeDtypeStruct((LANE, DIM), BF16)...  11 us
    pallas_call x1, Pallas kernels, lookup_call(): pl.pallas_call(kernel, grid=(NDEV // TILE,), out_shape=jax.ShapeDtypeStru...  10.8 us

profile of v1, /device:TPU:0, one launch (start us, length us, event | category | flops | bytes accessed | tf_op | source)
XLA Modules:
  0.0 486.3 jit_solution(3429263021546534007)
XLA Ops:
  0.6 0.1 pad.13.clone
  0.7 1.3 reshape.30.gm_ref
  2.0 1.3 reshape.31.gf_ref
  3.3 1.3 add_add_fusion.in_ref
  4.6 21.6 %gather1.1.tok_ref = s32[32,8,128]{2,1,0:T(8,128)} custom-call(s32[8,128]{1,0:T(8,128)} %add_add_fusion.in_ref), custom_call_target="tpu_custom_call" | custom-call | tf_op jit(solution)/shard_map/gather1/pallas_call | solution.py:176
  26.2 1.0 pad_maximum_fusion.1
  27.2 1.7 pad_maximum_fusion.in_ref
  28.9 2.6 pad.4.emb_ref
  31.6 10.8 %lookup.1.in_ref = bf16[32,128,768]{2,1,0:T(8,128)(2,1)} custom-call(s32[32,8,128]{2,1,0:T(8,128)} %gather1.1.tok_ref, bf16[1024,768]{1,0:T(8,128)(2,1)} %pad.4.emb_ref), custom_call_target="tpu_custom_call" | custom-call | flops 6400000000 | bytes 8000000 | tf_op jit(solution)/shard_map/lookup/pallas_call | solution.py:375
  42.4 49.2 %scatter2.1.x_ref = f32[128,768]{1,0:T(8,128)} custom-call(bf16[32,128,768]{2,1,0:T(8,128)(2,1)} %lookup.1.in_ref), custom_call_target="tpu_custom_call" | custom-call | tf_op jit(solution)/shard_map/scatter2/pallas_call | solution.py:334
  91.7 68.0 %gather0.1.wall_ref = bf16[32,288,768]{2,1,0:T(8,128)(2,1)} custom-call(bf16[288,768]{1,0:T(8,128)(2,1)} %pad_maximum_fusion.in_ref), custom_call_target="tpu_custom_call" | custom-call | tf_op jit(solution)/shard_map/gather0/pallas_call | solution.py:176
  159.7 11.0 %mlp_forward.1 = (bf16[128,768]{1,0:T(8,128)(2,1)}, bf16[128,768]{1,0:T(8,128)(2,1)}, bf16[4,256,768]{2,1,0:T(8,128)(2,1)}) custom-call(f32[128,768]{1,0:T(8,128)} %scatter2.1.x_ref, bf16[32,288,768]{2,1,0:T(8,128)(2,1)} %gather0.1.wall_ref, f32[1,768]{1,0:T(1,128)} %reshape.30.gm_ref, f32[1,768]{1,0:T(1,128)} %reshape.31.gf_ref), custom_call_target="tpu_custom_call" | custom-call | flops 3000000000 | bytes 15000000 | tf_op jit(solution)/shard_map/mlp_forward/pallas_call | solution.py:541
  170.7 36.5 %gather3.1.hid_ref = bf16[32,128,768]{2,1,0:T(8,128)(2,1)} custom-call(bf16[128,768]{1,0:T(8,128)(2,1)} %get-tuple-element.15.in_ref), custom_call_target="tpu_custom_call" | custom-call | tf_op jit(solution)/shard_map/gather3/pallas_call | solution.py:176
  207.2 13.8 %head_forward.1 = (f32[32,128]{1,0:T(8,128)}, f32[8,128]{1,0:T(8,128)}) custom-call(s32[32,8,128]{2,1,0:T(8,128)} %gather1.1.tok_ref, bf16[1024,768]{1,0:T(8,128)(2,1)} %pad.4.emb_ref, bf16[32,128,768]{2,1,0:T(8,128)(2,1)} %gather3.1.hid_ref), custom_call_target="tpu_custom_call" | custom-call | flops 6400000000 | bytes 8000000 | tf_op jit(solution)/shard_map/head_forward/pallas_call | solution.py:409
  221.0 1.3 pad_maximum_fusion.2.in_ref
  222.3 18.8 %gather4.1.stat_ref = f32[32,40,128]{2,1,0:T(8,128)} custom-call(f32[40,128]{1,0:T(8,128)} %pad_maximum_fusion.2.in_ref), custom_call_target="tpu_custom_call" | custom-call | tf_op jit(solution)/shard_map/gather4/pallas_call | solution.py:176
  241.1 26.1 %head_backward.1 = (bf16[32,128,768]{2,1,0:T(8,128)(2,1)}, f32[1024,768]{1,0:T(8,128)}, f32[8,128]{1,0:T(8,128)}) custom-call(s32[32,8,128]{2,1,0:T(8,128)} %gather1.1.tok_ref, bf16[1024,768]{1,0:T(8,128)(2,1)} %pad.4.emb_ref, bf16[32,128,768]{2,1,0:T(8,128)(2,1)} %gather3.1.hid_ref, f32[32,40,128]{2,1,0:T(8,128)} %gather4.1.stat_ref), custom_call_target="tpu_custom_call" | custom-call | flops 19299999744 | bytes 17000000 | tf_op jit(solution)/shard_map/head_backward/pallas_call | solution.py:445
  267.2 1.2 slice.21
  268.4 48.6 %scatter5.1.dhn_ref = f32[128,768]{1,0:T(8,128)} custom-call(bf16[32,128,768]{2,1,0:T(8,128)(2,1)} %get-tuple-element.20.in_ref), custom_call_target="tpu_custom_call" | custom-call | tf_op jit(solution)/shard_map/scatter5/pallas_call | solution.py:334
  316.9 19.8 %mlp_backward.1 = (bf16[128,768]{1,0:T(8,128)(2,1)}, bf16[32,288,768]{2,1,0:T(8,128)(2,1)}) custom-call(f32[128,768]{1,0:T(8,128)} %scatter5.1.dhn_ref, f32[128,768]{1,0:T(8,128)} %scatter2.1.x_ref, bf16[128,768]{1,0:T(8,128)(2,1)} %get-tuple-element.21.h_ref, bf16[4,256,768]{2,1,0:T(8,128)(2,1)} %get-tuple-element.22.gu_ref, ...), custom_call_target="tpu_custom_call" | custom-call | flops 8999999488 | bytes 30000000 | tf_op jit(solution)/shard_map/mlp_backward/pallas_call | solution.py:586
  336.8 95.8 %scatter6.1 = f32[288,768]{1,0:T(8,128)} custom-call(bf16[32,288,768]{2,1,0:T(8,128)(2,1)} %get-tuple-element.24.in_ref), custom_call_target="tpu_custom_call" | custom-call | tf_op jit(solution)/shard_map/scatter6/pallas_call | solution.py:334
  432.6 1.7 slice.27
  434.3 1.1 slice.22
  435.4 0.7 copy.18
  436.1 0.7 copy.17
  436.9 36.5 %gather7.1.dx_ref = bf16[32,128,768]{2,1,0:T(8,128)(2,1)} custom-call(bf16[128,768]{1,0:T(8,128)(2,1)} %get-tuple-element.23.in_ref), custom_call_target="tpu_custom_call" | custom-call | tf_op jit(solution)/shard_map/gather7/pallas_call | solution.py:176
  473.4 12.9 %scatter_rows.1 = f32[1004,768]{1,0:T(8,128)} custom-call(s32[32,8,128]{2,1,0:T(8,128)} %gather1.1.tok_ref, f32[1024,768]{1,0:T(8,128)} %get-tuple-element.19.head_ref, bf16[32,128,768]{2,1,0:T(8,128)(2,1)} %gather7.1.dx_ref), custom_call_target="tpu_custom_call" | custom-call | flops 6400000000 | bytes 13000000 | tf_op jit(solution)/shard_map/scatter_rows/pallas_call | solution.py:474
  (3 shorter events, 0.1 us)

commit v2 on v1

v2 whole, which is shorter than its diff:
```python
import math
import jax
import jax.numpy as jnp
from jax import lax
from jax.experimental import pallas as pl
from jax.experimental.pallas import tpu as pltpu
from jax.sharding import PartitionSpec as P

NORM_EPS = 1e-6
MESH = pl.DeviceIdType.MESH
F32 = jnp.float32
BF16 = jnp.bfloat16
VMEM_CAP = 63 * 1024 * 1024
LANE = 128
DIM = 768
PAIR = 48
UNITS = 384
NDEV = 32
VPAD = 1024
VROWS = 1004
LEVEL = 8
HEIGHT = 4
DROWS = 96
CHIPS = 16
GROWS = 24
TWO = 2
TOP = 3
VSPEC = pl.BlockSpec(memory_space=pltpu.VMEM)


def my_place():
    me = lax.axis_index('fsdp')
    core = lax.rem(me, TWO)
    x = lax.rem(lax.div(me, TWO), TWO)
    y = lax.rem(lax.div(me, HEIGHT), TWO)
    z = lax.div(me, LEVEL)
    p = x * (1 - core) + y * core
    q = y * (1 - core) + x * core
    return me, z, p, q, core


def chip_of(z, p, q, core):
    x = p * (1 - core) + q * core
    y = q * (1 - core) + p * core
    return (z * TWO + y) * TWO + x


def device_of(z, p, q, core):
    return chip_of(z, p, q, core) * TWO + core


def barrier_neighbours(place):
    me, z, p, q, core = place
    sem = pltpu.get_barrier_semaphore()
    for step in range(1, LEVEL):
        dev = z * LEVEL + lax.rem(me + step, LEVEL)
        pl.semaphore_signal(sem, inc=1, device_id=(dev,), device_id_type=MESH)

    @pl.when(z > 0)
    def _():
        pl.semaphore_signal(sem, inc=1, device_id=(me - LEVEL,), device_id_type=MESH)

    @pl.when(z < TOP)
    def _():
        pl.semaphore_signal(sem, inc=1, device_id=(me + LEVEL,), device_id_type=MESH)

    at_end = jnp.logical_or(z == 0, z == TOP)

    @pl.when(at_end)
    def _():
        pl.semaphore_wait(sem, LEVEL)

    @pl.when(jnp.logical_not(at_end))
    def _():
        pl.semaphore_wait(sem, 9)


def when_level(z, step, body):
    if step == 0:
        body()
    elif step > 0:
        pl.when(z + step < HEIGHT)(body)
    else:
        pl.when(z + step >= 0)(body)


def gather_blocks(in_ref, out_ref, send_sem, recv_sem, place, on_block=None):
    me, z, p, q, core = place
    peers = (me + LEVEL, me - LEVEL, device_of(z, 1 - p, q, core), device_of(z, p, 1 - q, core), me + 1 - TWO * core)

    def desc(block, way):
        src = out_ref.at[block]
        return pltpu.make_async_remote_copy(
            src_ref=src, dst_ref=out_ref.at[block], send_sem=send_sem.at[way, block], recv_sem=recv_sem.at[block],
            device_id=(peers[way],), device_id_type=MESH)

    def desc_own(way):
        return pltpu.make_async_remote_copy(
            src_ref=in_ref, dst_ref=out_ref.at[me], send_sem=send_sem.at[way, me], recv_sem=recv_sem.at[me],
            device_id=(peers[way],), device_id_type=MESH)

    pl.when(z < TOP)(lambda: desc_own(0).start())
    pl.when(z > 0)(lambda: desc_own(1).start())
    for way in (TOP, TWO, HEIGHT):
        desc_own(way).start()
    out_ref[me] = in_ref[...]
    if on_block is not None:
        on_block(me)

    def got(block):
        desc(block, HEIGHT).wait_recv()

    def take_z(step):
        def body():
            block = me + LEVEL * step
            got(block)
            if step < 0:
                pl.when(z < TOP)(lambda: desc(block, 0).start())
            else:
                pl.when(z > 0)(lambda: desc(block, 1).start())
            for way in (TOP, TWO, HEIGHT):
                desc(block, way).start()
            if on_block is not None:
                on_block(block)
        when_level(z, step, body)

    def take_p(step):
        def body():
            block = device_of(z + step, 1 - p, q, core)
            got(block)
            for way in (TOP, HEIGHT):
                desc(block, way).start()
            if on_block is not None:
                on_block(block)
        when_level(z, step, body)

    def take_q(step, mid):
        def body():
            block = device_of(z + step, mid, 1 - q, core)
            got(block)
            desc(block, HEIGHT).start()
            if on_block is not None:
                on_block(block)
        when_level(z, step, body)

    for far in range(6):
        for step in ((far + 1, -far - 1) if far < TOP else ()):
            take_z(step)
        for step in ((far, -far) if far else (0,)) if far < HEIGHT else ():
            take_p(step)
        for step in ((far, -far) if far else (0,)) if far < HEIGHT else ():
            take_q(step, p)
        if far >= 1:
            near = far - 1
            for step in ((near, -near) if near else (0,)) if near < HEIGHT else ():
                take_q(step, 1 - p)

    for chip in range(CHIPS):
        block = chip * TWO + 1 - core
        got(block)
        if on_block is not None:
            on_block(block)
    for level in range(HEIGHT):
        desc(device_of(level, p, q, core), TWO).wait_send()
        for mid in range(TWO):
            desc(device_of(level, mid, q, core), TOP).wait_send()
        pl.when(jnp.logical_and(z < TOP, level <= z))(lambda: desc(device_of(level, p, q, core), 0).wait_send())
        pl.when(jnp.logical_and(z > 0, level >= z))(lambda: desc(device_of(level, p, q, core), 1).wait_send())
    for chip in range(CHIPS):
        desc(chip * TWO + core, HEIGHT).wait_send()


def gather_call(block, cid):
    rows, cols = block.shape

    def kernel(in_ref, out_ref, send_sem, recv_sem):
        place = my_place()
        barrier_neighbours(place)
        gather_blocks(in_ref, out_ref, send_sem, recv_sem, place)

    return pl.pallas_call(
        kernel,
        out_shape=jax.ShapeDtypeStruct((NDEV, rows, cols), block.dtype),
        in_specs=[VSPEC], out_specs=VSPEC,
        scratch_shapes=[pltpu.SemaphoreType.DMA((5, NDEV)), pltpu.SemaphoreType.DMA((NDEV,))],
        compiler_params=pltpu.CompilerParams(collective_id=cid, has_side_effects=True, vmem_limit_bytes=VMEM_CAP),
        name='gather%d' % cid,
    )(block)


def add_into(dst, srcs, rows):
    step = 32

    def body(i, carry):
        sl = pl.ds(pl.multiple_of(i * step, step), step)
        total = srcs[0][sl, :].astype(F32)
        for src in srcs[1:]:
            total = total + src[sl, :].astype(F32)
        dst[sl, :] = total.astype(dst.dtype)
        return carry

    lax.fori_loop(0, rows // step, body, 0)


def scatter_scratch(rows, cols):
    return [
        pltpu.VMEM((CHIPS, rows, cols), BF16), pltpu.VMEM((LEVEL, rows, cols), BF16), pltpu.VMEM((HEIGHT, rows, cols), BF16),
        pltpu.VMEM((HEIGHT, rows, cols), BF16), pltpu.VMEM((HEIGHT, rows, cols), BF16), pltpu.VMEM((CHIPS, rows, cols), BF16),
        pltpu.VMEM((rows, cols), F32),
        pltpu.SemaphoreType.DMA((TWO, CHIPS)), pltpu.SemaphoreType.DMA((TWO, LEVEL)), pltpu.SemaphoreType.DMA((TWO, HEIGHT)),
        pltpu.SemaphoreType.DMA((TWO, HEIGHT)), pltpu.SemaphoreType.DMA((TWO, HEIGHT)),
    ]


def far_first(z):
    half = lax.div(z, TWO)
    inner = lax.rem(z + half, TWO)
    return (TOP - TOP * half, (1 - inner) * (TWO - half) + inner * TOP * half, 1 + lax.rem(z, TWO), z)


def scatter_blocks(in_ref, out_ref, scratch, place):
    from_core, from_q, from_p, from_low, from_high, outgo, acc, sem_c, sem_q, sem_p, sem_up, sem_dn = scratch
    me, z, p, q, core = place
    rows = out_ref.shape[0]

    def copy(src, dst, sems, slot, dev):
        return pltpu.make_async_remote_copy(
            src_ref=src, dst_ref=dst, send_sem=sems.at[0, slot], recv_sem=sems.at[1, slot],
            device_id=(dev,), device_id_type=MESH)

    def core_copy(chip):
        return copy(in_ref.at[chip * TWO + 1 - core], from_core.at[chip], sem_c, chip, me + 1 - TWO * core)

    def local(level, mid, last):
        return level * HEIGHT + mid * TWO + last

    def q_copy(level, mid):
        return copy(outgo.at[local(level, mid, 1 - q)], from_q.at[level * TWO + mid], sem_q, level * TWO + mid,
                    device_of(z, p, 1 - q, core))

    def p_copy(level):
        return copy(outgo.at[local(level, 1 - p, q)], from_p.at[level], sem_p, level, device_of(z, 1 - p, q, core))

    def up_copy(level):
        return copy(outgo.at[local(level, p, q)], from_low.at[level], sem_up, level, me + LEVEL)

    def dn_copy(level):
        return copy(outgo.at[local(level, p, q)], from_high.at[level], sem_dn, level, me - LEVEL)

    levels = far_first(z)
    other = 1 - core
    for level in levels:
        for last in (1 - p, p):
            for mid in (1 - q, q):
                core_copy(chip_of(level, mid, last, other)).start()

    def own(level, mid, last):
        chip = chip_of(level, mid, last, core)
        return [in_ref.at[chip * TWO + core], from_core.at[chip]]

    def wait_core(level, mid, last):
        core_copy(chip_of(level, mid, last, core)).wait_recv()

    for level in levels:
        for mid in (1 - p, p):
            wait_core(level, mid, 1 - q)
            add_into(outgo.at[local(level, mid, 1 - q)], own(level, mid, 1 - q), rows)
            q_copy(level, mid).start()

    def send_p(level):
        wait_core(level, 1 - p, q)
        q_copy(level, 1 - p).wait_recv()
        add_into(outgo.at[local(level, 1 - p, q)], own(level, 1 - p, q) + [from_q.at[level * TWO + 1 - p]], rows)
        p_copy(level).start()

    def gather_here(level):
        wait_core(level, p, q)
        q_copy(level, p).wait_recv()
        p_copy(level).wait_recv()
        return own(level, p, q) + [from_q.at[level * TWO + p], from_p.at[level]]

    def send_z(level):
        add_into(acc, gather_here(level), rows)

        @pl.when(level > z)
        def _():
            @pl.when(z > 0)
            def _():
                up_copy(level).wait_recv()
                add_into(acc, [acc, from_low.at[level]], rows)
            add_into(outgo.at[local(level, p, q)], [acc], rows)
            up_copy(level).start()

        @pl.when(level < z)
        def _():
            @pl.when(z < TOP)
            def _():
                dn_copy(level).wait_recv()
                add_into(acc, [acc, from_high.at[level]], rows)
            add_into(outgo.at[local(level, p, q)], [acc], rows)
            dn_copy(level).start()

    send_p(levels[0])
    for at in range(TOP):
        send_p(levels[at + 1])
        send_z(levels[at])
    add_into(out_ref, gather_here(z), rows)

    @pl.when(z > 0)
    def _():
        up_copy(z).wait_recv()
        add_into(out_ref, [out_ref, from_low.at[z]], rows)

    @pl.when(z < TOP)
    def _():
        dn_copy(z).wait_recv()
        add_into(out_ref, [out_ref, from_high.at[z]], rows)

    for chip in range(CHIPS):
        core_copy(chip).wait_send()
    for level in range(HEIGHT):
        for mid in range(TWO):
            q_copy(level, mid).wait_send()
        p_copy(level).wait_send()
        pl.when(level > z)(lambda: up_copy(level).wait_send())
        pl.when(level < z)(lambda: dn_copy(level).wait_send())


def scatter_call(parts, cid):
    _, rows, cols = parts.shape

    def kernel(in_ref, out_ref, *scratch):
        place = my_place()
        barrier_neighbours(place)
        scatter_blocks(in_ref, out_ref, scratch, place)

    return pl.pallas_call(
        kernel,
        out_shape=jax.ShapeDtypeStruct((rows, cols), F32),
        in_specs=[VSPEC], out_specs=VSPEC,
        scratch_shapes=scatter_scratch(rows, cols),
        compiler_params=pltpu.CompilerParams(collective_id=cid, has_side_effects=True, vmem_limit_bytes=VMEM_CAP),
        name='scatter%d' % cid,
    )(parts)


def dot(left, right, ld, rd):
    return lax.dot_general(left, right, (((ld,), (rd,)), ((), ())), preferred_element_type=F32)


TILE = HEIGHT
TOKS = TILE * LANE


def id_rows(tok_ref, row, start):
    ids = jnp.concatenate([tok_ref[t, row:row + 1, :] for t in range(TILE)], axis=1) - start
    return jnp.where(jnp.logical_and(ids >= 0, ids < VROWS), ids, -1)


def hits_of(ids):
    return lax.broadcasted_iota(jnp.int32, (VPAD, TOKS), 0) == ids


def shard_start():
    return lax.axis_index('fsdp') * VROWS


TOK_SPEC = pl.BlockSpec((TILE, LEVEL, LANE), lambda i: (i, 0, 0))
ACT_SPEC = pl.BlockSpec((TILE, LANE, DIM), lambda i: (i, 0, 0))
EMB_SPEC = pl.BlockSpec((VPAD, DIM), lambda i: (0, 0))


def lookup_call(toks, emb_pad):
    def kernel(tok_ref, emb_ref, out_ref):
        hit = hits_of(id_rows(tok_ref, 0, shard_start())).astype(F32).astype(BF16)
        out_ref[...] = dot(hit, emb_ref[...], 0, 0).astype(BF16).reshape(TILE, LANE, DIM)

    return pl.pallas_call(
        kernel, grid=(NDEV // TILE,),
        out_shape=jax.ShapeDtypeStruct((NDEV, LANE, DIM), BF16),
        in_specs=[TOK_SPEC, EMB_SPEC], out_specs=ACT_SPEC,
        compiler_params=pltpu.CompilerParams(vmem_limit_bytes=VMEM_CAP),
        cost_estimate=pl.CostEstimate(flops=6400000000, bytes_accessed=8000000, transcendentals=0),
        name='lookup',
    )(toks, emb_pad)


def head_forward_call(toks, emb_pad, hid_all):
    def kernel(tok_ref, emb_ref, hid_ref, out_ref, lab_ref):
        i = pl.program_id(0)
        hid = hid_ref[...].reshape(TOKS, DIM)
        logits = dot(emb_ref[...], hid, 1, 1)
        row = lax.broadcasted_iota(jnp.int32, (VPAD, TOKS), 0)
        real = row < VROWS
        hit = row == id_rows(tok_ref, 1, shard_start())
        lab = jnp.sum(jnp.where(hit, logits, 0.0), axis=0, keepdims=True)
        logits = jnp.where(real, logits, -1e30)
        top = jnp.max(logits, axis=0, keepdims=True)
        total = jnp.sum(jnp.exp(logits - top), axis=0, keepdims=True)
        local = top + jnp.log(total)
        for t in range(TILE):
            out_ref[pl.ds(i * TILE + t, 1), :] = local[:, t * LANE:(t + 1) * LANE]

        @pl.when(i == 0)
        def _():
            lab_ref[...] = jnp.zeros_like(lab_ref)
        part = lab[:, 0:LANE]
        for t in range(1, TILE):
            part = part + lab[:, t * LANE:(t + 1) * LANE]
        lab_ref[0:1, :] = lab_ref[0:1, :] + part

    return pl.pallas_call(
        kernel, grid=(NDEV // TILE,),
        out_shape=(jax.ShapeDtypeStruct((NDEV, LANE), F32), jax.ShapeDtypeStruct((LEVEL, LANE), F32)),
        in_specs=[TOK_SPEC, EMB_SPEC, ACT_SPEC],
        out_specs=(pl.BlockSpec((NDEV, LANE), lambda i: (0, 0)), pl.BlockSpec((LEVEL, LANE), lambda i: (0, 0))),
        compiler_params=pltpu.CompilerParams(vmem_limit_bytes=VMEM_CAP),
        cost_estimate=pl.CostEstimate(flops=6400000000, bytes_accessed=8000000, transcendentals=4200000),
        name='head_forward',
    )(toks, emb_pad, hid_all)


def head_backward_call(toks, emb_pad, hid_all, stats, inv_count):
    def kernel(tok_ref, emb_ref, hid_ref, stat_ref, dhid_ref, demb_ref, loss_ref, lse_ref):
        i = pl.program_id(0)

        @pl.when(i == 0)
        def _():
            local = stat_ref[:, 0:NDEV, :]
            top = jnp.max(local, axis=0)
            lse = top + jnp.log(jnp.sum(jnp.exp(local - top[None]), axis=0))
            lse_ref[...] = lse
            labs = jnp.sum(jnp.sum(stat_ref[:, NDEV:40, :], axis=0))
            loss_ref[...] = jnp.full((LEVEL, LANE), (jnp.sum(lse) - labs) * inv_count, F32)
            demb_ref[...] = jnp.zeros_like(demb_ref)

        hid = hid_ref[...].reshape(TOKS, DIM)
        emb = emb_ref[...]
        logits = dot(emb, hid, 1, 1)
        lse_row = jnp.concatenate([lse_ref[pl.ds(i * TILE + t, 1), :] for t in range(TILE)], axis=1)
        row = lax.broadcasted_iota(jnp.int32, (VPAD, TOKS), 0)
        hit = row == id_rows(tok_ref, 1, shard_start())
        prob = jnp.exp(jnp.where(row < VROWS, logits, -1e30) - lse_row)
        grad = ((prob - jnp.where(hit, 1.0, 0.0)) * inv_count).astype(BF16)
        dhid_ref[...] = dot(grad, emb, 0, 0).astype(BF16).reshape(TILE, LANE, DIM)
        demb_ref[...] += dot(grad, hid, 1, 0)

    return pl.pallas_call(
        kernel, grid=(NDEV // TILE,),
        out_shape=(jax.ShapeDtypeStruct((NDEV, LANE, DIM), BF16), jax.ShapeDtypeStruct((VPAD, DIM), F32),
                   jax.ShapeDtypeStruct((LEVEL, LANE), F32)),
        in_specs=[TOK_SPEC, EMB_SPEC, ACT_SPEC, pl.BlockSpec((NDEV, 40, LANE), lambda i: (0, 0, 0))],
        out_specs=(ACT_SPEC, EMB_SPEC, pl.BlockSpec((LEVEL, LANE), lambda i: (0, 0))),
        scratch_shapes=[pltpu.VMEM((NDEV, LANE), F32)],
        compiler_params=pltpu.CompilerParams(vmem_limit_bytes=VMEM_CAP),
        cost_estimate=pl.CostEstimate(flops=19300000000, bytes_accessed=17000000, transcendentals=4200000),
        name='head_backward',
    )(toks, emb_pad, hid_all, stats)


def scatter_rows_call(toks, d_head, dx_all, emb_scale):
    steps = NDEV // TILE

    def kernel(tok_ref, head_ref, dx_ref, out_ref, acc_ref):
        i = pl.program_id(0)

        @pl.when(i == 0)
        def _():
            acc_ref[...] = jnp.zeros_like(acc_ref)
        hit = hits_of(id_rows(tok_ref, 0, shard_start())).astype(F32).astype(BF16)
        acc_ref[...] += dot(hit, dx_ref[...].reshape(TOKS, DIM), 1, 0)

        @pl.when(i == steps - 1)
        def _():
            out_ref[...] = head_ref[0:VROWS, :] + acc_ref[0:VROWS, :] * emb_scale

    return pl.pallas_call(
        kernel, grid=(steps,),
        out_shape=jax.ShapeDtypeStruct((VROWS, DIM), F32),
        in_specs=[TOK_SPEC, EMB_SPEC, ACT_SPEC],
        out_specs=pl.BlockSpec((VROWS, DIM), lambda i: (0, 0)),
        scratch_shapes=[pltpu.VMEM((VPAD, DIM), F32)],
        compiler_params=pltpu.CompilerParams(vmem_limit_bytes=VMEM_CAP),
        cost_estimate=pl.CostEstimate(flops=6400000000, bytes_accessed=13000000, transcendentals=0),
        name='scatter_rows',
    )(toks, d_head, dx_all)


def rms_inv(values):
    return lax.rsqrt(jnp.mean(values * values, axis=-1, keepdims=True) + NORM_EPS)


def rms_backward(values, inv_rms, gain_vec, grad_out):
    scaled = grad_out * gain_vec
    return inv_rms * scaled - values * (inv_rms ** TOP) * jnp.mean(scaled * values, axis=-1, keepdims=True)


def side_specs(n):
    return [pltpu.SemaphoreType.DMA((n,)), pltpu.SemaphoreType.DMA((n,))]


def weights_call(pieces, down_shard, cid):
    def kernel(piece_ref, down_ref, gu_ref, wd_ref, a_send, a_recv, z_send, z_recv, d_send, d_recv):
        place = my_place()
        me, z, p, q, core = place
        rank = lax.rem(me, LEVEL)
        barrier_neighbours(place)

        def exchange(step):
            peer = lax.rem(rank + step, LEVEL)
            return pltpu.make_async_remote_copy(
                src_ref=piece_ref.at[peer], dst_ref=gu_ref.at[me], send_sem=a_send.at[step], recv_sem=a_recv.at[step],
                device_id=(z * LEVEL + peer,), device_id_type=MESH)

        def slab(level, way):
            part = gu_ref.at[pl.ds(level * LEVEL, LEVEL)]
            return pltpu.make_async_remote_copy(
                src_ref=part, dst_ref=part, send_sem=z_send.at[way * HEIGHT + level], recv_sem=z_recv.at[level],
                device_id=(me + LEVEL - CHIPS * way,), device_id_type=MESH)

        def slab_down(level, way, src):
            return pltpu.make_async_remote_copy(
                src_ref=src, dst_ref=wd_ref.at[level], send_sem=d_send.at[way * HEIGHT + level], recv_sem=d_recv.at[level],
                device_id=(me + LEVEL - CHIPS * way,), device_id_type=MESH)

        for step in range(1, LEVEL):
            exchange(step).start()
        pl.when(z < TOP)(lambda: slab_down(z, 0, down_ref).start())
        pl.when(z > 0)(lambda: slab_down(z, 1, down_ref).start())
        wd_ref[z] = down_ref[...]
        gu_ref[me] = piece_ref[rank]
        for step in range(1, LEVEL):
            exchange(step).wait_recv()
        pl.when(z < TOP)(lambda: slab(z, 0).start())
        pl.when(z > 0)(lambda: slab(z, 1).start())

        def take(level, way, more):
            slab_down(level, 0, wd_ref.at[level]).wait_recv()
            pl.when(more)(lambda: slab_down(level, way, wd_ref.at[level]).start())
            slab(level, 0).wait_recv()
            pl.when(more)(lambda: slab(level, way).start())

        for far in (1, TWO, TOP):
            pl.when(z - far >= 0)(lambda: take(z - far, 0, z < TOP))
            pl.when(z + far < HEIGHT)(lambda: take(z + far, 1, z > 0))
        for step in range(1, LEVEL):
            exchange(step).wait_send()

        def sent(level, way):
            slab(level, way).wait_send()
            slab_down(level, way, wd_ref.at[level]).wait_send()

        for level in range(HEIGHT):
            pl.when(jnp.logical_and(z < TOP, level <= z))(lambda: sent(level, 0))
            pl.when(jnp.logical_and(z > 0, level >= z))(lambda: sent(level, 1))

    return pl.pallas_call(
        kernel,
        out_shape=(jax.ShapeDtypeStruct((NDEV, PAIR, UNITS), BF16), jax.ShapeDtypeStruct((HEIGHT, DROWS, DIM), BF16)),
        in_specs=[VSPEC] * TWO, out_specs=(VSPEC,) * TWO,
        scratch_shapes=side_specs(LEVEL) + [pltpu.SemaphoreType.DMA((LEVEL,)), pltpu.SemaphoreType.DMA((HEIGHT,))] * TWO,
        compiler_params=pltpu.CompilerParams(collective_id=cid, has_side_effects=True, vmem_limit_bytes=VMEM_CAP),
        name='weights',
    )(pieces, down_shard)


def grads_call(gu_parts, down_parts, cid):
    def kernel(gu_ref, gd_ref, out_ref, dn_ref, from_low, from_high, low_d, high_d, outgo, outgo_d, acc, acc_d,
               a_send, a_recv, z_send, z_recv, d_send, d_recv):
        place = my_place()
        me, z, p, q, core = place
        rank = lax.rem(me, LEVEL)
        barrier_neighbours(place)

        def rows_of(ref, level):
            return ref.at[pl.ds(level * LEVEL, LEVEL)]

        def add_slab(dst, srcs):
            def body(i, carry):
                total = srcs[0][i].astype(F32)
                for src in srcs[1:]:
                    total = total + src[i].astype(F32)
                dst[i] = total.astype(dst.dtype)
                return carry
            lax.fori_loop(0, LEVEL, body, 0)

        def hop(level, way):
            land = (from_low, from_high)[way]
            return pltpu.make_async_remote_copy(
                src_ref=rows_of(outgo, level), dst_ref=rows_of(land, level), send_sem=z_send.at[way * HEIGHT + level],
                recv_sem=z_recv.at[way * HEIGHT + level], device_id=(me + LEVEL - CHIPS * way,), device_id_type=MESH)

        def hop_d(level, way):
            land = (low_d, high_d)[way]
            return pltpu.make_async_remote_copy(
                src_ref=outgo_d.at[level], dst_ref=land.at[level], send_sem=d_send.at[way * HEIGHT + level],
                recv_sem=d_recv.at[way * HEIGHT + level], device_id=(me + LEVEL - CHIPS * way,), device_id_type=MESH)

        def send(level, way, more):
            @pl.when(more)
            def _():
                hop(level, way).wait_recv()
                add_slab(rows_of(outgo, level), [rows_of(gu_ref, level), rows_of((from_low, from_high)[way], level)])

            @pl.when(jnp.logical_not(more))
            def _():
                add_slab(rows_of(outgo, level), [rows_of(gu_ref, level)])
            hop(level, way).start()

            @pl.when(more)
            def _():
                hop_d(level, way).wait_recv()
                add_into(outgo_d.at[level], [gd_ref.at[level], (low_d, high_d)[way].at[level]], DROWS)

            @pl.when(jnp.logical_not(more))
            def _():
                add_into(outgo_d.at[level], [gd_ref.at[level]], DROWS)
            hop_d(level, way).start()

        for far in (TOP, TWO, 1):
            pl.when(z + far < HEIGHT)(lambda: send(z + far, 0, z > 0))
            pl.when(z - far >= 0)(lambda: send(z - far, 1, z < TOP))
        add_slab(acc, [rows_of(gu_ref, z)])
        add_into(dn_ref, [gd_ref.at[z]], DROWS)

        def last(way):
            hop(z, way).wait_recv()
            add_slab(acc, [acc, rows_of((from_low, from_high)[way], z)])
            hop_d(z, way).wait_recv()
            add_into(dn_ref, [dn_ref, (low_d, high_d)[way].at[z]], DROWS)

        pl.when(z > 0)(lambda: last(0))
        pl.when(z < TOP)(lambda: last(1))

        def exchange(step):
            peer = lax.rem(rank + step, LEVEL)
            return pltpu.make_async_remote_copy(
                src_ref=acc.at[peer], dst_ref=out_ref.at[rank], send_sem=a_send.at[step], recv_sem=a_recv.at[step],
                device_id=(z * LEVEL + peer,), device_id_type=MESH)

        for step in range(1, LEVEL):
            exchange(step).start()
        out_ref[rank] = acc[rank]
        for step in range(1, LEVEL):
            exchange(step).wait_recv()
        for step in range(1, LEVEL):
            exchange(step).wait_send()

        def sent(level, way):
            hop(level, way).wait_send()
            hop_d(level, way).wait_send()

        for level in range(HEIGHT):
            pl.when(level > z)(lambda: sent(level, 0))
            pl.when(level < z)(lambda: sent(level, 1))

    slab = pltpu.VMEM((NDEV, PAIR, UNITS), BF16)
    slab_d = pltpu.VMEM((HEIGHT, DROWS, DIM), BF16)
    return pl.pallas_call(
        kernel,
        out_shape=(jax.ShapeDtypeStruct((LEVEL, PAIR, UNITS), F32), jax.ShapeDtypeStruct((DROWS, DIM), F32)),
        in_specs=[VSPEC] * TWO, out_specs=(VSPEC,) * TWO,
        scratch_shapes=[slab, slab, slab_d, slab_d, slab, slab_d, pltpu.VMEM((LEVEL, PAIR, UNITS), F32),
                        pltpu.VMEM((DROWS, DIM), F32)] + side_specs(LEVEL) * TOP,
        compiler_params=pltpu.CompilerParams(collective_id=cid, has_side_effects=True, vmem_limit_bytes=VMEM_CAP),
        name='grads',
    )(gu_parts, down_parts)


def rank_of(p, q, core):
    return device_of(0, p, q, core)


def level_gather(in_ref, out_ref, send_sem, recv_sem, place):
    me, z, p, q, core = place
    rank = lax.rem(me, LEVEL)
    peers = (device_of(z, 1 - p, q, core), device_of(z, p, 1 - q, core), me + 1 - TWO * core)

    def desc(block, way, src=None):
        return pltpu.make_async_remote_copy(
            src_ref=out_ref.at[block] if src is None else src, dst_ref=out_ref.at[block],
            send_sem=send_sem.at[way * LEVEL + block], recv_sem=recv_sem.at[block],
            device_id=(peers[way],), device_id_type=MESH)

    for way in (1, 0, TWO):
        desc(rank, way, in_ref).start()
    out_ref[rank] = in_ref[...]
    side = rank_of(1 - p, q, core)
    desc(side, 0).wait_recv()
    for way in (1, TWO):
        desc(side, way).start()
    for mid in (p, 1 - p):
        block = rank_of(mid, 1 - q, core)
        desc(block, 1).wait_recv()
        desc(block, TWO).start()
    for chip in range(HEIGHT):
        desc(chip * TWO + 1 - core, TWO).wait_recv()
    desc(rank, 0, in_ref).wait_send()
    desc(rank, 1, in_ref).wait_send()
    desc(side, 1).wait_send()
    for chip in range(HEIGHT):
        desc(chip * TWO + core, TWO).wait_send()


def level_scatter(in_ref, out_ref, from_core, from_q, from_p, outgo, sem_s, sem_r, place):
    me, z, p, q, core = place
    rows = out_ref.shape[0]

    def copy(src, dst, slot, dev):
        return pltpu.make_async_remote_copy(
            src_ref=src, dst_ref=dst, send_sem=sem_s.at[slot], recv_sem=sem_r.at[slot],
            device_id=(dev,), device_id_type=MESH)

    def core_copy(chip):
        return copy(in_ref.at[chip * TWO + 1 - core], from_core.at[chip], chip, me + 1 - TWO * core)

    def q_copy(mid):
        return copy(outgo.at[mid], from_q.at[mid], HEIGHT + mid, device_of(z, p, 1 - q, core))

    def p_copy():
        return copy(outgo.at[TWO], from_p, 6, device_of(z, 1 - p, q, core))

    def own(mid, last):
        chip = chip_of(0, mid, last, core)
        core_copy(chip).wait_recv()
        return [in_ref.at[chip * TWO + core], from_core.at[chip]]

    for last in (1 - p, p):
        for mid in (1 - q, q):
            core_copy(chip_of(0, mid, last, 1 - core)).start()
    for mid in (1 - p, p):
        add_into(outgo.at[mid], own(mid, 1 - q), rows)
        q_copy(mid).start()
    side = own(1 - p, q)
    q_copy(1 - p).wait_recv()
    add_into(outgo.at[TWO], side + [from_q.at[1 - p]], rows)
    p_copy().start()
    mine = own(p, q)
    q_copy(p).wait_recv()
    p_copy().wait_recv()
    add_into(out_ref, mine + [from_q.at[p], from_p], rows)
    for chip in range(HEIGHT):
        core_copy(chip).wait_send()
    for mid in range(TWO):
        q_copy(mid).wait_send()
    p_copy().wait_send()


LEVEL_SCRATCH = [
    pltpu.VMEM((LANE, DIM), BF16), pltpu.VMEM((LEVEL, LANE, DIM), BF16), pltpu.VMEM((LANE, DIM), F32),
    pltpu.VMEM((HEIGHT, LANE, DIM), BF16), pltpu.VMEM((TWO, LANE, DIM), BF16), pltpu.VMEM((LANE, DIM), BF16),
    pltpu.VMEM((TOP, LANE, DIM), BF16),
    pltpu.SemaphoreType.DMA((GROWS,)), pltpu.SemaphoreType.DMA((LEVEL,)),
    pltpu.SemaphoreType.DMA((7,)), pltpu.SemaphoreType.DMA((7,)),
]


def split_weights(gu_ref):
    wide = gu_ref[...].astype(F32)
    return (wide[:, 0:GROWS, :].reshape(DIM, UNITS).astype(BF16), wide[:, GROWS:PAIR, :].reshape(DIM, UNITS).astype(BF16))


def mlp_forward_call(x_raw, w_gu, w_dn, gain_mlp, gain_final, emb_scale, cid):
    def kernel(x_ref, wgu_ref, wd_ref, gm_ref, gf_ref, hn_ref, h_ref, a_ref, g_ref, u_ref, mine, parts, total, *scratch):
        place = my_place()
        barrier_neighbours(place)
        x = x_ref[...] * emb_scale
        mine[...] = (x * rms_inv(x) * gm_ref[...]).astype(BF16)
        level_gather(mine, a_ref, scratch[HEIGHT], scratch[5], place)
        wg, wu = split_weights(wgu_ref)
        wd = wd_ref[...].reshape(UNITS, DIM)
        for half in range(TWO):
            four = slice(HEIGHT * half, HEIGHT * half + HEIGHT)
            act_in = a_ref[four].reshape(TOKS, DIM)
            g = dot(act_in, wg, 1, 0).astype(BF16)
            u = dot(act_in, wu, 1, 0).astype(BF16)
            g_ref[four] = g.reshape(HEIGHT, LANE, UNITS)
            u_ref[four] = u.reshape(HEIGHT, LANE, UNITS)
            act = (jax.nn.silu(g.astype(F32)) * u.astype(F32)).astype(BF16)
            parts[four] = dot(act, wd, 1, 0).astype(BF16).reshape(HEIGHT, LANE, DIM)
        level_scatter(parts, total, *scratch[:HEIGHT], *scratch[6:], place)
        h = (x + total[...].astype(BF16).astype(F32)).astype(BF16)
        h_ref[...] = h
        h32 = h.astype(F32)
        hn_ref[...] = (h32 * rms_inv(h32) * gf_ref[...]).astype(BF16)

    act = jax.ShapeDtypeStruct((LANE, DIM), BF16)
    unit = jax.ShapeDtypeStruct((LEVEL, LANE, UNITS), BF16)
    return pl.pallas_call(
        kernel,
        out_shape=(act, act, jax.ShapeDtypeStruct((LEVEL, LANE, DIM), BF16), unit, unit),
        in_specs=[VSPEC] * 5, out_specs=(VSPEC,) * 5,
        scratch_shapes=LEVEL_SCRATCH,
        compiler_params=pltpu.CompilerParams(collective_id=cid, has_side_effects=True, vmem_limit_bytes=VMEM_CAP),
        name='mlp_forward',
    )(x_raw, w_gu, w_dn, gain_mlp, gain_final)


def mlp_backward_call(dhn, x_raw, h, a_all, g_all, u_all, w_gu, w_dn, gain_mlp, gain_final, emb_scale, cid):
    def kernel(dhn_ref, x_ref, h_ref, a_ref, g_ref, u_ref, wgu_ref, wd_ref, gm_ref, gf_ref, dx_ref, ggu_ref, gd_ref,
               dm_ref, grad_gate, grad_up, grad_down, mine, parts, total, *scratch):
        place = my_place()
        barrier_neighbours(place)
        h32 = h_ref[...].astype(F32)
        dh = rms_backward(h32, rms_inv(h32), gf_ref[...], dhn_ref[...])
        mine[...] = dh.astype(BF16)
        level_gather(mine, dm_ref, scratch[HEIGHT], scratch[5], place)
        wg, wu = split_weights(wgu_ref)
        wd = wd_ref[...].reshape(UNITS, DIM)
        for half in range(TWO):
            four = slice(HEIGHT * half, HEIGHT * half + HEIGHT)
            act_in = a_ref[four].reshape(TOKS, DIM)
            dm = dm_ref[four].reshape(TOKS, DIM)
            g = g_ref[four].reshape(TOKS, UNITS).astype(F32)
            u = u_ref[four].reshape(TOKS, UNITS).astype(F32)
            act = (jax.nn.silu(g) * u).astype(BF16)
            dq = dot(dm, wd, 1, 1)
            sig = jax.nn.sigmoid(g)
            dg = (dq * u * sig * (1.0 + g * (1.0 - sig))).astype(BF16)
            du = (dq * g * sig).astype(BF16)
            parts[four] = (dot(dg, wg, 1, 1) + dot(du, wu, 1, 1)).astype(BF16).reshape(HEIGHT, LANE, DIM)
            news = (dot(act_in, dg, 0, 0), dot(act_in, du, 0, 0), dot(act, dm, 0, 0))
            for ref, new in zip((grad_gate, grad_up, grad_down), news):
                ref[...] = new if half == 0 else ref[...] + new
        level_scatter(parts, total, *scratch[:HEIGHT], *scratch[6:], place)
        both = jnp.concatenate([grad_gate[...].reshape(NDEV, GROWS, UNITS), grad_up[...].reshape(NDEV, GROWS, UNITS)], axis=1)
        ggu_ref[...] = both.astype(BF16)
        gd_ref[...] = grad_down[...].astype(BF16).reshape(HEIGHT, DROWS, DIM)
        x = x_ref[...] * emb_scale
        dx_ref[...] = (dh + rms_backward(x, rms_inv(x), gm_ref[...], total[...])).astype(BF16)

    return pl.pallas_call(
        kernel,
        out_shape=(jax.ShapeDtypeStruct((LANE, DIM), BF16), jax.ShapeDtypeStruct((NDEV, PAIR, UNITS), BF16),
                   jax.ShapeDtypeStruct((HEIGHT, DROWS, DIM), BF16)),
        in_specs=[VSPEC] * 10, out_specs=(VSPEC,) * TOP,
        scratch_shapes=[pltpu.VMEM((LEVEL, LANE, DIM), BF16), pltpu.VMEM((DIM, UNITS), F32), pltpu.VMEM((DIM, UNITS), F32),
                        pltpu.VMEM((UNITS, DIM), F32)] + LEVEL_SCRATCH,
        compiler_params=pltpu.CompilerParams(collective_id=cid, has_side_effects=True, vmem_limit_bytes=VMEM_CAP),
        name='mlp_backward',
    )(dhn, x_raw, h, a_all, g_all, u_all, w_gu, w_dn, gain_mlp, gain_final)


def solution(mesh):
    group = mesh.shape['fsdp']

    def local_step(ids_blk, lab_blk, emb_shard, gate_shard, up_shard, down_shard, gain_mlp, gain_final):
        model_dim = emb_shard.shape[1]
        emb_scale = math.sqrt(model_dim)
        inv_count = 1.0 / (ids_blk.size * group)
        gm, gf = gain_mlp.reshape(1, -1), gain_final.reshape(1, -1)
        emb_pad = jnp.pad(emb_shard, ((0, VPAD - VROWS), (0, 0)))
        tok_blk = jnp.concatenate([ids_blk, lab_blk, jnp.zeros((6, LANE), jnp.int32)], axis=0)
        pieces = jnp.concatenate([gate_shard, up_shard], axis=0).reshape(PAIR, HEIGHT, LEVEL, DROWS)
        pieces = pieces.transpose(TWO, 0, 1, TOP).reshape(LEVEL, PAIR, UNITS)
        w_gu, w_dn = weights_call(pieces, down_shard, 0)
        toks = gather_call(tok_blk, 1)
        x_raw = scatter_call(lookup_call(toks, emb_pad), TWO)
        hid_norm, h, a_all, g_all, u_all = mlp_forward_call(x_raw, w_gu, w_dn, gm, gf, emb_scale, LEVEL)
        hid_all = gather_call(hid_norm, TOP)
        local_lse, lab_part = head_forward_call(toks, emb_pad, hid_all)
        stats = gather_call(jnp.concatenate([local_lse, lab_part], axis=0), HEIGHT)
        d_hid, d_head, loss = head_backward_call(toks, emb_pad, hid_all, stats, inv_count)
        dhn = scatter_call(d_hid, 5)
        d_x, g_gu, g_dn = mlp_backward_call(dhn, x_raw, h, a_all, g_all, u_all, w_gu, w_dn, gm, gf, emb_scale, 9)
        d_gu, d_down = grads_call(g_gu, g_dn, 6)
        dx_all = gather_call(d_x, 7)
        d_embed = scatter_rows_call(toks, d_head, dx_all, emb_scale)
        d_gu = d_gu.reshape(LEVEL, PAIR, HEIGHT, DROWS).transpose(1, TWO, 0, TOP).reshape(PAIR, 3072)
        return loss[0, 0], d_embed, d_gu[0:GROWS], d_gu[GROWS:PAIR], d_down

    shard_spec = P('fsdp', None)
    return jax.shard_map(local_step, mesh=mesh, in_specs=(shard_spec, shard_spec, shard_spec, shard_spec, shard_spec, shard_spec, P(), P()), out_specs=(P(), shard_spec, shard_spec, shard_spec, shard_spec), check_vma=False)
```

time: 487 us -> 414 us (0.85)
  Pallas kernels: 469 us -> 396 us
    pallas_call x3 -> x2, Pallas kernels: 194 us -> 70.9 us  [scatter_call(): pl.pallas_call(kernel, out_shape=jax.ShapeDtypeStruct((rows, cols), F32),...]
    pallas_call x1 -> x3, Pallas kernels: 11 us -> 111 us  [the longest x1 40.9 us: grads_call(): pl.pallas_call(kernel, out_shape=(jax.ShapeDtypeStruct((LEVEL, PAIR, UNIT...]
    pallas_call x5 -> x4, Pallas kernels: 181 us -> 117 us  [gather_call(): pl.pallas_call(kernel, out_shape=jax.ShapeDtypeStruct((NDEV, rows, cols),...]
    pallas_call x1, Pallas kernels: 19.8 us -> 34.3 us  [mlp_backward_call(): pl.pallas_call(kernel, out_shape=(jax.ShapeDtypeStruct((LANE, DIM), BF16)...]
where the time goes in v2:
time: 414 us; the launch traced here: 413 us
  Pallas kernels  396 us (96%)
  local copies, waits for them, and re-layouts  12.6 us (3%)
    pallas_call x4, Pallas kernels, gather_call(): pl.pallas_call(kernel, out_shape=jax.ShapeDtypeStruct((NDEV, rows, cols),...  117 us
    pallas_call x2, Pallas kernels, scatter_call(): pl.pallas_call(kernel, out_shape=jax.ShapeDtypeStruct((rows, cols), F32),...  70.9 us
    pallas_call x1, Pallas kernels, grads_call(): pl.pallas_call(kernel, out_shape=(jax.ShapeDtypeStruct((LEVEL, PAIR, UNIT...  40.9 us
    pallas_call x1, Pallas kernels, weights_call(): pl.pallas_call(kernel, out_shape=(jax.ShapeDtypeStruct((NDEV, PAIR, UNITS...  38.2 us
    pallas_call x1, Pallas kernels, mlp_backward_call(): pl.pallas_call(kernel, out_shape=(jax.ShapeDtypeStruct((LANE, DIM), BF16)...  34.3 us
    pallas_call x1, Pallas kernels, mlp_forward_call(): pl.pallas_call(kernel, out_shape=(act, act, jax.ShapeDtypeStruct((LEVEL,...  31.8 us
    pallas_call x1, Pallas kernels, head_backward_call(): pl.pallas_call(kernel, grid=(NDEV // TILE,), out_shape=(jax.ShapeDtypeStr...  26 us
    pallas_call x1, Pallas kernels, head_forward_call(): pl.pallas_call(kernel, grid=(NDEV // TILE,), out_shape=(jax.ShapeDtypeStr...  13.8 us

profile of v2, /device:TPU:0, one launch (start us, length us, event | category | flops | bytes accessed | tf_op | source)
XLA Modules:
  0.0 413.3 jit_solution(4708883291471385806)
XLA Ops:
  0.6 0.1 pad.11.clone
  0.7 1.3 reshape.30.gm_ref
  2.0 1.3 reshape.31.gf_ref
  3.3 1.3 add_add_fusion.in_ref
  4.6 21.6 %gather1.1.tok_ref = s32[32,8,128]{2,1,0:T(8,128)} custom-call(s32[8,128]{1,0:T(8,128)} %add_add_fusion.in_ref), custom_call_target="tpu_custom_call" | custom-call | tf_op jit(solution)/shard_map/gather1/pallas_call | solution.py:181
  26.2 1.0 pad_maximum_fusion
  27.2 0.4 reshape.28
  27.5 0.2 copy.17
  27.7 1.0 reshape.29.piece_ref
  28.7 38.2 %weights.1 = (bf16[32,48,384]{2,1,0:T(8,128)(2,1)}, bf16[4,96,768]{2,1,0:T(8,128)(2,1)}) custom-call(bf16[8,48,384]{2,1,0:T(8,128)(2,1)} %reshape.29.piece_ref, bf16[96,768]{1,0:T(8,128)(2,1)} %down_ref.1), custom_call_target="tpu_custom_call" | custom-call | tf_op jit(solution)/shard_map/weights/pallas_call | solution.py:557
  66.9 2.6 pad.4.emb_ref
  69.5 10.8 %lookup.1.in_ref = bf16[32,128,768]{2,1,0:T(8,128)(2,1)} custom-call(s32[32,8,128]{2,1,0:T(8,128)} %gather1.1.tok_ref, bf16[1024,768]{1,0:T(8,128)(2,1)} %pad.4.emb_ref), custom_call_target="tpu_custom_call" | custom-call | flops 6400000000 | bytes 8000000 | tf_op jit(solution)/shard_map/lookup/pallas_call | solution.py:378
  80.3 35.6 %scatter2.1.x_ref = f32[128,768]{1,0:T(8,128)} custom-call(bf16[32,128,768]{2,1,0:T(8,128)(2,1)} %lookup.1.in_ref), custom_call_target="tpu_custom_call" | custom-call | tf_op jit(solution)/shard_map/scatter2/pallas_call | solution.py:337
  116.0 31.8 %mlp_forward.1 = (bf16[128,768]{1,0:T(8,128)(2,1)}, bf16[128,768]{1,0:T(8,128)(2,1)}, bf16[8,128,768]{2,1,0:T(8,128)(2,1)}, bf16[8,128,384]{2,1,0:T(8,128)(2,1)}, bf16[8,128,384]{2,1,0:T(8,128)(2,1)}) custom-call(f32[128,768]{1,0:T(8,128)} %scatter2.1.x_ref, bf16[32,48,384]{2,1,0:T(8,128)(2,1)} %get-tuple-element.22.wgu_ref, ...), custom_call_target="tpu_custom_call" | custom-call | tf_op jit(solution)/shard_map/mlp_forward/pallas_call | solution.py:789
  147.8 37.2 %gather3.1.hid_ref = bf16[32,128,768]{2,1,0:T(8,128)(2,1)} custom-call(bf16[128,768]{1,0:T(8,128)(2,1)} %get-tuple-element.24.in_ref), custom_call_target="tpu_custom_call" | custom-call | tf_op jit(solution)/shard_map/gather3/pallas_call | solution.py:181
  185.0 13.8 %head_forward.1 = (f32[32,128]{1,0:T(8,128)}, f32[8,128]{1,0:T(8,128)}) custom-call(s32[32,8,128]{2,1,0:T(8,128)} %gather1.1.tok_ref, bf16[1024,768]{1,0:T(8,128)(2,1)} %pad.4.emb_ref, bf16[32,128,768]{2,1,0:T(8,128)(2,1)} %gather3.1.hid_ref), custom_call_target="tpu_custom_call" | custom-call | flops 6400000000 | bytes 8000000 | tf_op jit(solution)/shard_map/head_forward/pallas_call | solution.py:412
  198.7 1.3 pad_maximum_fusion.1.in_ref
  200.1 19.2 %gather4.1.stat_ref = f32[32,40,128]{2,1,0:T(8,128)} custom-call(f32[40,128]{1,0:T(8,128)} %pad_maximum_fusion.1.in_ref), custom_call_target="tpu_custom_call" | custom-call | tf_op jit(solution)/shard_map/gather4/pallas_call | solution.py:181
  219.2 26.0 %head_backward.1 = (bf16[32,128,768]{2,1,0:T(8,128)(2,1)}, f32[1024,768]{1,0:T(8,128)}, f32[8,128]{1,0:T(8,128)}) custom-call(s32[32,8,128]{2,1,0:T(8,128)} %gather1.1.tok_ref, bf16[1024,768]{1,0:T(8,128)(2,1)} %pad.4.emb_ref, bf16[32,128,768]{2,1,0:T(8,128)(2,1)} %gather3.1.hid_ref, f32[32,40,128]{2,1,0:T(8,128)} %gather4.1.stat_ref), custom_call_target="tpu_custom_call" | custom-call | flops 19299999744 | bytes 17000000 | tf_op jit(solution)/shard_map/head_backward/pallas_call | solution.py:448
  245.2 1.2 slice.15
  246.4 35.3 %scatter5.1.dhn_ref = f32[128,768]{1,0:T(8,128)} custom-call(bf16[32,128,768]{2,1,0:T(8,128)(2,1)} %get-tuple-element.29.in_ref), custom_call_target="tpu_custom_call" | custom-call | tf_op jit(solution)/shard_map/scatter5/pallas_call | solution.py:337
  281.8 34.3 %mlp_backward.1 = (bf16[128,768]{1,0:T(8,128)(2,1)}, bf16[32,48,384]{2,1,0:T(8,128)(2,1)}, bf16[4,96,768]{2,1,0:T(8,128)(2,1)}) custom-call(f32[128,768]{1,0:T(8,128)} %scatter5.1.dhn_ref, f32[128,768]{1,0:T(8,128)} %scatter2.1.x_ref, bf16[128,768]{1,0:T(8,128)(2,1)} %get-tuple-element.30.h_ref, bf16[8,128,768]{2,1,0:T(8,128)(2,1)} %get-tuple-element.31.a_ref, ...), custom_call_target="tpu_custom_call" | custom-call | tf_op jit(solution)/shard_map/mlp_backward/pallas_call | solution.py:832
  316.1 40.9 %grads.1 = (f32[8,48,384]{2,1,0:T(8,128)}, f32[96,768]{1,0:T(8,128)}) custom-call(bf16[32,48,384]{2,1,0:T(8,128)(2,1)} %get-tuple-element.35.gu_ref, bf16[4,96,768]{2,1,0:T(8,128)(2,1)} %get-tuple-element.36.gd_ref), custom_call_target="tpu_custom_call" | custom-call | tf_op jit(solution)/shard_map/grads/pallas_call | solution.py:659
  357.0 1.5 reshape.32
  358.5 0.1 fusion
  358.6 0.2 copy.15
  358.8 0.9 slice.19
  359.7 0.2 copy.14
  360.0 0.9 slice.17
  360.9 38.8 %gather7.1.dx_ref = bf16[32,128,768]{2,1,0:T(8,128)(2,1)} custom-call(bf16[128,768]{1,0:T(8,128)(2,1)} %get-tuple-element.34.in_ref), custom_call_target="tpu_custom_call" | custom-call | tf_op jit(solution)/shard_map/gather7/pallas_call | solution.py:181
  399.7 0.0 copy-start
  399.7 12.9 %scatter_rows.1 = f32[1004,768]{1,0:T(8,128)} custom-call(s32[32,8,128]{2,1,0:T(8,128)} %gather1.1.tok_ref, f32[1024,768]{1,0:T(8,128)} %get-tuple-element.28.head_ref, bf16[32,128,768]{2,1,0:T(8,128)(2,1)} %gather7.1.dx_ref), custom_call_target="tpu_custom_call" | custom-call | flops 6400000000 | bytes 13000000 | tf_op jit(solution)/shard_map/scatter_rows/pallas_call | solution.py:477
  412.6 0.0 copy-done
  412.6 0.7 copy.19
  (1 shorter events, 0.0 us)
Async XLA Ops:
  399.7 12.9 %copy-start = (f32[96,768]{1,0:T(8,128)S(1)}, f32[96,768]{1,0:T(8,128)}, u32[]{:S(2)}) copy-start(f32[96,768]{1,0:T(8,128)} %get-tuple-element.50) | copy-start | bytes 884740

commit v3 on v0

v3 whole, which is shorter than its diff:
```python
import math
import jax
import jax.numpy as jnp
from jax import lax
from jax.experimental import pallas as pl
from jax.experimental.pallas import tpu as pltpu
from jax.sharding import PartitionSpec as P

NORM_EPS = 1e-6
MESH = pl.DeviceIdType.MESH
F32 = jnp.float32
BF16 = jnp.bfloat16
VMEM_CAP = 63 * 1024 * 1024
LANE = 128
DIM = 768
PAIR = 48
UNITS = 384
NDEV = 32
LEVEL = 8
HEIGHT = 4
DROWS = 96
CHIPS = 16
GROWS = 24
TWO = 2
TOP = 3
VSPEC = pl.BlockSpec(memory_space=pltpu.VMEM)


def my_place():
    me = lax.axis_index('fsdp')
    core = lax.rem(me, TWO)
    x = lax.rem(lax.div(me, TWO), TWO)
    y = lax.rem(lax.div(me, HEIGHT), TWO)
    z = lax.div(me, LEVEL)
    p = x * (1 - core) + y * core
    q = y * (1 - core) + x * core
    return me, z, p, q, core


def chip_of(z, p, q, core):
    x = p * (1 - core) + q * core
    y = q * (1 - core) + p * core
    return (z * TWO + y) * TWO + x


def device_of(z, p, q, core):
    return chip_of(z, p, q, core) * TWO + core


def barrier_peers(place):
    me, z = place[0], place[1]
    sem = pltpu.get_barrier_semaphore()
    for step in range(1, LEVEL):
        dev = z * LEVEL + lax.rem(me + step, LEVEL)
        pl.semaphore_signal(sem, inc=1, device_id=(dev,), device_id_type=MESH)
    for step in range(1, HEIGHT):
        dev = lax.rem(me + LEVEL * step, NDEV)
        pl.semaphore_signal(sem, inc=1, device_id=(dev,), device_id_type=MESH)
    pl.semaphore_wait(sem, 10)


def far_level(z, at):
    half = lax.div(z, TWO)
    inner = lax.rem(z + half, TWO)
    order = (TOP - TOP * half, (1 - inner) * (TWO - half) + inner * TOP * half, 1 + lax.rem(z, TWO), z)
    if isinstance(at, int):
        return order[at]
    low, high = lax.rem(at, TWO), lax.div(at, TWO)
    return ((1 - low) * (1 - high) * order[0] + low * (1 - high) * order[1]
            + (1 - low) * high * order[TWO] + low * high * order[TOP])


def remote(src, dst, sems, slot, dev):
    return pltpu.make_async_remote_copy(
        src_ref=src, dst_ref=dst, send_sem=sems.at[0, slot], recv_sem=sems.at[1, slot],
        device_id=(dev,), device_id_type=MESH)


def sem_pair(n):
    return pltpu.SemaphoreType.DMA((TWO, n))


def gather_levels(in_ref, out_ref, send_sem, recv_sem, place, work):
    me, z, p, q, core = place
    peers = (me + LEVEL, me - LEVEL, device_of(z, 1 - p, q, core), device_of(z, p, 1 - q, core), me + 1 - TWO * core)

    def desc(block, way, src=None):
        return pltpu.make_async_remote_copy(
            src_ref=out_ref.at[block] if src is None else src, dst_ref=out_ref.at[block],
            send_sem=send_sem.at[way, block], recv_sem=recv_sem.at[block],
            device_id=(peers[way],), device_id_type=MESH)

    def got(block):
        desc(block, HEIGHT).wait_recv()

    pl.when(z < TOP)(lambda: desc(me, 0, in_ref).start())
    pl.when(z > 0)(lambda: desc(me, 1, in_ref).start())
    for way in (TOP, TWO, HEIGHT):
        desc(me, way, in_ref).start()
    out_ref[me] = in_ref[...]

    def take_z(level):
        block = device_of(level, p, q, core)
        got(block)
        pl.when(jnp.logical_and(level < z, z < TOP))(lambda: desc(block, 0).start())
        pl.when(jnp.logical_and(level > z, z > 0))(lambda: desc(block, 1).start())
        for way in (TOP, TWO, HEIGHT):
            desc(block, way).start()

    def take_p(level):
        block = device_of(level, 1 - p, q, core)
        got(block)
        for way in (TOP, HEIGHT):
            desc(block, way).start()

    def take_q(level):
        for mid in (p, 1 - p):
            block = device_of(level, mid, 1 - q, core)
            got(block)
            desc(block, HEIGHT).start()
        for chip in range(HEIGHT):
            got(level * LEVEL + chip * TWO + 1 - core)

    def step(t, carry):
        pl.when(t < TOP)(lambda: take_z(far_level(z, TWO - lax.rem(t, TOP))))
        pl.when(t < HEIGHT)(lambda: take_p(far_level(z, TOP - lax.rem(t, HEIGHT))))

        @pl.when(t > 0)
        def _():
            level = far_level(z, HEIGHT - (t + lax.div(HEIGHT - t, HEIGHT)))
            take_q(level)
            work(t, level)
        return carry

    lax.fori_loop(0, 5, step, 0)
    for level in range(HEIGHT):
        desc(device_of(level, p, q, core), TWO).wait_send()
        for mid in range(TWO):
            desc(device_of(level, mid, q, core), TOP).wait_send()
        pl.when(jnp.logical_and(z < TOP, level <= z))(lambda: desc(device_of(level, p, q, core), 0).wait_send())
        pl.when(jnp.logical_and(z > 0, level >= z))(lambda: desc(device_of(level, p, q, core), 1).wait_send())
    for chip in range(CHIPS):
        desc(chip * TWO + core, HEIGHT).wait_send()


def add_into(dst, srcs, rows):
    step = 32

    def body(i, carry):
        sl = pl.ds(pl.multiple_of(i * step, step), step)
        total = srcs[0][sl, :].astype(F32)
        for src in srcs[1:]:
            total = total + src[sl, :].astype(F32)
        dst[sl, :] = total.astype(dst.dtype)
        return carry

    lax.fori_loop(0, rows // step, body, 0)


def scatter_scratch(rows, cols):
    return [
        pltpu.VMEM((CHIPS, rows, cols), BF16), pltpu.VMEM((LEVEL, rows, cols), BF16), pltpu.VMEM((HEIGHT, rows, cols), BF16),
        pltpu.VMEM((HEIGHT, rows, cols), BF16), pltpu.VMEM((HEIGHT, rows, cols), BF16), pltpu.VMEM((CHIPS, rows, cols), BF16),
        pltpu.VMEM((rows, cols), F32),
        pltpu.SemaphoreType.DMA((TWO, CHIPS)), pltpu.SemaphoreType.DMA((TWO, LEVEL)), pltpu.SemaphoreType.DMA((TWO, HEIGHT)),
        pltpu.SemaphoreType.DMA((TWO, HEIGHT)), pltpu.SemaphoreType.DMA((TWO, HEIGHT)),
    ]


def scatter_levels(in_ref, out_ref, scratch, place, work):
    from_core, from_q, from_p, from_low, from_high, outgo, acc, sem_c, sem_q, sem_p, sem_up, sem_dn = scratch
    me, z, p, q, core = place
    rows = out_ref.shape[0]
    other = 1 - core

    def core_copy(chip):
        return remote(in_ref.at[chip * TWO + other], from_core.at[chip], sem_c, chip, me + 1 - TWO * core)

    def local(level, mid, last):
        return level * HEIGHT + mid * TWO + last

    def q_copy(level, mid):
        return remote(outgo.at[local(level, mid, 1 - q)], from_q.at[level * TWO + mid], sem_q, level * TWO + mid,
                      device_of(z, p, 1 - q, core))

    def p_copy(level):
        return remote(outgo.at[local(level, 1 - p, q)], from_p.at[level], sem_p, level, device_of(z, 1 - p, q, core))

    def up_copy(level):
        return remote(outgo.at[local(level, p, q)], from_low.at[level], sem_up, level, me + LEVEL)

    def dn_copy(level):
        return remote(outgo.at[local(level, p, q)], from_high.at[level], sem_dn, level, me - LEVEL)

    def own(level, mid, last):
        chip = chip_of(level, mid, last, core)
        core_copy(chip).wait_recv()
        return [in_ref.at[chip * TWO + core], from_core.at[chip]]

    def make(level):
        work(level)
        for last in (1 - p, p):
            for mid in (1 - q, q):
                core_copy(chip_of(level, mid, last, other)).start()

    def send_q(level):
        for mid in (1 - p, p):
            add_into(outgo.at[local(level, mid, 1 - q)], own(level, mid, 1 - q), rows)
            q_copy(level, mid).start()

    def send_p(level):
        side = own(level, 1 - p, q)
        q_copy(level, 1 - p).wait_recv()
        add_into(outgo.at[local(level, 1 - p, q)], side + [from_q.at[level * TWO + 1 - p]], rows)
        p_copy(level).start()

    def gather_here(level):
        mine = own(level, p, q)
        q_copy(level, p).wait_recv()
        p_copy(level).wait_recv()
        return mine + [from_q.at[level * TWO + p], from_p.at[level]]

    def send_z(level):
        add_into(acc, gather_here(level), rows)

        @pl.when(level > z)
        def _():
            @pl.when(z > 0)
            def _():
                up_copy(level).wait_recv()
                add_into(acc, [acc, from_low.at[level]], rows)
            add_into(outgo.at[local(level, p, q)], [acc], rows)
            up_copy(level).start()

        @pl.when(level < z)
        def _():
            @pl.when(z < TOP)
            def _():
                dn_copy(level).wait_recv()
                add_into(acc, [acc, from_high.at[level]], rows)
            add_into(outgo.at[local(level, p, q)], [acc], rows)
            dn_copy(level).start()

    def level_at(t):
        return far_level(z, lax.rem(t, HEIGHT))

    def step(t, carry):
        pl.when(t < HEIGHT)(lambda: make(level_at(t)))
        pl.when(jnp.logical_and(t > 0, t < 5))(lambda: send_q(level_at(t + TOP)))
        pl.when(jnp.logical_and(t > 1, t < 6))(lambda: send_p(level_at(t + TWO)))
        pl.when(t > TWO)(lambda: send_z(level_at(t + 1)))
        return carry

    lax.fori_loop(0, 6, step, 0)
    add_into(out_ref, gather_here(z), rows)

    @pl.when(z > 0)
    def _():
        up_copy(z).wait_recv()
        add_into(out_ref, [out_ref, from_low.at[z]], rows)

    @pl.when(z < TOP)
    def _():
        dn_copy(z).wait_recv()
        add_into(out_ref, [out_ref, from_high.at[z]], rows)

    for chip in range(CHIPS):
        core_copy(chip).wait_send()
    for level in range(HEIGHT):
        for mid in range(TWO):
            q_copy(level, mid).wait_send()
        p_copy(level).wait_send()
        pl.when(level > z)(lambda: up_copy(level).wait_send())
        pl.when(level < z)(lambda: dn_copy(level).wait_send())


def rank_of(p, q, core):
    return device_of(0, p, q, core)


def level_gather(in_ref, out_ref, send_sem, recv_sem, place):
    me, z, p, q, core = place
    rank = lax.rem(me, LEVEL)
    peers = (device_of(z, 1 - p, q, core), device_of(z, p, 1 - q, core), me + 1 - TWO * core)

    def desc(block, way, src=None):
        return pltpu.make_async_remote_copy(
            src_ref=out_ref.at[block] if src is None else src, dst_ref=out_ref.at[block],
            send_sem=send_sem.at[way * LEVEL + block], recv_sem=recv_sem.at[block],
            device_id=(peers[way],), device_id_type=MESH)

    for way in (1, 0, TWO):
        desc(rank, way, in_ref).start()
    out_ref[rank] = in_ref[...]
    side = rank_of(1 - p, q, core)
    desc(side, 0).wait_recv()
    for way in (1, TWO):
        desc(side, way).start()
    for mid in (p, 1 - p):
        block = rank_of(mid, 1 - q, core)
        desc(block, 1).wait_recv()
        desc(block, TWO).start()
    for chip in range(HEIGHT):
        desc(chip * TWO + 1 - core, TWO).wait_recv()
    desc(rank, 0, in_ref).wait_send()
    desc(rank, 1, in_ref).wait_send()
    desc(side, 1).wait_send()
    for chip in range(HEIGHT):
        desc(chip * TWO + core, TWO).wait_send()


def level_scatter(in_ref, out_ref, from_core, from_q, from_p, outgo, sem_s, sem_r, place):
    me, z, p, q, core = place
    rows = out_ref.shape[0]

    def copy(src, dst, slot, dev):
        return pltpu.make_async_remote_copy(
            src_ref=src, dst_ref=dst, send_sem=sem_s.at[slot], recv_sem=sem_r.at[slot],
            device_id=(dev,), device_id_type=MESH)

    def core_copy(chip):
        return copy(in_ref.at[chip * TWO + 1 - core], from_core.at[chip], chip, me + 1 - TWO * core)

    def q_copy(mid):
        return copy(outgo.at[mid], from_q.at[mid], HEIGHT + mid, device_of(z, p, 1 - q, core))

    def p_copy():
        return copy(outgo.at[TWO], from_p, 6, device_of(z, 1 - p, q, core))

    def own(mid, last):
        chip = chip_of(0, mid, last, core)
        core_copy(chip).wait_recv()
        return [in_ref.at[chip * TWO + core], from_core.at[chip]]

    for last in (1 - p, p):
        for mid in (1 - q, q):
            core_copy(chip_of(0, mid, last, 1 - core)).start()
    for mid in (1 - p, p):
        add_into(outgo.at[mid], own(mid, 1 - q), rows)
        q_copy(mid).start()
    side = own(1 - p, q)
    q_copy(1 - p).wait_recv()
    add_into(outgo.at[TWO], side + [from_q.at[1 - p]], rows)
    p_copy().start()
    mine = own(p, q)
    q_copy(p).wait_recv()
    p_copy().wait_recv()
    add_into(out_ref, mine + [from_q.at[p], from_p], rows)
    for chip in range(HEIGHT):
        core_copy(chip).wait_send()
    for mid in range(TWO):
        q_copy(mid).wait_send()
    p_copy().wait_send()


def dot(left, right, ld, rd):
    return lax.dot_general(left, right, (((ld,), (rd,)), ((), ())), preferred_element_type=F32)


TOKS = 512
VPAD = 1024
VROWS = 1004


def id_rows(tok_ref, row, first):
    ids = jnp.concatenate([tok_ref[first + t, row:row + 1, :] for t in range(HEIGHT)], axis=1) - shard_start()
    return jnp.where(jnp.logical_and(ids >= 0, ids < VROWS), ids, -1)


def vocab_iota():
    return lax.broadcasted_iota(jnp.int32, (VPAD, TOKS), 0)


def shard_start():
    return lax.axis_index('fsdp') * VROWS


def fill_table(table, emb_ref):
    table[VPAD - 32:VPAD, :] = jnp.zeros((32, DIM), BF16)
    table[0:VROWS, :] = emb_ref[...]


def halves(level, body):
    def one(i, carry):
        body(level * LEVEL + i * HEIGHT)
        return carry
    lax.fori_loop(0, TWO, one, 0)


def rms_inv(values):
    return lax.rsqrt(jnp.mean(values * values, axis=-1, keepdims=True) + NORM_EPS)


def rms_backward(values, inv_rms, gain_vec, grad_out):
    scaled = grad_out * gain_vec
    return inv_rms * scaled - values * (inv_rms ** TOP) * jnp.mean(scaled * values, axis=-1, keepdims=True)


LEVEL_SCRATCH = [
    pltpu.VMEM((LANE, DIM), BF16), pltpu.VMEM((LEVEL, LANE, DIM), BF16), pltpu.VMEM((LANE, DIM), F32),
    pltpu.VMEM((HEIGHT, LANE, DIM), BF16), pltpu.VMEM((TWO, LANE, DIM), BF16), pltpu.VMEM((LANE, DIM), BF16),
    pltpu.VMEM((TOP, LANE, DIM), BF16),
    pltpu.SemaphoreType.DMA((GROWS,)), pltpu.SemaphoreType.DMA((LEVEL,)),
    pltpu.SemaphoreType.DMA((7,)), pltpu.SemaphoreType.DMA((7,)),
]


def split_weights(gu_ref):
    wide = gu_ref[...].astype(F32)
    return (wide[:, 0:GROWS, :].reshape(DIM, UNITS).astype(BF16), wide[:, GROWS:PAIR, :].reshape(DIM, UNITS).astype(BF16))


GU_SHAPE = (NDEV, PAIR, UNITS)
WD_SHAPE = (HEIGHT, DROWS, DIM)


def call(kernel, name, cid, outs, ins, scratch):
    return pl.pallas_call(
        kernel, out_shape=outs, in_specs=[VSPEC] * len(ins), out_specs=(VSPEC,) * len(outs), scratch_shapes=scratch,
        compiler_params=pltpu.CompilerParams(collective_id=cid, has_side_effects=True, vmem_limit_bytes=VMEM_CAP),
        name=name)(*ins)


def start_call(ids, labs, emb, pieces, down_shard, gain_mlp, gain_final, emb_scale):
    def kernel(ids_ref, lab_ref, emb_ref, piece_ref, down_ref, gm_ref, gf_ref,
               tok_ref, x_ref, gu_ref, wd_ref, hn_ref, h_ref, a_ref, g_ref, u_ref,
               tok_mine, table, rows, sem_t, sem_a, z_send, z_recv, d_send, d_recv, *scratch):
        ring, (mine, parts, total, *level) = scratch[:12], scratch[12:]
        place = my_place()
        me, z, p, q, core = place
        rank = lax.rem(me, LEVEL)
        tok_mine[...] = jnp.zeros((LEVEL, LANE), jnp.int32)
        tok_mine[0:1, :] = ids_ref[...]
        tok_mine[1:TWO, :] = lab_ref[...]
        barrier_peers(place)

        def exchange(step):
            peer = lax.rem(rank + step, LEVEL)
            return remote(piece_ref.at[peer], gu_ref.at[me], sem_a, step, z * LEVEL + peer)

        def slab(lv, way):
            part = gu_ref.at[pl.ds(lv * LEVEL, LEVEL)]
            return pltpu.make_async_remote_copy(
                src_ref=part, dst_ref=part, send_sem=z_send.at[way * HEIGHT + lv], recv_sem=z_recv.at[lv],
                device_id=(me + LEVEL - CHIPS * way,), device_id_type=MESH)

        def slab_down(lv, way, src):
            return pltpu.make_async_remote_copy(
                src_ref=src, dst_ref=wd_ref.at[lv], send_sem=d_send.at[way * HEIGHT + lv], recv_sem=d_recv.at[lv],
                device_id=(me + LEVEL - CHIPS * way,), device_id_type=MESH)

        pair = remote(tok_mine, tok_ref.at[me], sem_t, 0, me + 1 - TWO * core)
        pair.start()
        for step in range(1, LEVEL):
            exchange(step).start()
        pl.when(z < TOP)(lambda: slab_down(z, 0, down_ref).start())
        pl.when(z > 0)(lambda: slab_down(z, 1, down_ref).start())
        tok_ref[me] = tok_mine[...]
        wd_ref[z] = down_ref[...]
        gu_ref[me] = piece_ref[rank]
        fill_table(table, emb_ref)
        pair.wait()
        for stage, (size, dev) in enumerate(((TWO, device_of(z, *flip_x(p, q, core))), (HEIGHT, device_of(z, *flip_y(p, q, core))))):
            part = tok_ref.at[pl.ds(lax.div(me, size) * size, size)]
            ship = remote(part, part, sem_t, stage + 1, dev)
            ship.start()
            ship.wait()
        part = tok_ref.at[pl.ds(z * LEVEL, LEVEL)]
        ships = [remote(part, part, sem_t, TWO + step, lax.rem(me + LEVEL * step, NDEV)) for step in range(1, HEIGHT)]
        for ship in ships:
            ship.start()
        for ship in ships:
            ship.wait()
        for step in range(1, LEVEL):
            exchange(step).wait_recv()
        pl.when(z < TOP)(lambda: slab(z, 0).start())
        pl.when(z > 0)(lambda: slab(z, 1).start())

        def take(lv, way, more):
            slab_down(lv, 0, wd_ref.at[lv]).wait_recv()
            pl.when(more)(lambda: slab_down(lv, way, wd_ref.at[lv]).start())
            slab(lv, 0).wait_recv()
            pl.when(more)(lambda: slab(lv, way).start())

        def take_far(far):
            pl.when(z - far >= 0)(lambda: take(z - far, 0, z < TOP))
            pl.when(z + far < HEIGHT)(lambda: take(z + far, 1, z > 0))

        def find(lv):
            def body(first):
                hit = (vocab_iota() == id_rows(tok_ref, 0, first)).astype(F32).astype(BF16)
                rows[pl.ds(first, HEIGHT)] = dot(hit, table[...], 0, 0).astype(BF16).reshape(HEIGHT, LANE, DIM)
            halves(lv, body)

        scatter_levels(rows, x_ref, ring, place, find)
        take_far(1)
        x = x_ref[...] * emb_scale
        mine[...] = (x * rms_inv(x) * gm_ref[...]).astype(BF16)
        level_gather(mine, a_ref, level[HEIGHT], level[5], place)
        take_far(TWO)
        take_far(TOP)
        wg, wu = split_weights(gu_ref)
        wd = wd_ref[...].reshape(UNITS, DIM)
        for half in range(TWO):
            four = slice(HEIGHT * half, HEIGHT * half + HEIGHT)
            act_in = a_ref[four].reshape(TOKS, DIM)
            g = dot(act_in, wg, 1, 0).astype(BF16)
            u = dot(act_in, wu, 1, 0).astype(BF16)
            g_ref[four] = g.reshape(HEIGHT, LANE, UNITS)
            u_ref[four] = u.reshape(HEIGHT, LANE, UNITS)
            act = (jax.nn.silu(g.astype(F32)) * u.astype(F32)).astype(BF16)
            parts[four] = dot(act, wd, 1, 0).astype(BF16).reshape(HEIGHT, LANE, DIM)
        level_scatter(parts, total, *level[:HEIGHT], *level[6:], place)
        h = (x + total[...].astype(BF16).astype(F32)).astype(BF16)
        h_ref[...] = h
        h32 = h.astype(F32)
        hn_ref[...] = (h32 * rms_inv(h32) * gf_ref[...]).astype(BF16)
        for step in range(1, LEVEL):
            exchange(step).wait_send()

        def sent(lv, way):
            slab(lv, way).wait_send()
            slab_down(lv, way, wd_ref.at[lv]).wait_send()

        for lv in range(HEIGHT):
            pl.when(jnp.logical_and(z < TOP, lv <= z))(lambda: sent(lv, 0))
            pl.when(jnp.logical_and(z > 0, lv >= z))(lambda: sent(lv, 1))

    act = jax.ShapeDtypeStruct((LANE, DIM), BF16)
    unit = jax.ShapeDtypeStruct((LEVEL, LANE, UNITS), BF16)
    return call(
        kernel, 'start', 0,
        (jax.ShapeDtypeStruct((NDEV, LEVEL, LANE), jnp.int32), jax.ShapeDtypeStruct((LANE, DIM), F32),
         jax.ShapeDtypeStruct(GU_SHAPE, BF16), jax.ShapeDtypeStruct(WD_SHAPE, BF16), act, act,
         jax.ShapeDtypeStruct((LEVEL, LANE, DIM), BF16), unit, unit),
        (ids, labs, emb, pieces, down_shard, gain_mlp, gain_final),
        [pltpu.VMEM((LEVEL, LANE), jnp.int32), pltpu.VMEM((VPAD, DIM), BF16), pltpu.VMEM((NDEV, LANE, DIM), BF16),
         sem_pair(6), sem_pair(LEVEL), pltpu.SemaphoreType.DMA((LEVEL,)), pltpu.SemaphoreType.DMA((HEIGHT,)),
         pltpu.SemaphoreType.DMA((LEVEL,)), pltpu.SemaphoreType.DMA((HEIGHT,))] + scatter_scratch(LANE, DIM) + LEVEL_SCRATCH)


def flip_x(p, q, core):
    return p * core + (1 - p) * (1 - core), q * (1 - core) + (1 - q) * core, core


def flip_y(p, q, core):
    return p * (1 - core) + (1 - p) * core, q * core + (1 - q) * (1 - core), core


STAT = 40


def merge_stats(blocks):
    logs = [b[0:32, :] for b in blocks]
    top = logs[0]
    for one in logs[1:]:
        top = jnp.maximum(top, one)
    total = jnp.exp(logs[0] - top)
    labs = blocks[0][32:STAT, :]
    for one, b in zip(logs[1:], blocks[1:]):
        total = total + jnp.exp(one - top)
        labs = labs + b[32:STAT, :]
    return jnp.concatenate([top + jnp.log(total), labs], axis=0)


def head_call(toks, emb, hid_norm, inv_count):
    def kernel(tok_ref, emb_ref, hn_ref, dhn_ref, demb_ref, loss_ref,
               table, hid_all, parts, stat, land, land_z, lse_ref, g_send, g_recv, sem_s, *ring):
        place = my_place()
        me, z, p, q, core = place
        barrier_peers(place)
        fill_table(table, emb_ref)
        stat[...] = jnp.zeros_like(stat)
        demb_ref[...] = jnp.zeros_like(demb_ref)

        def forward(t, lv):
            def body(first):
                logits = dot(table[...], hid_all[pl.ds(first, HEIGHT)].reshape(TOKS, DIM), 1, 1)
                row = vocab_iota()
                lab = jnp.sum(jnp.where(row == id_rows(tok_ref, 1, first), logits, 0.0), axis=0, keepdims=True)
                logits = jnp.where(row < VROWS, logits, -1e30)
                top = jnp.max(logits, axis=0, keepdims=True)
                local = top + jnp.log(jnp.sum(jnp.exp(logits - top), axis=0, keepdims=True))
                for t in range(HEIGHT):
                    stat[0, pl.ds(first + t, 1), :] = local[:, t * LANE:(t + 1) * LANE]
                    stat[0, 32:33, :] = stat[0, 32:33, :] + lab[:, t * LANE:(t + 1) * LANE]
            halves(lv, body)

        gather_levels(hn_ref, hid_all, g_send, g_recv, place, forward)

        devs = (me + 1 - TWO * core, device_of(z, *flip_x(p, q, core)), device_of(z, *flip_y(p, q, core)))
        for stage, dev in enumerate(devs):
            ship = remote(stat.at[stage], land.at[stage], sem_s, stage, dev)
            ship.start()
            ship.wait()
            stat[stage + 1] = merge_stats([stat[stage], land[stage]])
        ships = [remote(stat.at[TOP], land_z.at[z], sem_s, TWO + step, lax.rem(me + LEVEL * step, NDEV)) for step in range(1, HEIGHT)]
        for ship in ships:
            ship.start()
        land_z[z] = stat[TOP]
        for ship in ships:
            ship.wait()
        final = merge_stats([land_z[lv] for lv in range(HEIGHT)])
        lse_ref[...] = final[0:32, :]
        loss_ref[...] = jnp.full((LEVEL, LANE), (jnp.sum(final[0:32, :]) - jnp.sum(final[32:STAT, :])) * inv_count, F32)

        def backward(lv):
            def body(first):
                hid = hid_all[pl.ds(first, HEIGHT)].reshape(TOKS, DIM)
                logits = dot(table[...], hid, 1, 1)
                lse_row = jnp.concatenate([lse_ref[pl.ds(first + t, 1), :] for t in range(HEIGHT)], axis=1)
                row = vocab_iota()
                prob = jnp.exp(jnp.where(row < VROWS, logits, -1e30) - lse_row)
                hit = jnp.where(row == id_rows(tok_ref, 1, first), 1.0, 0.0)
                grad = ((prob - hit) * inv_count).astype(BF16)
                parts[pl.ds(first, HEIGHT)] = dot(grad, table[...], 0, 0).astype(BF16).reshape(HEIGHT, LANE, DIM)
                demb_ref[...] += dot(grad, hid, 1, 0)
            halves(lv, body)

        scatter_levels(parts, dhn_ref, ring, place, backward)

    whole = pltpu.VMEM((NDEV, LANE, DIM), BF16)
    return call(
        kernel, 'head', 1,
        (jax.ShapeDtypeStruct((LANE, DIM), F32), jax.ShapeDtypeStruct((VPAD, DIM), F32), jax.ShapeDtypeStruct((LEVEL, LANE), F32)),
        (toks, emb, hid_norm),
        [pltpu.VMEM((VPAD, DIM), BF16), whole, whole, pltpu.VMEM((HEIGHT, STAT, LANE), F32), pltpu.VMEM((TOP, STAT, LANE), F32),
         pltpu.VMEM((HEIGHT, STAT, LANE), F32), pltpu.VMEM((32, LANE), F32), pltpu.SemaphoreType.DMA((5, NDEV)),
         pltpu.SemaphoreType.DMA((NDEV,)), sem_pair(6)] + scatter_scratch(LANE, DIM))


def end_call(dhn, x_raw, h, a_all, g_all, u_all, w_gu, w_dn, gain_mlp, gain_final, toks, d_head, emb_scale):
    def kernel(dhn_ref, x_ref, h_ref, a_ref, g_ref, u_ref, wgu_ref, wd_ref, gm_ref, gf_ref, tok_ref, head_ref,
               out_ref, own_ref, dn_ref,
               dm_ref, grad_gate, grad_up, grad_down, ggu, gd, d_gate, d_up, acts, dx_ref, dx_all, acc_rows,
               from_low, from_high, low_d, high_d, outgo, outgo_d, acc, g_send, g_recv, sem_a, sem_z, sem_d,
               mine, parts, total, *scratch):
        place = my_place()
        me, z, p, q, core = place
        rank = lax.rem(me, LEVEL)
        barrier_peers(place)
        h32 = h_ref[...].astype(F32)
        dh = rms_backward(h32, rms_inv(h32), gf_ref[...], dhn_ref[...])
        mine[...] = dh.astype(BF16)
        level_gather(mine, dm_ref, scratch[HEIGHT], scratch[5], place)
        wg, wu = split_weights(wgu_ref)
        wd = wd_ref[...].reshape(UNITS, DIM)
        for half in range(TWO):
            four = slice(HEIGHT * half, HEIGHT * half + HEIGHT)
            g = g_ref[four].reshape(TOKS, UNITS).astype(F32)
            u = u_ref[four].reshape(TOKS, UNITS).astype(F32)
            dq = dot(dm_ref[four].reshape(TOKS, DIM), wd, 1, 1)
            sig = jax.nn.sigmoid(g)
            dg = (dq * u * sig * (1.0 + g * (1.0 - sig))).astype(BF16)
            du = (dq * g * sig).astype(BF16)
            d_gate[half] = dg
            d_up[half] = du
            acts[half] = (jax.nn.silu(g) * u).astype(BF16)
            parts[four] = (dot(dg, wg, 1, 1) + dot(du, wu, 1, 1)).astype(BF16).reshape(HEIGHT, LANE, DIM)
        level_scatter(parts, total, *scratch[:HEIGHT], *scratch[6:], place)
        x = x_ref[...] * emb_scale
        dx_ref[...] = (dh + rms_backward(x, rms_inv(x), gm_ref[...], total[...])).astype(BF16)
        acc_rows[...] = jnp.zeros_like(acc_rows)

        def rows_of(ref, lv):
            return ref.at[pl.ds(lv * LEVEL, LEVEL)]

        def add_slab(dst, srcs):
            def body(i, carry):
                value = srcs[0][i].astype(F32)
                for src in srcs[1:]:
                    value = value + src[i].astype(F32)
                dst[i] = value.astype(dst.dtype)
                return carry
            lax.fori_loop(0, LEVEL, body, 0)

        def hop(lv, way):
            land = (from_low, from_high)[way]
            return remote(rows_of(outgo, lv), rows_of(land, lv), sem_z, way * HEIGHT + lv, me + LEVEL - CHIPS * way)

        def hop_d(lv, way):
            land = (low_d, high_d)[way]
            return remote(outgo_d.at[lv], land.at[lv], sem_d, way * HEIGHT + lv, me + LEVEL - CHIPS * way)

        def send(lv, way, more):
            low = rows_of((from_low, from_high)[way], lv)
            low_down = (low_d, high_d)[way].at[lv]

            @pl.when(more)
            def _():
                hop(lv, way).wait_recv()
                add_slab(rows_of(outgo, lv), [rows_of(ggu, lv), low])
                hop_d(lv, way).wait_recv()
                add_into(outgo_d.at[lv], [gd.at[lv], low_down], DROWS)

            @pl.when(jnp.logical_not(more))
            def _():
                add_slab(rows_of(outgo, lv), [rows_of(ggu, lv)])
                add_into(outgo_d.at[lv], [gd.at[lv]], DROWS)
            hop(lv, way).start()
            hop_d(lv, way).start()

        def send_far(far):
            pl.when(z + far < HEIGHT)(lambda: send(z + far, 0, z > 0))
            pl.when(z - far >= 0)(lambda: send(z - far, 1, z < TOP))

        def weight_grads():
            for half in range(TWO):
                four = slice(HEIGHT * half, HEIGHT * half + HEIGHT)
                act_in = a_ref[four].reshape(TOKS, DIM)
                news = (dot(act_in, d_gate[half], 0, 0), dot(act_in, d_up[half], 0, 0),
                        dot(acts[half], dm_ref[four].reshape(TOKS, DIM), 0, 0))
                for ref, new in zip((grad_gate, grad_up, grad_down), news):
                    ref[...] = new if half == 0 else ref[...] + new
            both = jnp.concatenate([grad_gate[...].reshape(NDEV, GROWS, UNITS), grad_up[...].reshape(NDEV, GROWS, UNITS)], axis=1)
            ggu[...] = both.astype(BF16)
            gd[...] = grad_down[...].astype(BF16).reshape(WD_SHAPE)

        def add_rows(t, lv):
            def body(first):
                hit = (vocab_iota() == id_rows(tok_ref, 0, first)).astype(F32).astype(BF16)
                acc_rows[...] += dot(hit, dx_all[pl.ds(first, HEIGHT)].reshape(TOKS, DIM), 1, 0)
            halves(lv, body)

            @pl.when(t == 1)
            def _():
                weight_grads()
                send_far(TOP)
            pl.when(t == TWO)(lambda: send_far(TWO))
            pl.when(t == TOP)(lambda: send_far(1))

        gather_levels(dx_ref, dx_all, g_send, g_recv, place, add_rows)
        out_ref[...] = head_ref[0:VROWS, :] + acc_rows[0:VROWS, :] * emb_scale

        add_slab(acc, [rows_of(ggu, z)])
        add_into(dn_ref, [gd.at[z]], DROWS)

        def last(way):
            hop(z, way).wait_recv()
            add_slab(acc, [acc, rows_of((from_low, from_high)[way], z)])
            hop_d(z, way).wait_recv()
            add_into(dn_ref, [dn_ref, (low_d, high_d)[way].at[z]], DROWS)

        pl.when(z > 0)(lambda: last(0))
        pl.when(z < TOP)(lambda: last(1))

        def exchange(step):
            peer = lax.rem(rank + step, LEVEL)
            return remote(acc.at[peer], own_ref.at[rank], sem_a, step, z * LEVEL + peer)

        for step in range(1, LEVEL):
            exchange(step).start()
        own_ref[rank] = acc[rank]
        for step in range(1, LEVEL):
            exchange(step).wait_recv()
        for step in range(1, LEVEL):
            exchange(step).wait_send()

        def sent(lv, way):
            hop(lv, way).wait_send()
            hop_d(lv, way).wait_send()

        for lv in range(HEIGHT):
            pl.when(lv > z)(lambda: sent(lv, 0))
            pl.when(lv < z)(lambda: sent(lv, 1))

    slab, slab_d = pltpu.VMEM(GU_SHAPE, BF16), pltpu.VMEM(WD_SHAPE, BF16)
    wide, tall = pltpu.VMEM((DIM, UNITS), F32), pltpu.VMEM((UNITS, DIM), F32)
    unit = pltpu.VMEM((TWO, TOKS, UNITS), BF16)
    return call(
        kernel, 'end', TWO,
        (jax.ShapeDtypeStruct((VROWS, DIM), F32), jax.ShapeDtypeStruct((LEVEL, PAIR, UNITS), F32), jax.ShapeDtypeStruct((DROWS, DIM), F32)),
        (dhn, x_raw, h, a_all, g_all, u_all, w_gu, w_dn, gain_mlp, gain_final, toks, d_head),
        [pltpu.VMEM((LEVEL, LANE, DIM), BF16), wide, wide, tall, slab, slab_d, unit, unit, unit, pltpu.VMEM((LANE, DIM), BF16),
         pltpu.VMEM((NDEV, LANE, DIM), BF16), pltpu.VMEM((VPAD, DIM), F32), slab, slab, slab_d, slab_d, slab, slab_d,
         pltpu.VMEM((LEVEL, PAIR, UNITS), F32), pltpu.SemaphoreType.DMA((5, NDEV)), pltpu.SemaphoreType.DMA((NDEV,)),
         sem_pair(LEVEL), sem_pair(LEVEL), sem_pair(LEVEL)] + LEVEL_SCRATCH)


def solution(mesh):
    group = mesh.shape['fsdp']

    def local_step(ids_blk, lab_blk, emb_shard, gate_shard, up_shard, down_shard, gain_mlp, gain_final):
        emb_scale = math.sqrt(emb_shard.shape[1])
        inv_count = 1.0 / (ids_blk.size * group)
        gm, gf = gain_mlp.reshape(1, -1), gain_final.reshape(1, -1)
        pieces = jnp.concatenate([gate_shard, up_shard], axis=0).reshape(PAIR, HEIGHT, LEVEL, DROWS)
        pieces = pieces.transpose(TWO, 0, 1, TOP).reshape(LEVEL, PAIR, UNITS)
        toks, x_raw, w_gu, w_dn, hid_norm, h, a_all, g_all, u_all = start_call(
            ids_blk, lab_blk, emb_shard, pieces, down_shard, gm, gf, emb_scale)
        dhn, d_head, loss = head_call(toks, emb_shard, hid_norm, inv_count)
        d_embed, d_gu, d_down = end_call(dhn, x_raw, h, a_all, g_all, u_all, w_gu, w_dn, gm, gf, toks, d_head, emb_scale)
        d_gu = d_gu.reshape(LEVEL, PAIR, HEIGHT, DROWS).transpose(1, TWO, 0, TOP).reshape(PAIR, 3072)
        return loss[0, 0], d_embed, d_gu[0:GROWS], d_gu[GROWS:PAIR], d_down

    shard_spec = P('fsdp', None)
    return jax.shard_map(local_step, mesh=mesh, in_specs=(shard_spec, shard_spec, shard_spec, shard_spec, shard_spec, shard_spec, P(), P()), out_specs=(P(), shard_spec, shard_spec, shard_spec, shard_spec), check_vma=False)
```

time: 2150 us -> 311 us (0.14)
  blocking collectives: 1110 us -> 0 us
  waiting for transfers between devices: 420 us -> 0 us
  matrix products: 299 us -> 0 us
  Pallas kernels: 0 us -> 296 us
  local copies, waits for them, and re-layouts: 187 us -> 13.6 us
  loops' own time: 43.9 us -> 0 us
  starting transfers between devices: 38.1 us -> 0 us
  other arithmetic: 26 us -> 1 us
    unnamed x1 -> x0, blocking collectives: 1070 us -> none
    all_gather x4 -> x0, waiting for transfers between devices: 418 us -> none  [the longest x1 272 us: local_step(): embed_full = lax.all_gather(emb_shard, 'fsdp', tiled=True)]
    dot_general x137 -> x0, matrix products: 299 us -> none  [the longest x67 140 us: dot_last(): lax.dot_general(left_mat, right_mat, (((1,), (1,)), ((), ())), preferred_...]
    pallas_call x0 -> x3, Pallas kernels: none -> 296 us  [call(): pl.pallas_call(kernel, out_shape=outs, in_specs=[VSPEC] * len(ins), out_s...]
    reshape x1 -> x6, local copies, waits for them, and re-layouts: 95.1 us -> 5.57 us  [the longest x2 2.53 us: local_step(): gm, gf = (gain_mlp.reshape(1, -1), gain_final.reshape(1, -1))]
    unnamed x12 -> x4, local copies, waits for them, and re-layouts: 52.1 us -> 4.48 us
    another operation x2 -> x0, loops' own time: 43.9 us -> none  [the longest x1 22.2 us: head_forward(): lax.scan(chunk_step, start, (emb_chunks, chunk_ids))]
    unnamed x1 -> x0, starting transfers between devices: 37.6 us -> none
  transfers between devices with their start and end apart: 8 -> 0, of which waited for: 4 -> 0; matrix products, arithmetic and copies ran while one was open for 59% -> 0% of each run, Pallas kernels for 0% -> 0%
where the time goes in v3:
time: 311 us
  Pallas kernels  296 us (95%)
  local copies, waits for them, and re-layouts  13.6 us (4%)
    pallas_call x3, Pallas kernels, call(): pl.pallas_call(kernel, out_shape=outs, in_specs=[VSPEC] * len(ins), out_s...  296 us

profile of v3, /device:TPU:0, one launch (start us, length us, event | category | flops | bytes accessed | tf_op | source)
XLA Modules:
  0.0 310.9 jit_solution(3319919920576849240)
XLA Ops:
  0.6 1.0 pad_maximum_fusion
  1.6 0.4 reshape.28
  2.0 0.2 copy.17
  2.2 1.0 reshape.29.piece_ref
  3.2 1.3 reshape.30.gm_ref
  4.4 1.3 reshape.31.gf_ref
  5.7 97.0 %start.1 = (s32[32,8,128]{2,1,0:T(8,128)}, f32[128,768]{1,0:T(8,128)}, bf16[32,48,384]{2,1,0:T(8,128)(2,1)}, bf16[4,96,768]{2,1,0:T(8,128)(2,1)}, bf16[128,768]{...) custom-call(s32[1,128]{1,0:T(1,128)} %ids_ref.1, ...), custom_call_target="tpu_custom_call" | custom-call | tf_op jit(solution)/shard_map/start/pallas_call | solution.py:418
  102.7 100.1 %head.1 = (f32[128,768]{1,0:T(8,128)}, f32[1024,768]{1,0:T(8,128)}, f32[8,128]{1,0:T(8,128)}) custom-call(s32[32,8,128]{2,1,0:T(8,128)} %get-tuple-element.20.tok_ref, bf16[1004,768]{1,0:T(8,128)(2,1)} %emb_ref.3, bf16[128,768]{1,0:T(8,128)(2,1)} %get-tuple-element.21.hn_ref), custom_call_target="tpu_custom_call" | custom-call | tf_op jit(solution)/shard_map/head/pallas_call | solution.py:418
  202.8 1.2 slice.15
  204.0 98.5 %end.1 = (f32[1004,768]{1,0:T(8,128)}, f32[8,48,384]{2,1,0:T(8,128)}, f32[96,768]{1,0:T(8,128)}) custom-call(f32[128,768]{1,0:T(8,128)} %get-tuple-element.23.dhn_ref, f32[128,768]{1,0:T(8,128)} %get-tuple-element.24.x_ref, bf16[128,768]{1,0:T(8,128)(2,1)} %get-tuple-element.25.h_ref, bf16[8,128,768]{2,1,0:T(8,128)(2,1)} %get-tuple-element.26.a_ref, ...), custom_call_target="tpu_custom_call" | custom-call | tf_op jit(solution)/shard_map/end/pallas_call | solution.py:418
  302.4 1.5 reshape.32
  304.0 0.1 fusion
  304.0 0.2 copy.14
  304.3 0.9 slice.17
  305.2 0.2 copy.15
  305.4 0.9 slice.19
  306.4 0.0 copy-start
  306.4 3.8 %copy.20 = f32[1004,768]{1,0:T(8,128)} copy(f32[1004,768]{1,0:T(8,128)} %get-tuple-element.43) | data formatting | bytes 6168576
  310.1 0.0 copy-done
  310.1 0.7 copy.21
Async XLA Ops:
  306.4 3.8 %copy-start = (f32[96,768]{1,0:T(8,128)S(1)}, f32[96,768]{1,0:T(8,128)}, u32[]{:S(2)}) copy-start(f32[96,768]{1,0:T(8,128)} %get-tuple-element.46) | copy-start | bytes 884740

commit v4 on v3

--- a/solution.py
+++ b/solution.py
@@ -167,7 +167,7 @@
     ]
 
 
-def scatter_levels(in_ref, out_ref, scratch, place, work):
+def scatter_levels(in_ref, out_ref, scratch, place, work, hook=None):
     from_core, from_q, from_p, from_low, from_high, outgo, acc, sem_c, sem_q, sem_p, sem_up, sem_dn = scratch
     me, z, p, q, core = place
     rows = out_ref.shape[0]
@@ -245,6 +245,8 @@
         return far_level(z, lax.rem(t, HEIGHT))
 
     def step(t, carry):
+        if hook is not None:
+            hook(t)
         pl.when(t < HEIGHT)(lambda: make(level_at(t)))
         pl.when(jnp.logical_and(t > 0, t < 5))(lambda: send_q(level_at(t + TOP)))
         pl.when(jnp.logical_and(t > 1, t < 6))(lambda: send_p(level_at(t + TWO)))
@@ -421,124 +423,6 @@
         name=name)(*ins)
 
 
-def start_call(ids, labs, emb, pieces, down_shard, gain_mlp, gain_final, emb_scale):
-    def kernel(ids_ref, lab_ref, emb_ref, piece_ref, down_ref, gm_ref, gf_ref,
-               tok_ref, x_ref, gu_ref, wd_ref, hn_ref, h_ref, a_ref, g_ref, u_ref,
-               tok_mine, table, rows, sem_t, sem_a, z_send, z_recv, d_send, d_recv, *scratch):
-        ring, (mine, parts, total, *level) = scratch[:12], scratch[12:]
-        place = my_place()
-        me, z, p, q, core = place
-        rank = lax.rem(me, LEVEL)
-        tok_mine[...] = jnp.zeros((LEVEL, LANE), jnp.int32)
-        tok_mine[0:1, :] = ids_ref[...]
-        tok_mine[1:TWO, :] = lab_ref[...]
-        barrier_peers(place)
-
-        def exchange(step):
-            peer = lax.rem(rank + step, LEVEL)
-            return remote(piece_ref.at[peer], gu_ref.at[me], sem_a, step, z * LEVEL + peer)
-
-        def slab(lv, way):
-            part = gu_ref.at[pl.ds(lv * LEVEL, LEVEL)]
-            return pltpu.make_async_remote_copy(
-                src_ref=part, dst_ref=part, send_sem=z_send.at[way * HEIGHT + lv], recv_sem=z_recv.at[lv],
-                device_id=(me + LEVEL - CHIPS * way,), device_id_type=MESH)
-
-        def slab_down(lv, way, src):
-            return pltpu.make_async_remote_copy(
-                src_ref=src, dst_ref=wd_ref.at[lv], send_sem=d_send.at[way * HEIGHT + lv], recv_sem=d_recv.at[lv],
-                device_id=(me + LEVEL - CHIPS * way,), device_id_type=MESH)
-
-        pair = remote(tok_mine, tok_ref.at[me], sem_t, 0, me + 1 - TWO * core)
-        pair.start()
-        for step in range(1, LEVEL):
-            exchange(step).start()
-        pl.when(z < TOP)(lambda: slab_down(z, 0, down_ref).start())
-        pl.when(z > 0)(lambda: slab_down(z, 1, down_ref).start())
-        tok_ref[me] = tok_mine[...]
-        wd_ref[z] = down_ref[...]
-        gu_ref[me] = piece_ref[rank]
-        fill_table(table, emb_ref)
-        pair.wait()
-        for stage, (size, dev) in enumerate(((TWO, device_of(z, *flip_x(p, q, core))), (HEIGHT, device_of(z, *flip_y(p, q, core))))):
-            part = tok_ref.at[pl.ds(lax.div(me, size) * size, size)]
-            ship = remote(part, part, sem_t, stage + 1, dev)
-            ship.start()
-            ship.wait()
-        part = tok_ref.at[pl.ds(z * LEVEL, LEVEL)]
-        ships = [remote(part, part, sem_t, TWO + step, lax.rem(me + LEVEL * step, NDEV)) for step in range(1, HEIGHT)]
-        for ship in ships:
-            ship.start()
-        for ship in ships:
-            ship.wait()
-        for step in range(1, LEVEL):
-            exchange(step).wait_recv()
-        pl.when(z < TOP)(lambda: slab(z, 0).start())
-        pl.when(z > 0)(lambda: slab(z, 1).start())
-
-        def take(lv, way, more):
-            slab_down(lv, 0, wd_ref.at[lv]).wait_recv()
-            pl.when(more)(lambda: slab_down(lv, way, wd_ref.at[lv]).start())
-            slab(lv, 0).wait_recv()
-            pl.when(more)(lambda: slab(lv, way).start())
-
-        def take_far(far):
-            pl.when(z - far >= 0)(lambda: take(z - far, 0, z < TOP))
-            pl.when(z + far < HEIGHT)(lambda: take(z + far, 1, z > 0))
-
-        def find(lv):
-            def body(first):
-                hit = (vocab_iota() == id_rows(tok_ref, 0, first)).astype(F32).astype(BF16)
-                rows[pl.ds(first, HEIGHT)] = dot(hit, table[...], 0, 0).astype(BF16).reshape(HEIGHT, LANE, DIM)
-            halves(lv, body)
-
-        scatter_levels(rows, x_ref, ring, place, find)
-        take_far(1)
-        x = x_ref[...] * emb_scale
-        mine[...] = (x * rms_inv(x) * gm_ref[...]).astype(BF16)
-        level_gather(mine, a_ref, level[HEIGHT], level[5], place)
-        take_far(TWO)
-        take_far(TOP)
-        wg, wu = split_weights(gu_ref)
-        wd = wd_ref[...].reshape(UNITS, DIM)
-        for half in range(TWO):
-            four = slice(HEIGHT * half, HEIGHT * half + HEIGHT)
-            act_in = a_ref[four].reshape(TOKS, DIM)
-            g = dot(act_in, wg, 1, 0).astype(BF16)
-            u = dot(act_in, wu, 1, 0).astype(BF16)
-            g_ref[four] = g.reshape(HEIGHT, LANE, UNITS)
-            u_ref[four] = u.reshape(HEIGHT, LANE, UNITS)
-            act = (jax.nn.silu(g.astype(F32)) * u.astype(F32)).astype(BF16)
-            parts[four] = dot(act, wd, 1, 0).astype(BF16).reshape(HEIGHT, LANE, DIM)
-        level_scatter(parts, total, *level[:HEIGHT], *level[6:], place)
-        h = (x + total[...].astype(BF16).astype(F32)).astype(BF16)
-        h_ref[...] = h
-        h32 = h.astype(F32)
-        hn_ref[...] = (h32 * rms_inv(h32) * gf_ref[...]).astype(BF16)
-        for step in range(1, LEVEL):
-            exchange(step).wait_send()
-
-        def sent(lv, way):
-            slab(lv, way).wait_send()
-            slab_down(lv, way, wd_ref.at[lv]).wait_send()
-
-        for lv in range(HEIGHT):
-            pl.when(jnp.logical_and(z < TOP, lv <= z))(lambda: sent(lv, 0))
-            pl.when(jnp.logical_and(z > 0, lv >= z))(lambda: sent(lv, 1))
-
-    act = jax.ShapeDtypeStruct((LANE, DIM), BF16)
-    unit = jax.ShapeDtypeStruct((LEVEL, LANE, UNITS), BF16)
-    return call(
-        kernel, 'start', 0,
-        (jax.ShapeDtypeStruct((NDEV, LEVEL, LANE), jnp.int32), jax.ShapeDtypeStruct((LANE, DIM), F32),
-         jax.ShapeDtypeStruct(GU_SHAPE, BF16), jax.ShapeDtypeStruct(WD_SHAPE, BF16), act, act,
-         jax.ShapeDtypeStruct((LEVEL, LANE, DIM), BF16), unit, unit),
-        (ids, labs, emb, pieces, down_shard, gain_mlp, gain_final),
-        [pltpu.VMEM((LEVEL, LANE), jnp.int32), pltpu.VMEM((VPAD, DIM), BF16), pltpu.VMEM((NDEV, LANE, DIM), BF16),
-         sem_pair(6), sem_pair(LEVEL), pltpu.SemaphoreType.DMA((LEVEL,)), pltpu.SemaphoreType.DMA((HEIGHT,)),
-         pltpu.SemaphoreType.DMA((LEVEL,)), pltpu.SemaphoreType.DMA((HEIGHT,))] + scatter_scratch(LANE, DIM) + LEVEL_SCRATCH)
-
-
 def flip_x(p, q, core):
     return p * core + (1 - p) * (1 - core), q * (1 - core) + (1 - q) * core, core
 
@@ -563,19 +447,121 @@
     return jnp.concatenate([top + jnp.log(total), labs], axis=0)
 
 
-def head_call(toks, emb, hid_norm, inv_count):
-    def kernel(tok_ref, emb_ref, hn_ref, dhn_ref, demb_ref, loss_ref,
-               table, hid_all, parts, stat, land, land_z, lse_ref, g_send, g_recv, sem_s, *ring):
+def step_call(ids, labs, emb, pieces, down_shard, gain_mlp, gain_final, emb_scale, inv_count):
+    def kernel(ids_ref, lab_ref, emb_ref, piece_ref, down_ref, gm_ref, gf_ref,
+               demb_ref, own_ref, dn_ref, loss_ref,
+               tok_mine, tok_ref, table, spread, whole, gu_ref, wd_ref, a_ref, g_ref, u_ref, dm_ref,
+               d_gate, d_up, acts, grad_gate, grad_up, grad_down, ggu, gd, land_g, land_d, outgo, outgo_d, acc,
+               block, x_ref, h_ref, dh_ref, dhn_ref, stat, land, land_z, lse_ref,
+               sem_t, sem_a, z_send, z_recv, d_send, d_recv, g_send, g_recv, e_send, e_recv, sem_s, sem_b, sem_z, sem_d,
+               *scratch):
+        ring, (mine, parts, total, *level) = scratch[:12], scratch[12:]
         place = my_place()
         me, z, p, q, core = place
+        rank = lax.rem(me, LEVEL)
+        gain_m, gain_f = gm_ref[...].reshape(1, DIM), gf_ref[...].reshape(1, DIM)
+        tok_mine[...] = jnp.zeros((LEVEL, LANE), jnp.int32)
+        tok_mine[0:1, :] = ids_ref[...]
+        tok_mine[1:TWO, :] = lab_ref[...]
         barrier_peers(place)
+
+        def exchange(step):
+            peer = lax.rem(rank + step, LEVEL)
+            return remote(piece_ref.at[peer], gu_ref.at[me], sem_a, step, z * LEVEL + peer)
+
+        def rows_of(ref, lv):
+            return ref.at[pl.ds(lv * LEVEL, LEVEL)]
+
+        def slab(lv, way):
+            part = rows_of(gu_ref, lv)
+            return pltpu.make_async_remote_copy(
+                src_ref=part, dst_ref=part, send_sem=z_send.at[way * HEIGHT + lv], recv_sem=z_recv.at[lv],
+                device_id=(me + LEVEL - CHIPS * way,), device_id_type=MESH)
+
+        def slab_down(lv, way, src):
+            return pltpu.make_async_remote_copy(
+                src_ref=src, dst_ref=wd_ref.at[lv], send_sem=d_send.at[way * HEIGHT + lv], recv_sem=d_recv.at[lv],
+                device_id=(me + LEVEL - CHIPS * way,), device_id_type=MESH)
+
+        devs = (me + 1 - TWO * core, device_of(z, *flip_x(p, q, core)), device_of(z, *flip_y(p, q, core)))
+        pair = remote(tok_mine, tok_ref.at[me], sem_t, 0, devs[0])
+        pair.start()
+        for step in range(1, LEVEL):
+            exchange(step).start()
+        pl.when(z < TOP)(lambda: slab_down(z, 0, down_ref).start())
+        pl.when(z > 0)(lambda: slab_down(z, 1, down_ref).start())
+        tok_ref[me] = tok_mine[...]
+        wd_ref[z] = down_ref[...]
+        gu_ref[me] = piece_ref[rank]
         fill_table(table, emb_ref)
         stat[...] = jnp.zeros_like(stat)
         demb_ref[...] = jnp.zeros_like(demb_ref)
+        pair.wait()
+        for stage, size in ((1, TWO), (TWO, HEIGHT)):
+            part = tok_ref.at[pl.ds(lax.div(me, size) * size, size)]
+            ship = remote(part, part, sem_t, stage, devs[stage])
+            ship.start()
+            ship.wait()
+        part = rows_of(tok_ref, z)
+        ships = [remote(part, part, sem_t, TWO + step, lax.rem(me + LEVEL * step, NDEV)) for step in range(1, HEIGHT)]
+        for ship in ships:
+            ship.start()
+        for ship in ships:
+            ship.wait()
+        for step in range(1, LEVEL):
+            exchange(step).wait_recv()
+        pl.when(z < TOP)(lambda: slab(z, 0).start())
+        pl.when(z > 0)(lambda: slab(z, 1).start())
+
+        def take(lv, way, more):
+            slab_down(lv, 0, wd_ref.at[lv]).wait_recv()
+            pl.when(more)(lambda: slab_down(lv, way, wd_ref.at[lv]).start())
+            slab(lv, 0).wait_recv()
+            pl.when(more)(lambda: slab(lv, way).start())
+
+        def take_far(far):
+            pl.when(z - far >= 0)(lambda: take(z - far, 0, z < TOP))
+            pl.when(z + far < HEIGHT)(lambda: take(z + far, 1, z > 0))
+
+        def hit_rows(first):
+            return (vocab_iota() == id_rows(tok_ref, 0, first)).astype(F32).astype(BF16)
+
+        def find(lv):
+            def body(first):
+                spread[pl.ds(first, HEIGHT)] = dot(hit_rows(first), table[...], 0, 0).astype(BF16).reshape(HEIGHT, LANE, DIM)
+            halves(lv, body)
+
+        scatter_levels(spread, x_ref, ring, place, find, lambda t: pl.when(t == HEIGHT)(lambda: take_far(1)))
+        take_far(TWO)
+        x = x_ref[...] * emb_scale
+        mine[...] = (x * rms_inv(x) * gain_m).astype(BF16)
+        level_gather(mine, a_ref, level[HEIGHT], level[5], place)
+        take_far(TOP)
+        for half in range(TWO):
+            four = slice(HEIGHT * half, HEIGHT * half + HEIGHT)
+            wg, wu = split_weights(gu_ref)
+            act_in = a_ref[four].reshape(TOKS, DIM)
+            g = dot(act_in, wg, 1, 0).astype(BF16)
+            u = dot(act_in, wu, 1, 0).astype(BF16)
+            g_ref[half] = g
+            u_ref[half] = u
+            act = (jax.nn.silu(g.astype(F32)) * u.astype(F32)).astype(BF16)
+            acts[half] = act
+            parts[four] = dot(act, wd_ref[...].reshape(UNITS, DIM), 1, 0).astype(BF16).reshape(HEIGHT, LANE, DIM)
+        level_scatter(parts, total, *level[:HEIGHT], *level[6:], place)
+        h_ref[...] = (x_ref[...] * emb_scale + total[...].astype(BF16).astype(F32)).astype(BF16)
+        h32 = h_ref[...].astype(F32)
+        block[...] = (h32 * rms_inv(h32) * gain_f).astype(BF16)
+        for step in range(1, LEVEL):
+            exchange(step).wait_send()
+
+        def sent(lv, way):
+            slab(lv, way).wait_send()
+            slab_down(lv, way, wd_ref.at[lv]).wait_send()
 
         def forward(t, lv):
             def body(first):
-                logits = dot(table[...], hid_all[pl.ds(first, HEIGHT)].reshape(TOKS, DIM), 1, 1)
+                logits = dot(table[...], whole[pl.ds(first, HEIGHT)].reshape(TOKS, DIM), 1, 1)
                 row = vocab_iota()
                 lab = jnp.sum(jnp.where(row == id_rows(tok_ref, 1, first), logits, 0.0), axis=0, keepdims=True)
                 logits = jnp.where(row < VROWS, logits, -1e30)
@@ -586,9 +572,11 @@
                     stat[0, 32:33, :] = stat[0, 32:33, :] + lab[:, t * LANE:(t + 1) * LANE]
             halves(lv, body)
 
-        gather_levels(hn_ref, hid_all, g_send, g_recv, place, forward)
-
-        devs = (me + 1 - TWO * core, device_of(z, *flip_x(p, q, core)), device_of(z, *flip_y(p, q, core)))
+        gather_levels(block, whole, g_send, g_recv, place, forward)
+        for lv in range(HEIGHT):
+            pl.when(jnp.logical_and(z < TOP, lv <= z))(lambda: sent(lv, 0))
+            pl.when(jnp.logical_and(z > 0, lv >= z))(lambda: sent(lv, 1))
+
         for stage, dev in enumerate(devs):
             ship = remote(stat.at[stage], land.at[stage], sem_s, stage, dev)
             ship.start()
@@ -606,64 +594,38 @@
 
         def backward(lv):
             def body(first):
-                hid = hid_all[pl.ds(first, HEIGHT)].reshape(TOKS, DIM)
+                hid = whole[pl.ds(first, HEIGHT)].reshape(TOKS, DIM)
                 logits = dot(table[...], hid, 1, 1)
                 lse_row = jnp.concatenate([lse_ref[pl.ds(first + t, 1), :] for t in range(HEIGHT)], axis=1)
                 row = vocab_iota()
                 prob = jnp.exp(jnp.where(row < VROWS, logits, -1e30) - lse_row)
                 hit = jnp.where(row == id_rows(tok_ref, 1, first), 1.0, 0.0)
                 grad = ((prob - hit) * inv_count).astype(BF16)
-                parts[pl.ds(first, HEIGHT)] = dot(grad, table[...], 0, 0).astype(BF16).reshape(HEIGHT, LANE, DIM)
+                spread[pl.ds(first, HEIGHT)] = dot(grad, table[...], 0, 0).astype(BF16).reshape(HEIGHT, LANE, DIM)
                 demb_ref[...] += dot(grad, hid, 1, 0)
             halves(lv, body)
 
-        scatter_levels(parts, dhn_ref, ring, place, backward)
-
-    whole = pltpu.VMEM((NDEV, LANE, DIM), BF16)
-    return call(
-        kernel, 'head', 1,
-        (jax.ShapeDtypeStruct((LANE, DIM), F32), jax.ShapeDtypeStruct((VPAD, DIM), F32), jax.ShapeDtypeStruct((LEVEL, LANE), F32)),
-        (toks, emb, hid_norm),
-        [pltpu.VMEM((VPAD, DIM), BF16), whole, whole, pltpu.VMEM((HEIGHT, STAT, LANE), F32), pltpu.VMEM((TOP, STAT, LANE), F32),
-         pltpu.VMEM((HEIGHT, STAT, LANE), F32), pltpu.VMEM((32, LANE), F32), pltpu.SemaphoreType.DMA((5, NDEV)),
-         pltpu.SemaphoreType.DMA((NDEV,)), sem_pair(6)] + scatter_scratch(LANE, DIM))
-
-
-def end_call(dhn, x_raw, h, a_all, g_all, u_all, w_gu, w_dn, gain_mlp, gain_final, toks, d_head, emb_scale):
-    def kernel(dhn_ref, x_ref, h_ref, a_ref, g_ref, u_ref, wgu_ref, wd_ref, gm_ref, gf_ref, tok_ref, head_ref,
-               out_ref, own_ref, dn_ref,
-               dm_ref, grad_gate, grad_up, grad_down, ggu, gd, d_gate, d_up, acts, dx_ref, dx_all, acc_rows,
-               from_low, from_high, low_d, high_d, outgo, outgo_d, acc, g_send, g_recv, sem_a, sem_z, sem_d,
-               mine, parts, total, *scratch):
-        place = my_place()
-        me, z, p, q, core = place
-        rank = lax.rem(me, LEVEL)
-        barrier_peers(place)
+        scatter_levels(spread, dhn_ref, ring, place, backward)
+
         h32 = h_ref[...].astype(F32)
-        dh = rms_backward(h32, rms_inv(h32), gf_ref[...], dhn_ref[...])
-        mine[...] = dh.astype(BF16)
-        level_gather(mine, dm_ref, scratch[HEIGHT], scratch[5], place)
-        wg, wu = split_weights(wgu_ref)
-        wd = wd_ref[...].reshape(UNITS, DIM)
+        dh_ref[...] = rms_backward(h32, rms_inv(h32), gain_f, dhn_ref[...])
+        mine[...] = dh_ref[...].astype(BF16)
+        level_gather(mine, dm_ref, level[HEIGHT], level[5], place)
         for half in range(TWO):
             four = slice(HEIGHT * half, HEIGHT * half + HEIGHT)
-            g = g_ref[four].reshape(TOKS, UNITS).astype(F32)
-            u = u_ref[four].reshape(TOKS, UNITS).astype(F32)
-            dq = dot(dm_ref[four].reshape(TOKS, DIM), wd, 1, 1)
+            wg, wu = split_weights(gu_ref)
+            g = g_ref[half].astype(F32)
+            u = u_ref[half].astype(F32)
+            dq = dot(dm_ref[four].reshape(TOKS, DIM), wd_ref[...].reshape(UNITS, DIM), 1, 1)
             sig = jax.nn.sigmoid(g)
             dg = (dq * u * sig * (1.0 + g * (1.0 - sig))).astype(BF16)
             du = (dq * g * sig).astype(BF16)
             d_gate[half] = dg
             d_up[half] = du
-            acts[half] = (jax.nn.silu(g) * u).astype(BF16)
             parts[four] = (dot(dg, wg, 1, 1) + dot(du, wu, 1, 1)).astype(BF16).reshape(HEIGHT, LANE, DIM)
-        level_scatter(parts, total, *scratch[:HEIGHT], *scratch[6:], place)
+        level_scatter(parts, total, *level[:HEIGHT], *level[6:], place)
         x = x_ref[...] * emb_scale
-        dx_ref[...] = (dh + rms_backward(x, rms_inv(x), gm_ref[...], total[...])).astype(BF16)
-        acc_rows[...] = jnp.zeros_like(acc_rows)
-
-        def rows_of(ref, lv):
-            return ref.at[pl.ds(lv * LEVEL, LEVEL)]
+        block[...] = (dh_ref[...] + rms_backward(x, rms_inv(x), gain_m, total[...])).astype(BF16)
 
         def add_slab(dst, srcs):
             def body(i, carry):
@@ -674,35 +636,31 @@
                 return carry
             lax.fori_loop(0, LEVEL, body, 0)
 
-        def hop(lv, way):
-            land = (from_low, from_high)[way]
-            return remote(rows_of(outgo, lv), rows_of(land, lv), sem_z, way * HEIGHT + lv, me + LEVEL - CHIPS * way)
-
-        def hop_d(lv, way):
-            land = (low_d, high_d)[way]
-            return remote(outgo_d.at[lv], land.at[lv], sem_d, way * HEIGHT + lv, me + LEVEL - CHIPS * way)
-
-        def send(lv, way, more):
-            low = rows_of((from_low, from_high)[way], lv)
-            low_down = (low_d, high_d)[way].at[lv]
-
+        def hop(lv, way, here=False):
+            land = rows_of(land_g, HEIGHT if here and way else lv)
+            return remote(rows_of(outgo, lv), land, sem_z, way * HEIGHT + lv, me + LEVEL - CHIPS * way)
+
+        def hop_d(lv, way, here=False):
+            return remote(outgo_d.at[lv], land_d.at[HEIGHT if here and way else lv], sem_d, way * HEIGHT + lv, me + LEVEL - CHIPS * way)
+
+        def send(lv, way, more, here):
             @pl.when(more)
             def _():
                 hop(lv, way).wait_recv()
-                add_slab(rows_of(outgo, lv), [rows_of(ggu, lv), low])
+                add_slab(rows_of(outgo, lv), [rows_of(ggu, lv), rows_of(land_g, lv)])
                 hop_d(lv, way).wait_recv()
-                add_into(outgo_d.at[lv], [gd.at[lv], low_down], DROWS)
+                add_into(outgo_d.at[lv], [gd.at[lv], land_d.at[lv]], DROWS)
 
             @pl.when(jnp.logical_not(more))
             def _():
                 add_slab(rows_of(outgo, lv), [rows_of(ggu, lv)])
                 add_into(outgo_d.at[lv], [gd.at[lv]], DROWS)
-            hop(lv, way).start()
-            hop_d(lv, way).start()
+            hop(lv, way, here).start()
+            hop_d(lv, way, here).start()
 
         def send_far(far):
-            pl.when(z + far < HEIGHT)(lambda: send(z + far, 0, z > 0))
-            pl.when(z - far >= 0)(lambda: send(z - far, 1, z < TOP))
+            pl.when(z + far < HEIGHT)(lambda: send(z + far, 0, z > 0, far == 1))
+            pl.when(z - far >= 0)(lambda: send(z - far, 1, z < TOP, far == 1))
 
         def weight_grads():
             for half in range(TWO):
@@ -718,8 +676,7 @@
 
         def add_rows(t, lv):
             def body(first):
-                hit = (vocab_iota() == id_rows(tok_ref, 0, first)).astype(F32).astype(BF16)
-                acc_rows[...] += dot(hit, dx_all[pl.ds(first, HEIGHT)].reshape(TOKS, DIM), 1, 0)
+                demb_ref[...] += dot(hit_rows(first), whole[pl.ds(first, HEIGHT)].reshape(TOKS, DIM), 1, 0) * emb_scale
             halves(lv, body)
 
             @pl.when(t == 1)
@@ -729,52 +686,59 @@
             pl.when(t == TWO)(lambda: send_far(TWO))
             pl.when(t == TOP)(lambda: send_far(1))
 
-        gather_levels(dx_ref, dx_all, g_send, g_recv, place, add_rows)
-        out_ref[...] = head_ref[0:VROWS, :] + acc_rows[0:VROWS, :] * emb_scale
-
+        gather_levels(block, whole, e_send, e_recv, place, add_rows)
         add_slab(acc, [rows_of(ggu, z)])
         add_into(dn_ref, [gd.at[z]], DROWS)
 
         def last(way):
             hop(z, way).wait_recv()
-            add_slab(acc, [acc, rows_of((from_low, from_high)[way], z)])
+            add_slab(acc, [acc, rows_of(land_g, HEIGHT if way else z)])
             hop_d(z, way).wait_recv()
-            add_into(dn_ref, [dn_ref, (low_d, high_d)[way].at[z]], DROWS)
+            add_into(dn_ref, [dn_ref, land_d.at[HEIGHT if way else z]], DROWS)
 
         pl.when(z > 0)(lambda: last(0))
         pl.when(z < TOP)(lambda: last(1))
 
-        def exchange(step):
+        def give(step):
             peer = lax.rem(rank + step, LEVEL)
-            return remote(acc.at[peer], own_ref.at[rank], sem_a, step, z * LEVEL + peer)
+            return remote(acc.at[peer], own_ref.at[rank], sem_b, step, z * LEVEL + peer)
 
         for step in range(1, LEVEL):
-            exchange(step).start()
+            give(step).start()
         own_ref[rank] = acc[rank]
         for step in range(1, LEVEL):
-            exchange(step).wait_recv()
+            give(step).wait_recv()
         for step in range(1, LEVEL):
-            exchange(step).wait_send()
-
-        def sent(lv, way):
+            give(step).wait_send()
+
+        def gone(lv, way):
             hop(lv, way).wait_send()
             hop_d(lv, way).wait_send()
 
         for lv in range(HEIGHT):
-            pl.when(lv > z)(lambda: sent(lv, 0))
-            pl.when(lv < z)(lambda: sent(lv, 1))
-
+            pl.when(lv > z)(lambda: gone(lv, 0))
+            pl.when(lv < z)(lambda: gone(lv, 1))
+
+    whole = pltpu.VMEM((NDEV, LANE, DIM), BF16)
+    block, flat = pltpu.VMEM((LANE, DIM), BF16), pltpu.VMEM((LANE, DIM), F32)
     slab, slab_d = pltpu.VMEM(GU_SHAPE, BF16), pltpu.VMEM(WD_SHAPE, BF16)
+    unit, eight = pltpu.VMEM((TWO, TOKS, UNITS), BF16), pltpu.VMEM((LEVEL, LANE, DIM), BF16)
     wide, tall = pltpu.VMEM((DIM, UNITS), F32), pltpu.VMEM((UNITS, DIM), F32)
-    unit = pltpu.VMEM((TWO, TOKS, UNITS), BF16)
+    dma = pltpu.SemaphoreType.DMA
     return call(
-        kernel, 'end', TWO,
-        (jax.ShapeDtypeStruct((VROWS, DIM), F32), jax.ShapeDtypeStruct((LEVEL, PAIR, UNITS), F32), jax.ShapeDtypeStruct((DROWS, DIM), F32)),
-        (dhn, x_raw, h, a_all, g_all, u_all, w_gu, w_dn, gain_mlp, gain_final, toks, d_head),
-        [pltpu.VMEM((LEVEL, LANE, DIM), BF16), wide, wide, tall, slab, slab_d, unit, unit, unit, pltpu.VMEM((LANE, DIM), BF16),
-         pltpu.VMEM((NDEV, LANE, DIM), BF16), pltpu.VMEM((VPAD, DIM), F32), slab, slab, slab_d, slab_d, slab, slab_d,
-         pltpu.VMEM((LEVEL, PAIR, UNITS), F32), pltpu.SemaphoreType.DMA((5, NDEV)), pltpu.SemaphoreType.DMA((NDEV,)),
-         sem_pair(LEVEL), sem_pair(LEVEL), sem_pair(LEVEL)] + LEVEL_SCRATCH)
+        kernel, 'step', 0,
+        (jax.ShapeDtypeStruct((VPAD, DIM), F32), jax.ShapeDtypeStruct((LEVEL, PAIR, UNITS), F32),
+         jax.ShapeDtypeStruct((DROWS, DIM), F32), jax.ShapeDtypeStruct((LEVEL, LANE), F32)),
+        (ids, labs, emb, pieces, down_shard, gain_mlp, gain_final),
+        [pltpu.VMEM((LEVEL, LANE), jnp.int32), pltpu.VMEM((NDEV, LEVEL, LANE), jnp.int32), pltpu.VMEM((VPAD, DIM), BF16), whole, whole,
+         slab, slab_d, eight, unit, unit, eight, unit, unit, unit, wide, wide, tall, slab, slab_d,
+         pltpu.VMEM((5 * LEVEL, PAIR, UNITS), BF16), pltpu.VMEM((5, DROWS, DIM), BF16), slab, slab_d,
+         pltpu.VMEM((LEVEL, PAIR, UNITS), F32), block, flat, block, flat, flat,
+         pltpu.VMEM((HEIGHT, STAT, LANE), F32), pltpu.VMEM((TOP, STAT, LANE), F32), pltpu.VMEM((HEIGHT, STAT, LANE), F32),
+         pltpu.VMEM((32, LANE), F32),
+         sem_pair(6), sem_pair(LEVEL), dma((LEVEL,)), dma((HEIGHT,)), dma((LEVEL,)), dma((HEIGHT,)), dma((5, NDEV)), dma((NDEV,)),
+         dma((5, NDEV)), dma((NDEV,)), sem_pair(6), sem_pair(LEVEL), sem_pair(LEVEL), sem_pair(LEVEL)]
+        + scatter_scratch(LANE, DIM) + LEVEL_SCRATCH)
 
 
 def solution(mesh):
@@ -783,15 +747,12 @@
     def local_step(ids_blk, lab_blk, emb_shard, gate_shard, up_shard, down_shard, gain_mlp, gain_final):
         emb_scale = math.sqrt(emb_shard.shape[1])
         inv_count = 1.0 / (ids_blk.size * group)
-        gm, gf = gain_mlp.reshape(1, -1), gain_final.reshape(1, -1)
         pieces = jnp.concatenate([gate_shard, up_shard], axis=0).reshape(PAIR, HEIGHT, LEVEL, DROWS)
         pieces = pieces.transpose(TWO, 0, 1, TOP).reshape(LEVEL, PAIR, UNITS)
-        toks, x_raw, w_gu, w_dn, hid_norm, h, a_all, g_all, u_all = start_call(
-            ids_blk, lab_blk, emb_shard, pieces, down_shard, gm, gf, emb_scale)
-        dhn, d_head, loss = head_call(toks, emb_shard, hid_norm, inv_count)
-        d_embed, d_gu, d_down = end_call(dhn, x_raw, h, a_all, g_all, u_all, w_gu, w_dn, gm, gf, toks, d_head, emb_scale)
+        d_embed, d_gu, d_down, loss = step_call(
+            ids_blk, lab_blk, emb_shard, pieces, down_shard, gain_mlp, gain_final, emb_scale, inv_count)
         d_gu = d_gu.reshape(LEVEL, PAIR, HEIGHT, DROWS).transpose(1, TWO, 0, TOP).reshape(PAIR, 3072)
-        return loss[0, 0], d_embed, d_gu[0:GROWS], d_gu[GROWS:PAIR], d_down
+        return loss[0, 0], d_embed[0:VROWS], d_gu[0:GROWS], d_gu[GROWS:PAIR], d_down
 
     shard_spec = P('fsdp', None)
     return jax.shard_map(local_step, mesh=mesh, in_specs=(shard_spec, shard_spec, shard_spec, shard_spec, shard_spec, shard_spec, P(), P()), out_specs=(P(), shard_spec, shard_spec, shard_spec, shard_spec), check_vma=False)

time: 311 us -> 286 us (0.920)
  Pallas kernels: 296 us -> 272 us
    pallas_call x3 -> x1, Pallas kernels: 296 us -> 272 us  [call(): pl.pallas_call(kernel, out_shape=outs, in_specs=[VSPEC] * len(ins), out_s...]
    unnamed x4 -> x3, local copies, waits for them, and re-layouts: 4.48 us -> 0.72 us
    slice x6 -> x7, local copies, waits for them, and re-layouts: 3.57 us -> 7.33 us  [the longest x1 3.77 us: local_step(): d_embed[0:VROWS]]
where the time goes in v4:
time: 286 us; the launch traced here: 285 us
  Pallas kernels  272 us (95%)
  local copies, waits for them, and re-layouts  11.1 us (4%)
    pallas_call x1, Pallas kernels, call(): pl.pallas_call(kernel, out_shape=outs, in_specs=[VSPEC] * len(ins), out_s...  272 us

profile of v4, /device:TPU:0, one launch (start us, length us, event | category | flops | bytes accessed | tf_op | source)
XLA Modules:
  0.0 284.9 jit_solution(7612490052411198883)
XLA Ops:
  0.6 1.0 pad_maximum_fusion
  1.6 0.4 reshape.22
  2.0 0.2 copy.17
  2.2 1.0 reshape.23.piece_ref
  3.2 272.1 %step.1 = (f32[1024,768]{1,0:T(8,128)}, f32[8,48,384]{2,1,0:T(8,128)}, f32[96,768]{1,0:T(8,128)}, f32[8,128]{1,0:T(8,128)}) custom-call(s32[1,128]{1,0:T(1,128)} %ids_ref.1, s32[1,128]{1,0:T(1,128)} %lab_ref.1, bf16[1004,768]{1,0:T(8,128)(2,1)} %emb_ref.1, bf16[8,48,384]{2,1,0:T(8,128)(2,1)} %reshape.23.piece_ref, bf16[96,768]{1,0:T(8,128)(2,1)} %down_ref.1, ...), custom_call_target="tpu_custom_call" | custom-call | tf_op jit(solution)/shard_map/step/pallas_call | solution.py:420
  275.3 1.2 slice.18
  276.5 1.5 reshape.24
  278.0 0.1 fusion
  278.1 0.2 copy.15
  278.3 0.9 slice.23
  279.3 0.2 copy.14
  279.5 0.9 slice.21
  280.4 0.0 copy-start
  280.4 3.8 %slice.19 = f32[1004,768]{1,0:T(8,128)} slice(f32[1024,768]{1,0:T(8,128)} %get-tuple-element.10), slice={[0:1004], [0:768]} | slice | bytes 6168576 | tf_op jit(solution)/shard_map/slice | solution.py:755
  284.2 0.0 copy-done
  284.2 0.7 copy.19
Async XLA Ops:
  280.4 3.8 %copy-start = (f32[96,768]{1,0:T(8,128)S(1)}, f32[96,768]{1,0:T(8,128)}, u32[]{:S(2)}) copy-start(f32[96,768]{1,0:T(8,128)} %get-tuple-element.24) | copy-start | bytes 884740

commit v5 on v4

--- a/solution.py
+++ b/solution.py
@@ -80,7 +80,7 @@
     return pltpu.SemaphoreType.DMA((TWO, n))
 
 
-def gather_levels(in_ref, out_ref, send_sem, recv_sem, place, work):
+def gather_levels(in_ref, out_ref, send_sem, recv_sem, place, work, hook=None):
     me, z, p, q, core = place
     peers = (me + LEVEL, me - LEVEL, device_of(z, 1 - p, q, core), device_of(z, p, 1 - q, core), me + 1 - TWO * core)
 
@@ -122,6 +122,8 @@
             got(level * LEVEL + chip * TWO + 1 - core)
 
     def step(t, carry):
+        if hook is not None:
+            hook(t)
         pl.when(t < TOP)(lambda: take_z(far_level(z, TWO - lax.rem(t, TOP))))
         pl.when(t < HEIGHT)(lambda: take_p(far_level(z, TOP - lax.rem(t, HEIGHT))))
 
@@ -129,7 +131,7 @@
         def _():
             level = far_level(z, HEIGHT - (t + lax.div(HEIGHT - t, HEIGHT)))
             take_q(level)
-            work(t, level)
+            work(level)
         return carry
 
     lax.fori_loop(0, 5, step, 0)
@@ -197,16 +199,18 @@
         core_copy(chip).wait_recv()
         return [in_ref.at[chip * TWO + core], from_core.at[chip]]
 
-    def make(level):
-        work(level)
-        for last in (1 - p, p):
-            for mid in (1 - q, q):
-                core_copy(chip_of(level, mid, last, other)).start()
-
-    def send_q(level):
-        for mid in (1 - p, p):
-            add_into(outgo.at[local(level, mid, 1 - q)], own(level, mid, 1 - q), rows)
-            q_copy(level, mid).start()
+    y = q * (1 - core) + p * core
+    x = p * (1 - core) + q * core
+
+    def make(level, half):
+        row = level * HEIGHT + TWO * (y * half + (1 - y) * (1 - half))
+        work(row * TWO)
+        for side in (1 - x, x):
+            core_copy(row + side).start()
+
+    def send_q(level, mid):
+        add_into(outgo.at[local(level, mid, 1 - q)], own(level, mid, 1 - q), rows)
+        q_copy(level, mid).start()
 
     def send_p(level):
         side = own(level, 1 - p, q)
@@ -242,18 +246,19 @@
             dn_copy(level).start()
 
     def level_at(t):
-        return far_level(z, lax.rem(t, HEIGHT))
+        return far_level(z, lax.rem(lax.div(t, TWO), HEIGHT))
 
     def step(t, carry):
+        odd = lax.rem(t, TWO)
         if hook is not None:
             hook(t)
-        pl.when(t < HEIGHT)(lambda: make(level_at(t)))
-        pl.when(jnp.logical_and(t > 0, t < 5))(lambda: send_q(level_at(t + TOP)))
-        pl.when(jnp.logical_and(t > 1, t < 6))(lambda: send_p(level_at(t + TWO)))
-        pl.when(t > TWO)(lambda: send_z(level_at(t + 1)))
+        pl.when(t < LEVEL)(lambda: make(level_at(t), odd))
+        pl.when(jnp.logical_and(t > 0, t < 9))(lambda: send_q(level_at(t + 7), odd * (1 - p) + (1 - odd) * p))
+        pl.when(jnp.logical_and(t > TWO, odd == 1))(lambda: send_p(level_at(t + 5)))
+        pl.when(jnp.logical_and(t > HEIGHT, odd == 1))(lambda: send_z(level_at(t + TOP)))
         return carry
 
-    lax.fori_loop(0, 6, step, 0)
+    lax.fori_loop(0, 10, step, 0)
     add_into(out_ref, gather_here(z), rows)
 
     @pl.when(z > 0)
@@ -311,7 +316,7 @@
         desc(chip * TWO + core, TWO).wait_send()
 
 
-def level_scatter(in_ref, out_ref, from_core, from_q, from_p, outgo, sem_s, sem_r, place):
+def level_scatter(in_ref, out_ref, from_core, from_q, from_p, outgo, sem_s, sem_r, place, hook=None):
     me, z, p, q, core = place
     rows = out_ref.shape[0]
 
@@ -340,6 +345,8 @@
     for mid in (1 - p, p):
         add_into(outgo.at[mid], own(mid, 1 - q), rows)
         q_copy(mid).start()
+    if hook is not None:
+        hook()
     side = own(1 - p, q)
     q_copy(1 - p).wait_recv()
     add_into(outgo.at[TWO], side + [from_q.at[1 - p]], rows)
@@ -421,14 +428,6 @@
         kernel, out_shape=outs, in_specs=[VSPEC] * len(ins), out_specs=(VSPEC,) * len(outs), scratch_shapes=scratch,
         compiler_params=pltpu.CompilerParams(collective_id=cid, has_side_effects=True, vmem_limit_bytes=VMEM_CAP),
         name=name)(*ins)
-
-
-def flip_x(p, q, core):
-    return p * core + (1 - p) * (1 - core), q * (1 - core) + (1 - q) * core, core
-
-
-def flip_y(p, q, core):
-    return p * (1 - core) + (1 - p) * core, q * core + (1 - q) * (1 - core), core
 
 
 STAT = 40
@@ -483,31 +482,31 @@
                 src_ref=src, dst_ref=wd_ref.at[lv], send_sem=d_send.at[way * HEIGHT + lv], recv_sem=d_recv.at[lv],
                 device_id=(me + LEVEL - CHIPS * way,), device_id_type=MESH)
 
-        devs = (me + 1 - TWO * core, device_of(z, *flip_x(p, q, core)), device_of(z, *flip_y(p, q, core)))
-        pair = remote(tok_mine, tok_ref.at[me], sem_t, 0, devs[0])
-        pair.start()
-        for step in range(1, LEVEL):
-            exchange(step).start()
-        pl.when(z < TOP)(lambda: slab_down(z, 0, down_ref).start())
-        pl.when(z > 0)(lambda: slab_down(z, 1, down_ref).start())
+        def tell(step):
+            return remote(tok_mine, tok_ref.at[me], sem_t, step, z * LEVEL + lax.rem(rank + step, LEVEL))
+
+        def along_z(src, dst, sems, step):
+            return remote(src, dst, sems, 7 + step, lax.rem(me + LEVEL * step, NDEV))
+
+        for step in range(1, LEVEL):
+            tell(step).start()
         tok_ref[me] = tok_mine[...]
         wd_ref[z] = down_ref[...]
         gu_ref[me] = piece_ref[rank]
         fill_table(table, emb_ref)
         stat[...] = jnp.zeros_like(stat)
         demb_ref[...] = jnp.zeros_like(demb_ref)
-        pair.wait()
-        for stage, size in ((1, TWO), (TWO, HEIGHT)):
-            part = tok_ref.at[pl.ds(lax.div(me, size) * size, size)]
-            ship = remote(part, part, sem_t, stage, devs[stage])
-            ship.start()
-            ship.wait()
+        for step in range(1, LEVEL):
+            tell(step).wait()
         part = rows_of(tok_ref, z)
-        ships = [remote(part, part, sem_t, TWO + step, lax.rem(me + LEVEL * step, NDEV)) for step in range(1, HEIGHT)]
-        for ship in ships:
-            ship.start()
-        for ship in ships:
-            ship.wait()
+        for step in range(1, HEIGHT):
+            along_z(part, part, sem_t, step).start()
+        for step in range(1, LEVEL):
+            exchange(step).start()
+        pl.when(z < TOP)(lambda: slab_down(z, 0, down_ref).start())
+        pl.when(z > 0)(lambda: slab_down(z, 1, down_ref).start())
+        for step in range(1, HEIGHT):
+            along_z(part, part, sem_t, step).wait()
         for step in range(1, LEVEL):
             exchange(step).wait_recv()
         pl.when(z < TOP)(lambda: slab(z, 0).start())
@@ -526,12 +525,10 @@
         def hit_rows(first):
             return (vocab_iota() == id_rows(tok_ref, 0, first)).astype(F32).astype(BF16)
 
-        def find(lv):
-            def body(first):
-                spread[pl.ds(first, HEIGHT)] = dot(hit_rows(first), table[...], 0, 0).astype(BF16).reshape(HEIGHT, LANE, DIM)
-            halves(lv, body)
-
-        scatter_levels(spread, x_ref, ring, place, find, lambda t: pl.when(t == HEIGHT)(lambda: take_far(1)))
+        def find(first):
+            spread[pl.ds(first, HEIGHT)] = dot(hit_rows(first), table[...], 0, 0).astype(BF16).reshape(HEIGHT, LANE, DIM)
+
+        scatter_levels(spread, x_ref, ring, place, find, lambda t: pl.when(t == LEVEL)(lambda: take_far(1)))
         take_far(TWO)
         x = x_ref[...] * emb_scale
         mine[...] = (x * rms_inv(x) * gain_m).astype(BF16)
@@ -559,7 +556,7 @@
             slab(lv, way).wait_send()
             slab_down(lv, way, wd_ref.at[lv]).wait_send()
 
-        def forward(t, lv):
+        def forward(lv):
             def body(first):
                 logits = dot(table[...], whole[pl.ds(first, HEIGHT)].reshape(TOKS, DIM), 1, 1)
                 row = vocab_iota()
@@ -577,33 +574,34 @@
             pl.when(jnp.logical_and(z < TOP, lv <= z))(lambda: sent(lv, 0))
             pl.when(jnp.logical_and(z > 0, lv >= z))(lambda: sent(lv, 1))
 
-        for stage, dev in enumerate(devs):
-            ship = remote(stat.at[stage], land.at[stage], sem_s, stage, dev)
-            ship.start()
-            ship.wait()
-            stat[stage + 1] = merge_stats([stat[stage], land[stage]])
-        ships = [remote(stat.at[TOP], land_z.at[z], sem_s, TWO + step, lax.rem(me + LEVEL * step, NDEV)) for step in range(1, HEIGHT)]
-        for ship in ships:
-            ship.start()
-        land_z[z] = stat[TOP]
-        for ship in ships:
-            ship.wait()
+        def share(step):
+            return remote(stat.at[0], land.at[rank], sem_s, step, z * LEVEL + lax.rem(rank + step, LEVEL))
+
+        for step in range(1, LEVEL):
+            share(step).start()
+        land[rank] = stat[0]
+        for step in range(1, LEVEL):
+            share(step).wait()
+        stat[1] = merge_stats([land[r] for r in range(LEVEL)])
+        for step in range(1, HEIGHT):
+            along_z(stat.at[1], land_z.at[z], sem_s, step).start()
+        land_z[z] = stat[1]
+        for step in range(1, HEIGHT):
+            along_z(stat.at[1], land_z.at[z], sem_s, step).wait()
         final = merge_stats([land_z[lv] for lv in range(HEIGHT)])
         lse_ref[...] = final[0:32, :]
         loss_ref[...] = jnp.full((LEVEL, LANE), (jnp.sum(final[0:32, :]) - jnp.sum(final[32:STAT, :])) * inv_count, F32)
 
-        def backward(lv):
-            def body(first):
-                hid = whole[pl.ds(first, HEIGHT)].reshape(TOKS, DIM)
-                logits = dot(table[...], hid, 1, 1)
-                lse_row = jnp.concatenate([lse_ref[pl.ds(first + t, 1), :] for t in range(HEIGHT)], axis=1)
-                row = vocab_iota()
-                prob = jnp.exp(jnp.where(row < VROWS, logits, -1e30) - lse_row)
-                hit = jnp.where(row == id_rows(tok_ref, 1, first), 1.0, 0.0)
-                grad = ((prob - hit) * inv_count).astype(BF16)
-                spread[pl.ds(first, HEIGHT)] = dot(grad, table[...], 0, 0).astype(BF16).reshape(HEIGHT, LANE, DIM)
-                demb_ref[...] += dot(grad, hid, 1, 0)
-            halves(lv, body)
+        def backward(first):
+            hid = whole[pl.ds(first, HEIGHT)].reshape(TOKS, DIM)
+            logits = dot(table[...], hid, 1, 1)
+            lse_row = jnp.concatenate([lse_ref[pl.ds(first + t, 1), :] for t in range(HEIGHT)], axis=1)
+            row = vocab_iota()
+            prob = jnp.exp(jnp.where(row < VROWS, logits, -1e30) - lse_row)
+            hit = jnp.where(row == id_rows(tok_ref, 1, first), 1.0, 0.0)
+            grad = ((prob - hit) * inv_count).astype(BF16)
+            spread[pl.ds(first, HEIGHT)] = dot(grad, table[...], 0, 0).astype(BF16).reshape(HEIGHT, LANE, DIM)
+            demb_ref[...] += dot(grad, hid, 1, 0)
 
         scatter_levels(spread, dhn_ref, ring, place, backward)
 
@@ -623,10 +621,6 @@
             d_gate[half] = dg
             d_up[half] = du
             parts[four] = (dot(dg, wg, 1, 1) + dot(du, wu, 1, 1)).astype(BF16).reshape(HEIGHT, LANE, DIM)
-        level_scatter(parts, total, *level[:HEIGHT], *level[6:], place)
-        x = x_ref[...] * emb_scale
-        block[...] = (dh_ref[...] + rms_backward(x, rms_inv(x), gain_m, total[...])).astype(BF16)
-
         def add_slab(dst, srcs):
             def body(i, carry):
                 value = srcs[0][i].astype(F32)
@@ -674,21 +668,20 @@
             ggu[...] = both.astype(BF16)
             gd[...] = grad_down[...].astype(BF16).reshape(WD_SHAPE)
 
-        def add_rows(t, lv):
+        def grads_off():
+            weight_grads()
+            send_far(TOP)
+
+        level_scatter(parts, total, *level[:HEIGHT], *level[6:], place, grads_off)
+        x = x_ref[...] * emb_scale
+        block[...] = (dh_ref[...] + rms_backward(x, rms_inv(x), gain_m, total[...])).astype(BF16)
+
+        demb_ref[...] = demb_ref[...] * (1.0 / emb_scale)
+
+        def add_rows(lv):
             def body(first):
-                demb_ref[...] += dot(hit_rows(first), whole[pl.ds(first, HEIGHT)].reshape(TOKS, DIM), 1, 0) * emb_scale
+                demb_ref[...] += dot(hit_rows(first), whole[pl.ds(first, HEIGHT)].reshape(TOKS, DIM), 1, 0)
             halves(lv, body)
-
-            @pl.when(t == 1)
-            def _():
-                weight_grads()
-                send_far(TOP)
-            pl.when(t == TWO)(lambda: send_far(TWO))
-            pl.when(t == TOP)(lambda: send_far(1))
-
-        gather_levels(block, whole, e_send, e_recv, place, add_rows)
-        add_slab(acc, [rows_of(ggu, z)])
-        add_into(dn_ref, [gd.at[z]], DROWS)
 
         def last(way):
             hop(z, way).wait_recv()
@@ -696,16 +689,25 @@
             hop_d(z, way).wait_recv()
             add_into(dn_ref, [dn_ref, land_d.at[HEIGHT if way else z]], DROWS)
 
-        pl.when(z > 0)(lambda: last(0))
-        pl.when(z < TOP)(lambda: last(1))
-
         def give(step):
             peer = lax.rem(rank + step, LEVEL)
             return remote(acc.at[peer], own_ref.at[rank], sem_b, step, z * LEVEL + peer)
 
-        for step in range(1, LEVEL):
-            give(step).start()
-        own_ref[rank] = acc[rank]
+        def grads_home():
+            add_slab(acc, [rows_of(ggu, z)])
+            add_into(dn_ref, [gd.at[z]], DROWS)
+            pl.when(z > 0)(lambda: last(0))
+            pl.when(z < TOP)(lambda: last(1))
+            for step in range(1, LEVEL):
+                give(step).start()
+            own_ref[rank] = acc[rank]
+
+        def grads_step(t):
+            pl.when(t == 1)(lambda: send_far(TWO))
+            pl.when(t == TWO)(lambda: send_far(1))
+            pl.when(t == HEIGHT)(grads_home)
+
+        gather_levels(block, whole, e_send, e_recv, place, add_rows, grads_step)
         for step in range(1, LEVEL):
             give(step).wait_recv()
         for step in range(1, LEVEL):
@@ -734,10 +736,10 @@
          slab, slab_d, eight, unit, unit, eight, unit, unit, unit, wide, wide, tall, slab, slab_d,
          pltpu.VMEM((5 * LEVEL, PAIR, UNITS), BF16), pltpu.VMEM((5, DROWS, DIM), BF16), slab, slab_d,
          pltpu.VMEM((LEVEL, PAIR, UNITS), F32), block, flat, block, flat, flat,
-         pltpu.VMEM((HEIGHT, STAT, LANE), F32), pltpu.VMEM((TOP, STAT, LANE), F32), pltpu.VMEM((HEIGHT, STAT, LANE), F32),
+         pltpu.VMEM((TWO, STAT, LANE), F32), pltpu.VMEM((LEVEL, STAT, LANE), F32), pltpu.VMEM((HEIGHT, STAT, LANE), F32),
          pltpu.VMEM((32, LANE), F32),
-         sem_pair(6), sem_pair(LEVEL), dma((LEVEL,)), dma((HEIGHT,)), dma((LEVEL,)), dma((HEIGHT,)), dma((5, NDEV)), dma((NDEV,)),
-         dma((5, NDEV)), dma((NDEV,)), sem_pair(6), sem_pair(LEVEL), sem_pair(LEVEL), sem_pair(LEVEL)]
+         sem_pair(11), sem_pair(LEVEL), dma((LEVEL,)), dma((HEIGHT,)), dma((LEVEL,)), dma((HEIGHT,)), dma((5, NDEV)), dma((NDEV,)),
+         dma((5, NDEV)), dma((NDEV,)), sem_pair(11), sem_pair(LEVEL), sem_pair(LEVEL), sem_pair(LEVEL)]
         + scatter_scratch(LANE, DIM) + LEVEL_SCRATCH)
 
 
@@ -752,7 +754,7 @@
         d_embed, d_gu, d_down, loss = step_call(
             ids_blk, lab_blk, emb_shard, pieces, down_shard, gain_mlp, gain_final, emb_scale, inv_count)
         d_gu = d_gu.reshape(LEVEL, PAIR, HEIGHT, DROWS).transpose(1, TWO, 0, TOP).reshape(PAIR, 3072)
-        return loss[0, 0], d_embed[0:VROWS], d_gu[0:GROWS], d_gu[GROWS:PAIR], d_down
+        return loss[0, 0], d_embed[0:VROWS] * emb_scale, d_gu[0:GROWS], d_gu[GROWS:PAIR], d_down
 
     shard_spec = P('fsdp', None)
     return jax.shard_map(local_step, mesh=mesh, in_specs=(shard_spec, shard_spec, shard_spec, shard_spec, shard_spec, shard_spec, P(), P()), out_specs=(P(), shard_spec, shard_spec, shard_spec, shard_spec), check_vma=False)

time: 286 us -> 272 us (0.951)
  Pallas kernels: 272 us -> 259 us
  other arithmetic: 1 us -> 4.84 us
  local copies, waits for them, and re-layouts: 11.1 us -> 7.32 us
    pallas_call x1, Pallas kernels: 272 us -> 259 us  [call(): pl.pallas_call(kernel, out_shape=outs, in_specs=[VSPEC] * len(ins), out_s...]
    mul x0 -> x1, other arithmetic: none -> 3.83 us  [local_step(): d_embed[0:VROWS] * emb_scale]
    slice x1 -> x0, local copies, waits for them, and re-layouts: 3.77 us -> none  [local_step(): d_embed[0:VROWS]]
where the time goes in v5:
time: 272 us
  Pallas kernels  259 us (95%)
  local copies, waits for them, and re-layouts  7.32 us (3%)
  other arithmetic  4.84 us (2%)
    pallas_call x1, Pallas kernels, call(): pl.pallas_call(kernel, out_shape=outs, in_specs=[VSPEC] * len(ins), out_s...  259 us

profile of v5, /device:TPU:0, one launch (start us, length us, event | category | flops | bytes accessed | tf_op | source)
XLA Modules:
  0.0 271.5 jit_solution(1775246037520616810)
XLA Ops:
  0.6 1.0 pad_maximum_fusion
  1.6 0.4 reshape.22
  2.0 0.2 copy.17
  2.2 1.0 reshape.23.piece_ref
  3.2 258.7 %step.1 = (f32[1024,768]{1,0:T(8,128)}, f32[8,48,384]{2,1,0:T(8,128)}, f32[96,768]{1,0:T(8,128)}, f32[8,128]{1,0:T(8,128)}) custom-call(s32[1,128]{1,0:T(1,128)} %ids_ref.1, s32[1,128]{1,0:T(1,128)} %lab_ref.1, bf16[1004,768]{1,0:T(8,128)(2,1)} %emb_ref.1, bf16[8,48,384]{2,1,0:T(8,128)(2,1)} %reshape.23.piece_ref, bf16[96,768]{1,0:T(8,128)(2,1)} %down_ref.1, ...), custom_call_target="tpu_custom_call" | custom-call | tf_op jit(solution)/shard_map/step/pallas_call | solution.py:427
  261.9 1.2 slice.18
  263.1 1.5 reshape.24
  264.6 0.1 fusion
  264.6 0.2 copy.15
  264.9 0.9 slice.23
  265.8 0.2 copy.14
  266.1 0.9 slice.21
  267.0 0.0 copy-start
  267.0 3.8 %slice_multiply_fusion = f32[1004,768]{1,0:T(8,128)} fusion(f32[1024,768]{1,0:T(8,128)} %get-tuple-element.10), kind=kLoop, calls=%fused_computation | loop fusion | flops 771072 | bytes 6168576 | tf_op jit(solution)/shard_map/mul | solution.py:757
  270.8 0.0 copy-done
  270.8 0.7 copy.19
Async XLA Ops:
  267.0 3.8 %copy-start = (f32[96,768]{1,0:T(8,128)S(1)}, f32[96,768]{1,0:T(8,128)}, u32[]{:S(2)}) copy-start(f32[96,768]{1,0:T(8,128)} %get-tuple-element.24) | copy-start | bytes 884740
